TPU v7x, 16 devices: a whole 2x2x2 slice. The times are simulated.
16 devices in a mesh: fsdp: 4 (over z, y), ep: 4 (over x, core).
Axes of the slice: x: 2, y: 2, z: 2, core: 2. Of those that a mesh axis runs over, the one named last changes fastest.
Arguments:
- x_tok: bfloat16 [16384, 512], P(('fsdp', 'ep'))
- dy_tok: bfloat16 [16384, 512], P(('fsdp', 'ep'))
- expert_ids: int32 [16384, 8], P(('fsdp', 'ep'))
- route_w: float32 [16384, 8], P(('fsdp', 'ep'))
- w_gate: bfloat16 [64, 512, 1280], P('ep', 'fsdp')
- w_up: bfloat16 [64, 512, 1280], P('ep', 'fsdp')
- w_down: bfloat16 [64, 1280, 512], P('ep', None, 'fsdp')
Outputs:
- output 1: bfloat16 [16384, 512], P(('fsdp', 'ep'))
- output 2: float32 [16384, 8], P(('fsdp', 'ep'))
- output 3: float32 [64, 512, 1280], P('ep', 'fsdp')
- output 4: float32 [64, 512, 1280], P('ep', 'fsdp')
- output 5: float32 [64, 1280, 512], P('ep', None, 'fsdp')
All inputs are finite; a program needn't handle non-finite values.
Results may differ from a plain program's by a relative error of at most 0.00989157.
Values are sent between devices in bfloat16 or wider.
A program may use at most 1 GiB of HBM per device.

v0:
```python
import jax
import jax.numpy as jnp
from jax import lax
from jax.sharding import PartitionSpec as P

CAP_FACTOR = 3


def capacity_of(tok_dev, top_k, experts):
    return max(8, ((CAP_FACTOR * tok_dev * top_k // experts + 7) // 8) * 8)


def route_slots(ids_dev, experts, capacity):
    n_pairs = ids_dev.shape[0]
    n_slots = experts * capacity
    onehot = (ids_dev[:, None] == jnp.arange(experts, dtype=jnp.int32)[None, :]).astype(jnp.int32)
    before = jnp.cumsum(onehot, axis=0) - onehot
    position = jnp.sum(before * onehot, axis=1)
    dest_slot = jnp.where(position < capacity, ids_dev * capacity + position, n_slots)
    held = jax.ops.segment_sum(jnp.arange(1, n_pairs + 1, dtype=jnp.int32), dest_slot, num_segments=n_slots + 1)[:n_slots]
    slot_src = jnp.where(held > 0, held - 1, n_pairs)
    return dest_slot, slot_src


def swiglu_grads(pre_gate, pre_up, grad_hidden):
    sigma = jax.nn.sigmoid(pre_gate)
    grad_gate = grad_hidden * pre_up * sigma * (1.0 + pre_gate * (1.0 - sigma))
    grad_up = grad_hidden * pre_gate * sigma
    return grad_gate.astype(jnp.bfloat16), grad_up.astype(jnp.bfloat16)


def expert_backward(x_rows, dy_rows, gate_rows, w_gate_full, w_up_full, w_down_full):
    pre_gate = jnp.einsum("secd,edf->secf", x_rows, w_gate_full, preferred_element_type=jnp.float32)
    pre_up = jnp.einsum("secd,edf->secf", x_rows, w_up_full, preferred_element_type=jnp.float32)
    hidden = (jax.nn.silu(pre_gate) * pre_up).astype(jnp.bfloat16)
    y_rows = jnp.einsum("secf,efd->secd", hidden, w_down_full, preferred_element_type=jnp.float32)
    dy_wide = dy_rows.astype(jnp.float32)
    scaled_dy = (gate_rows[..., None] * dy_wide).astype(jnp.bfloat16)
    dr_rows = jnp.sum(dy_wide * y_rows, axis=-1)
    grad_hidden = jnp.einsum("secd,efd->secf", scaled_dy, w_down_full, preferred_element_type=jnp.float32)
    grad_gate, grad_up = swiglu_grads(pre_gate, pre_up, grad_hidden)
    dx_rows = (jnp.einsum("secf,edf->secd", grad_gate, w_gate_full, preferred_element_type=jnp.float32)
               + jnp.einsum("secf,edf->secd", grad_up, w_up_full, preferred_element_type=jnp.float32)).astype(jnp.bfloat16)
    dw_gate = jnp.einsum("secd,secf->edf", x_rows, grad_gate, preferred_element_type=jnp.float32)
    dw_up = jnp.einsum("secd,secf->edf", x_rows, grad_up, preferred_element_type=jnp.float32)
    dw_down = jnp.einsum("secf,secd->efd", hidden, scaled_dy, preferred_element_type=jnp.float32)
    return dx_rows, dr_rows, dw_gate, dw_up, dw_down


def take_rows(rows, row_ids):
    return jnp.take(rows, row_ids, axis=0, mode="fill", fill_value=0)


def solution(mesh):
    n_ep = mesh.shape["ep"]
    tok_spec = P(("fsdp", "ep"), None)
    spec_in = P("ep", "fsdp", None)
    spec_out = P("ep", None, "fsdp")

    def per_device(x_tok, dy_tok, expert_ids, route_w, w_gate, w_up, w_down):
        tok_dev, top_k = expert_ids.shape
        exp_local = w_gate.shape[0]
        d_model = x_tok.shape[1]
        experts = exp_local * n_ep
        capacity = capacity_of(tok_dev, top_k, experts)
        dest_slot, slot_src = route_slots(expert_ids.reshape(-1), experts, capacity)
        tok_of_slot = slot_src // top_k
        x_send = take_rows(x_tok, tok_of_slot)
        dy_send = take_rows(dy_tok, tok_of_slot)
        gate_send = take_rows(route_w.reshape(-1), slot_src)
        x_recv = lax.all_to_all(x_send, "ep", 0, 0, tiled=True).reshape(n_ep, exp_local, capacity, d_model)
        dy_recv = lax.all_to_all(dy_send, "ep", 0, 0, tiled=True).reshape(n_ep, exp_local, capacity, d_model)
        gate_recv = lax.all_to_all(gate_send, "ep", 0, 0, tiled=True).reshape(n_ep, exp_local, capacity)
        w_gate_full = lax.all_gather(w_gate, "fsdp", axis=1, tiled=True)
        w_up_full = lax.all_gather(w_up, "fsdp", axis=1, tiled=True)
        w_down_full = lax.all_gather(w_down, "fsdp", axis=2, tiled=True)
        dx_rows, dr_rows, dw_gate, dw_up, dw_down = expert_backward(
            x_recv, dy_recv, gate_recv, w_gate_full, w_up_full, w_down_full)
        dx_back = lax.all_to_all(dx_rows.reshape(n_ep * exp_local * capacity, d_model), "ep", 0, 0, tiled=True)
        dr_back = lax.all_to_all(dr_rows.reshape(-1), "ep", 0, 0, tiled=True)
        dx_pairs = take_rows(dx_back, dest_slot).reshape(tok_dev, top_k, d_model)
        grad_x = jnp.sum(dx_pairs.astype(jnp.float32), axis=1).astype(jnp.bfloat16)
        route_grad = take_rows(dr_back, dest_slot).reshape(tok_dev, top_k)
        grad_w_gate = lax.psum_scatter(dw_gate, "fsdp", scatter_dimension=1, tiled=True)
        grad_w_up = lax.psum_scatter(dw_up, "fsdp", scatter_dimension=1, tiled=True)
        grad_w_down = lax.psum_scatter(dw_down, "fsdp", scatter_dimension=2, tiled=True)
        return grad_x, route_grad, grad_w_gate, grad_w_up, grad_w_down

    return jax.shard_map(
        per_device, mesh=mesh,
        in_specs=(tok_spec, tok_spec, tok_spec, tok_spec, spec_in, spec_in, spec_out),
        out_specs=(tok_spec, tok_spec, spec_in, spec_in, spec_out),
        check_vma=False)
```

profile of v0, /device:TPU:0, one launch (start us, length us, event | category | flops | bytes accessed | tf_op | source)
XLA Modules:
  0.0 2383.5 jit_solution(16403994005752153271)
XLA Ops:
  7.2 0.7 all-gather.6.cloned.1.call-update
  8.0 0.7 all-gather.4.cloned.1.call-update
  8.7 1.0 copy.47
  10.4 1.6 fusion.47
  12.0 34.0 %reduce-window.6 = s32[64,64,128]{2,1,0:T(8,128)S(1)} reduce-window(s32[64,64,128]{2,1,0:T(8,128)} %fusion.47, s32[]{:T(128)} %constant.58.clone.1), window={size=1x1x128 pad=0_0x0_0x127_0}, to_apply=%region_0.0 | reduce-window | flops 66584576 | bytes 4194308 | tf_op jit(solution)/shard_map/reduce-window
  46.0 1.7 slice_reduce_fusion
  47.9 1.9 broadcast_multiply_fusion
  49.8 1.3 mul.64
  51.1 1.8 copy.50
  52.9 1.3 reshape.171
  54.1 0.7 broadcast_add_fusion
  54.9 1.9 fusion.46
  56.7 0.7 compare_select_fusion.3
  57.4 43.2 %scatter_custom_fusion = s32[24577]{0:T(1024)S(1)} fusion(s32[8192]{0:T(1024)S(1)} %bitcast.140, s32[8192]{0:T(1024)S(1)} %iota_add_fusion, s32[]{:T(128)} %constant.58.clone.1), kind=kCustom, calls=%fused_computation.84 | custom fusion | flops 8192 | bytes 98312 | tf_op jit(solution)/shard_map/scatter-add | solution.py:20
  100.7 135.5 %gather_fusion = f32[24576]{0:T(1024)S(1)} fusion(f32[8192]{0:T(1024)S(1)} %reshape.171, s32[24576]{0:T(1024)S(1)} %get-tuple-element.30), kind=kCustom, calls=%fused_computation.2 | custom fusion | bytes 294912 | tf_op jit(solution)/shard_map/jit(_take)/gather | solution.py:51
  236.5 0.7 copy.51
  237.2 4.5 all-to-all-start
  241.7 99.0 %gather_fusion.3 = bf16[24576,512]{1,0:T(8,128)(2,1)} fusion(bf16[1024,512]{1,0:T(8,128)(2,1)S(1)} %copy-done, s32[24576]{0:T(1024)S(1)} %get-tuple-element.29), kind=kCustom, calls=%fused_computation.clone | custom fusion | bytes 50429952 | tf_op jit(solution)/shard_map/jit(_take)/gather | solution.py:51
  340.7 99.1 %gather_fusion.4 = bf16[24576,512]{1,0:T(8,128)(2,1)} fusion(bf16[1024,512]{1,0:T(8,128)(2,1)S(1)} %copy-done.2, s32[24576]{0:T(1024)S(1)} %get-tuple-element.29), kind=kCustom, calls=%fused_computation.1.clone | custom fusion | bytes 50429952 | tf_op jit(solution)/shard_map/jit(_take)/gather | solution.py:51
  439.9 34.3 %broadcast_select_fusion.1 = (bf16[24576,512]{1,0:T(8,128)(2,1)}, bf16[24576,512]{1,0:T(8,128)(2,1)}) fusion(bf16[24576,512]{1,0:T(8,128)(2,1)} %gather_fusion.3, pred[24576]{0:T(1024)(128)(4,1)S(1)} %compare_and_fusion.1, bf16[24576,512]{1,0:T(8,128)(2,1)} %gather_fusion.4), kind=kLoop, calls=%fused_computation.35 | loop fusion | flops 25165824 | bytes 100687872 | tf_op jit(solution)/shard_map/jit(_take)/select_n | solution.py:51
  474.3 8.4 all-to-all-start.2
  482.7 0.7 all-gather.8.cloned.1.call-update
  483.4 272.2 %all-to-all-done.2 = bf16[4,6144,512]{2,1,0:T(8,128)(2,1)} async-done(((bf16[4,6144,512]{2,1,0:T(8,128)(2,1)}), bf16[4,6144,512]{2,1,0:T(8,128)(2,1)}, u32[]{:S(2)}, u32[]{:S(2)}) %all-to-all-start.2) | async-done | bytes 25165856 | tf_op jit(solution)/shard_map/all_to_all | solution.py:71
  755.6 8.4 all-to-all-start.1
  764.0 0.5 reduce-scatter.8.cloned.1.call-start
  764.5 1.2 reduce.2
  765.7 59.6 %fusion.25 = f32[16,4,384,1280]{3,2,1,0:T(8,128)} fusion(bf16[4,16,384,512]{3,2,1,0:T(8,128)(2,1)} %bitcast.9, bf16[16,512,1280]{2,1,0:T(8,128)(2,1)} %all-gather.6.cloned.1.call-done), kind=kOutput, calls=%fused_computation.38 | convolution fusion | flops 32212254720 | bytes 171966464 | tf_op jit(solution)/shard_map/secd,edf->secf/dot_general | solution.py:34
  825.2 211.3 %all-to-all-done.1 = bf16[4,6144,512]{2,1,0:T(8,128)(2,1)} async-done(((bf16[4,6144,512]{2,1,0:T(8,128)(2,1)}), bf16[4,6144,512]{2,1,0:T(8,128)(2,1)}, u32[]{:S(2)}, u32[]{:S(2)}) %all-to-all-start.1) | async-done | bytes 25165856 | tf_op jit(solution)/shard_map/all_to_all | solution.py:72
  1036.5 59.8 %fusion.28 = f32[16,4,384,1280]{3,2,1,0:T(8,128)} fusion(bf16[16,1280,512]{2,1,0:T(8,128)(2,1)} %all-gather.4.cloned.1.call-done, f32[4,16,384]{2,1,0:T(8,128)S(1)} %bitcast.137, bf16[4,16,384,512]{3,2,1,0:T(8,128)(2,1)} %bitcast.22), kind=kOutput, calls=%fused_computation.41 | convolution fusion | flops 32250003456 | bytes 172064768 | tf_op jit(solution)/shard_map/secd,efd->secf/dot_general | solution.py:40
  1096.3 163.7 %fusion.9 = (bf16[4,16,384,1280]{3,2,0,1:T(8,128)(2,1)}, bf16[4,16,384,1280]{3,2,0,1:T(8,128)(2,1)}, bf16[4,16,384,1280]{3,2,0,1:T(8,128)(2,1)}) fusion(f32[16,4,384,1280]{3,2,1,0:T(8,128)} %fusion.25, f32[16,4,384,1280]{3,2,1,0:T(8,128)} %fusion.28, bf16[16,512,1280]{2,1,0:T(8,128)(2,1)} %all-gather.8.cloned.1.call-done, bf16[4,16,384,512]{3,2,1,0:T(8,128)(2,1)} %bitcast.9), kind=kOutput, calls=%fused_computation.19 | convolution fusion | flops 32715571200 | bytes 486539264 | tf_op jit(solution)/shard_map/secd,edf->secf/dot_general | solution.py:33
  1260.1 50.8 %convolution_bitcast_fusion = f32[16,1280,512]{2,1,0:T(8,128)} fusion(bf16[4,16,384,1280]{3,2,0,1:T(8,128)(2,1)} %get-tuple-element.25, f32[4,16,384]{2,1,0:T(8,128)S(1)} %bitcast.138, bf16[4,16,384,512]{3,2,1,0:T(8,128)(2,1)} %bitcast.22), kind=kOutput, calls=%fused_computation.30 | convolution fusion | flops 32250003456 | bytes 130121728 | tf_op jit(solution)/shard_map/secf,secd->efd/dot_general | solution.py:46
  1311.0 59.9 %fusion.16 = f32[16,512,1280]{2,1,0:T(8,128)} fusion(bf16[4,16,384,512]{3,2,1,0:T(8,128)(2,1)} %bitcast.9, bf16[4,16,384,1280]{3,2,0,1:T(8,128)(2,1)} %get-tuple-element.26), kind=kOutput, calls=%fused_computation.31 | convolution fusion | flops 32212254720 | bytes 130023424 | tf_op jit(solution)/shard_map/secd,secf->edf/dot_general | solution.py:44
  1370.9 60.0 %fusion.19 = f32[16,512,1280]{2,1,0:T(8,128)} fusion(bf16[4,16,384,512]{3,2,1,0:T(8,128)(2,1)} %bitcast.9, bf16[4,16,384,1280]{3,2,0,1:T(8,128)(2,1)} %get-tuple-element.27), kind=kOutput, calls=%fused_computation.32 | convolution fusion | flops 32212254720 | bytes 130023424 | tf_op jit(solution)/shard_map/secd,secf->edf/dot_general | solution.py:45
  1430.9 44.7 %fusion.15 = f32[4,16,384]{2,0,1:T(4,128)S(1)} fusion(bf16[4,16,384,1280]{3,2,0,1:T(8,128)(2,1)} %get-tuple-element.25, bf16[16,1280,512]{2,1,0:T(8,128)(2,1)} %all-gather.4.cloned.1.call-done, bf16[4,16,384,512]{3,2,1,0:T(8,128)(2,1)} %bitcast.22), kind=kOutput, calls=%fused_computation.27 | convolution fusion | flops 32249978880 | bytes 109150208 | tf_op jit(solution)/shard_map/secf,efd->secd/dot_general | solution.py:36
  1475.6 0.7 copy.57
  1476.3 3.6 all-to-all-start.4
  1479.9 56.5 %fusion.30 = f32[16,4,384,512]{3,2,1,0:T(8,128)} fusion(bf16[4,16,384,1280]{3,2,0,1:T(8,128)(2,1)} %get-tuple-element.26, bf16[16,512,1280]{2,1,0:T(8,128)(2,1)} %all-gather.8.cloned.1.call-done), kind=kOutput, calls=%fused_computation.43 | convolution fusion | flops 32212254720 | bytes 134217728 | tf_op jit(solution)/shard_map/secf,edf->secd/dot_general | solution.py:42
  1536.4 53.9 %fusion.22 = bf16[4,16,384,512]{3,2,0,1:T(8,128)(2,1)} fusion(f32[16,4,384,512]{3,2,1,0:T(8,128)} %fusion.30, bf16[4,16,384,1280]{3,2,0,1:T(8,128)(2,1)} %get-tuple-element.27, bf16[16,512,1280]{2,1,0:T(8,128)(2,1)} %all-gather.6.cloned.1.call-done), kind=kOutput, calls=%fused_computation.33 | convolution fusion | flops 32237420544 | bytes 159383552 | tf_op jit(solution)/shard_map/secf,edf->secd/dot_general | solution.py:43
  1590.3 20.7 copy.55
  1611.0 8.9 all-to-all-start.3
  1619.9 0.3 reduce_sum.35
  1620.3 45.5 %gather_fusion.2 = f32[8192]{0:T(1024)S(1)} fusion(f32[24576]{0:T(1024)S(1)} %bitcast.128, s32[8192]{0:T(1024)S(1)} %broadcast_clamp_fusion.1), kind=kCustom, calls=%fused_computation.4 | custom fusion | bytes 98304 | tf_op jit(solution)/shard_map/jit(_take)/gather | solution.py:51
  1666.4 0.8 copy.64
  1667.1 225.4 %all-to-all-done.3 = bf16[4,6144,512]{2,1,0:T(8,128)(2,1)} async-done(((bf16[4,6144,512]{2,1,0:T(8,128)(2,1)}), bf16[4,6144,512]{2,1,0:T(8,128)(2,1)}, u32[]{:S(2)}, u32[]{:S(2)}) %all-to-all-start.3) | async-done | bytes 25165856 | tf_op jit(solution)/shard_map/all_to_all | solution.py:79
  1892.5 45.4 %gather_fusion.1 = bf16[8192,512]{1,0:T(8,128)(2,1)} fusion(bf16[24576,512]{1,0:T(8,128)(2,1)} %bitcast.19, s32[8192]{0:T(1024)S(1)} %broadcast_clamp_fusion.1), kind=kCustom, calls=%fused_computation.3 | custom fusion | bytes 16809984 | tf_op jit(solution)/shard_map/jit(_take)/gather | solution.py:51
  1937.9 11.1 fusion.43
  1949.0 71.3 %reduce-scatter.4.cloned.1.call-done = f32[16,128,1280]{2,1,0:T(8,128)} async-done(((f32[16,512,1280]{2,1,0:T(8,128)}), f32[16,128,1280]{2,1,0:T(8,128)}) %reduce-scatter.4.cloned.1.call-update) | async-done | bytes 10485776 | tf_op jit(solution)/shard_map/reduce_scatter | solution.py:84
  2020.3 355.8 %reduce-scatter.6.cloned.1.call-done = f32[16,128,1280]{2,1,0:T(8,128)} async-done(((f32[16,512,1280]{2,1,0:T(8,128)}), f32[16,128,1280]{2,1,0:T(8,128)}) %reduce-scatter.6.cloned.1.call-update) | async-done | bytes 10485776 | tf_op jit(solution)/shard_map/reduce_scatter | solution.py:85
  (51 shorter events, 2.2 us)
Async XLA Ops:
  7.2 234.5 %copy-start = (bf16[1024,512]{1,0:T(8,128)(2,1)S(1)}, bf16[1024,512]{1,0:T(8,128)(2,1)}, u32[]{:S(2)}) copy-start(bf16[1024,512]{1,0:T(8,128)(2,1)} %param.10) | copy-start | bytes 3145732
  7.2 758.5 %all-gather.6.cloned.1.call-start = ((), (), s32[]{:S(2)}) async-start(), calls=%async_computation.9 | async-start | bytes 26214400 | tf_op jit(solution)/shard_map/all_gather | solution.py:75
  7.9 1028.6 %all-gather.4.cloned.1.call-start = ((), (), s32[]{:S(2)}) async-start(), calls=%async_computation.8 | async-start | bytes 26214400 | tf_op jit(solution)/shard_map/all_gather | solution.py:76
  9.6 0.8 copy-start.3
  56.7 0.7 copy-start.7
  100.6 135.7 %copy-start.5 = (s32[24577]{0:T(1024)}, s32[24577]{0:T(1024)S(1)}, u32[]{:S(2)}) copy-start(s32[24577]{0:T(1024)S(1)} %scatter_custom_fusion) | copy-start | bytes 294928
  237.2 237.1 %all-to-all-start = ((f32[4,6144,1]{1,2,0:T(1,128)}), f32[4,6144,1]{1,2,0:T(1,128)}, u32[]{:S(2)}, u32[]{:S(2)}) async-start(f32[4,6144,1]{1,2,0:T(1,128)} %copy.51), calls=%async_computation | async-start | bytes 196608 | tf_op jit(solution)/shard_map/all_to_all | solution.py:73
  241.7 99.0 %copy-start.2 = (bf16[1024,512]{1,0:T(8,128)(2,1)S(1)}, bf16[1024,512]{1,0:T(8,128)(2,1)}, u32[]{:S(2)}) copy-start(bf16[1024,512]{1,0:T(8,128)(2,1)} %param.9) | copy-start | bytes 3145732
  340.7 99.1 %copy-start.6 = (s32[24577]{0:T(1024)S(1)}, s32[24577]{0:T(1024)}, u32[]{:S(2)}) copy-start(s32[24577]{0:T(1024)} %copy-done.5) | copy-start | bytes 294928
  474.3 281.3 %all-to-all-start.2 = ((bf16[4,6144,512]{2,1,0:T(8,128)(2,1)}), bf16[4,6144,512]{2,1,0:T(8,128)(2,1)}, u32[]{:S(2)}, u32[]{:S(2)}) async-start(bf16[4,6144,512]{2,1,0:T(8,128)(2,1)} %bitcast.131), calls=%async_computation.2 | async-start | bytes 50331648 | tf_op jit(solution)/shard_map/all_to_all | solution.py:71
  482.7 613.6 %all-gather.8.cloned.1.call-start = ((), (), s32[]{:S(2)}) async-start(), calls=%async_computation.10 | async-start | bytes 26214400 | tf_op jit(solution)/shard_map/all_gather | solution.py:74
  755.6 281.0 %all-to-all-start.1 = ((bf16[4,6144,512]{2,1,0:T(8,128)(2,1)}), bf16[4,6144,512]{2,1,0:T(8,128)(2,1)}, u32[]{:S(2)}, u32[]{:S(2)}) async-start(bf16[4,6144,512]{2,1,0:T(8,128)(2,1)} %bitcast.130), calls=%async_computation.1 | async-start | bytes 50331648 | tf_op jit(solution)/shard_map/all_to_all | solution.py:72
  764.0 1185.0 %reduce-scatter.8.cloned.1.call-start = ((), (), s32[]{:S(2)}) async-start(), calls=%async_computation.13 | async-start | bytes 52428800 | tf_op jit(solution)/shard_map/reduce_scatter | solution.py:86
  765.6 270.9 %copy-start.10 = (f32[1,4,16,384]{3,2,1,0:T(8,128)}, f32[1,4,16,384]{3,2,1,0:T(8,128)S(1)}, u32[]{:S(2)}) copy-start(f32[1,4,16,384]{3,2,1,0:T(8,128)S(1)} %copy.99) | copy-start | bytes 294916
  1096.3 163.8 %copy-start.11 = (f32[1,4,16,384]{3,2,1,0:T(8,128)S(1)}, f32[1,4,16,384]{3,2,1,0:T(8,128)}, u32[]{:S(2)}) copy-start(f32[1,4,16,384]{3,2,1,0:T(8,128)} %copy-done.10) | copy-start | bytes 294916
  1310.9 709.4 %reduce-scatter.4.cloned.1.call-start = ((), (), s32[]{:S(2)}) async-start(), calls=%async_computation.11 | async-start | bytes 52428800 | tf_op jit(solution)/shard_map/reduce_scatter | solution.py:84
  1370.9 1005.3 %reduce-scatter.6.cloned.1.call-start = ((), (), s32[]{:S(2)}) async-start(), calls=%async_computation.12 | async-start | bytes 52428800 | tf_op jit(solution)/shard_map/reduce_scatter | solution.py:85
  1476.3 134.7 %all-to-all-start.4 = ((f32[4,6144,1]{1,2,0:T(1,128)}), f32[4,6144,1]{1,2,0:T(1,128)S(1)}, u32[]{:S(2)}, u32[]{:S(2)}) async-start(f32[4,6144,1]{1,2,0:T(1,128)} %copy.57), calls=%async_computation.4 | async-start | bytes 196608 | tf_op jit(solution)/shard_map/all_to_all | solution.py:80
  1611.0 8.9 copy-start.8
  1611.0 9.2 copy-start.9
  1611.0 281.5 %all-to-all-start.3 = ((bf16[4,6144,512]{2,1,0:T(8,128)(2,1)}), bf16[4,6144,512]{2,1,0:T(8,128)(2,1)}, u32[]{:S(2)}, u32[]{:S(2)}) async-start(bf16[4,6144,512]{2,1,0:T(8,128)(2,1)} %bitcast.129), calls=%async_computation.3 | async-start | bytes 50331648 | tf_op jit(solution)/shard_map/all_to_all | solution.py:79
  1619.9 46.2 %copy-start.4 = (s32[1024,8]{1,0:T(8,128)S(1)}, s32[1024,8]{1,0:T(8,128)}, u32[]{:S(2)}) copy-start(s32[1024,8]{1,0:T(8,128)} %copy-done.3) | copy-start | bytes 98308
  1892.5 483.6 %copy-start.1 = (bf16[1024,512]{1,0:T(8,128)(2,1)S(1)}, bf16[1024,512]{1,0:T(8,128)(2,1)}, u32[]{:S(2)}) copy-start(bf16[1024,512]{1,0:T(8,128)(2,1)} %param.10) | copy-start | bytes 3145732
Sparse Core Ops, SparseCore 0:
  9.8 192.0 all-gather.5
  203.7 189.2 all-gather.3
  485.3 191.9 all-gather.7
  1311.0 353.3 reduce-scatter.7
  1667.9 352.3 reduce-scatter.3
  2023.8 352.2 reduce-scatter.5
where the time goes:
time: 2390 us; the launch traced here: 2380 us
  waiting for transfers between devices  1140 us (48%)
  matrix products  609 us (25%)
  local copies, waits for them, and re-layouts  456 us (19%)
  other arithmetic  131 us (5%)
  starting transfers between devices  34.4 us (1%)
    gather x7, local copies, waits for them, and re-layouts, take_rows(): return jnp.take(rows, row_ids, axis=0, mode='fill', fill_value=0)  425 us
    reduce_scatter x1, waiting for transfers between devices, per_device(): grad_w_up = lax.psum_scatter(dw_up, 'fsdp', scatter_dimension=1, tiled=True)  356 us
    all_to_all x1, waiting for transfers between devices, per_device(): lax.all_to_all(x_send, 'ep', 0, 0, tiled=True)  272 us
    all_to_all x1, waiting for transfers between devices, per_device(): lax.all_to_all(dx_rows.reshape(n_ep * exp_local * capacity, d_model), 'ep...  225 us
    all_to_all x1, waiting for transfers between devices, per_device(): lax.all_to_all(dy_send, 'ep', 0, 0, tiled=True)  211 us
    dot_general x1, matrix products, expert_backward(): jnp.einsum('secd,edf->secf', x_rows, w_gate_full, preferred_element_type=...  164 us
    reduce_scatter x1, waiting for transfers between devices, per_device(): lax.psum_scatter(dw_gate, 'fsdp', scatter_dimension=1, tiled=True)  71.3 us
    dot_general x1, matrix products, expert_backward(): jnp.einsum('secd,secf->edf', x_rows, grad_up, preferred_element_type=jnp....  60 us
  transfers between devices with their start and end apart: 11, of which 5 were waited for; matrix products, arithmetic and copies ran while one was open for 41% of the time, Pallas kernels for 0%

commit v1 on v0

v1 whole, which is shorter than its diff:
```python
import functools

import jax
import jax.numpy as jnp
from jax import lax
from jax.experimental import pallas as pl
from jax.experimental.pallas import tpu as pltpu
from jax.sharding import PartitionSpec as P


CAP_FACTOR = 3
CHUNK = 128
TILE = 512
MM = 256
COPY = 64
VMEM_LIMIT = 60 * 1024 * 1024
F32 = jnp.float32
BF16 = jnp.bfloat16


def capacity_of(tok_dev, top_k, experts):
    return max(8, ((CAP_FACTOR * tok_dev * top_k // experts + 7) // 8) * 8)


def up(n, m):
    return (n + m - 1) // m * m


def blocks(n, size):
    return lax.div(n + (size - 1), jnp.full_like(n, size))


def dot(a, b):
    return lax.dot_general(a, b, (((1,), (0,)), ((), ())), preferred_element_type=F32)


def dot_nt(a, b):
    return lax.dot_general(a, b, (((1,), (1,)), ((), ())), preferred_element_type=F32)


def dot_tn(a, b):
    return lax.dot_general(a, b, (((0,), (0,)), ((), ())), preferred_element_type=F32)


def route_tables(expert_ids, route_w, experts, capacity):
    tok_dev, _ = expert_ids.shape
    ids_t, w_t = expert_ids.T, route_w.T
    hit = ids_t[:, None, :] == jnp.arange(experts, dtype=jnp.int32)[None, :, None]
    chosen = jnp.any(hit, axis=0)
    weight = jnp.sum(jnp.where(hit, w_t[:, None, :], 0.0), axis=0)
    earlier = jnp.arange(tok_dev)[:, None] < jnp.arange(tok_dev)[None, :]
    before = dot(chosen.astype(BF16), earlier.astype(BF16))
    position = jnp.where(chosen & (before < capacity), before, -1.0)
    return position, weight


def one_hot_block(pos_row, c):
    row = lax.broadcasted_iota(jnp.int32, (CHUNK, pos_row.shape[1]), 0) + c * CHUNK
    return row == pos_row


def aligned(v, m=16):
    return pl.multiple_of(v, m)


def gather_kernel(n_src, n_loc, region, with_r, *refs):
    if with_r:
        (cnt, off, pos_ref, r_ref, src_ref, out, r_out, hot, stage, pool, rstage, rpool, sem) = refs
    else:
        (cnt, off, pos_ref, src_ref, out, hot, stage, pool, sem) = refs
    s = pl.program_id(0)
    base = jnp.int32(0)
    starts = []
    for k in range(n_loc):
        n = cnt[s * n_loc + k]
        starts.append(base)
        pos_row = pos_ref[0, k:k + 1, :]

        def build(c, carry, base=base, pos_row=pos_row, k=k):
            m = one_hot_block(pos_row, c)
            at = pl.ds(aligned(base + c * CHUNK), CHUNK)
            hot[at, :] = jnp.where(m, 1.0, 0.0).astype(BF16)
            if with_r:
                r = jnp.sum(jnp.where(m, r_ref[0, k:k + 1, :], 0.0), axis=1, keepdims=True)
                rstage[at, :] = jnp.broadcast_to(r, (CHUNK, 128))
            return carry

        lax.fori_loop(0, blocks(n, CHUNK), build, 0)
        base = base + blocks(n, 16) * 16

    def mm(c, carry):
        at = pl.ds(aligned(c * MM), MM)
        stage[at, :] = dot(hot[at, :], src_ref[...]).astype(BF16)
        return carry

    lax.fori_loop(0, blocks(base, MM), mm, 0)

    for k in range(n_loc):
        n = cnt[s * n_loc + k]
        to = off[s * n_loc + k] + k * region

        def move(c, carry, start=starts[k], to=to):
            dst = pl.ds(aligned(to + c * COPY), COPY)
            frm = pl.ds(aligned(start + c * COPY), COPY)
            pool[dst, :] = stage[frm, :]
            if with_r:
                rpool[dst, :] = rstage[frm, :]
            return carry

        lax.fori_loop(0, blocks(n, COPY), move, 0)

    @pl.when(s == n_src - 1)
    def _():
        def copies(k, i):
            at = pl.ds(aligned(k * region + i * TILE, TILE), TILE)
            made = [pltpu.make_async_copy(pool.at[at], out.at[at], sem)]
            if with_r:
                made.append(pltpu.make_async_copy(rpool.at[at], r_out.at[at], sem))
            return made

        tiles = []
        for k in range(n_loc):
            end = off[s * n_loc + k] + blocks(cnt[s * n_loc + k], 16) * 16
            at = pl.ds(aligned(k * region + end), TILE)
            pool[at, :] = jnp.zeros((TILE, pool.shape[1]), BF16)
            if with_r:
                rpool[at, :] = jnp.zeros((TILE, 128), F32)
            tiles.append(jnp.maximum(1, blocks(end, TILE)))
        for k in range(n_loc):
            def start(i, carry, k=k):
                for copy in copies(k, i):
                    copy.start()
                return carry

            lax.fori_loop(0, tiles[k], start, 0)
        for k in range(n_loc):
            def wait(i, carry, k=k):
                for copy in copies(k, i):
                    copy.wait()
                return carry

            lax.fori_loop(0, tiles[k], wait, 0)


def gather_rows(src, cnt, off, pos, r, region):
    n_src, n_loc, tok = pos.shape
    d = src.shape[1]
    with_r = r is not None
    rows = n_loc * region
    scr = n_loc * ((region - TILE) // n_src) + CHUNK
    scr = up(scr, MM)
    table = pl.BlockSpec((1, n_loc, tok), lambda s, *_: (s, 0, 0))
    in_specs = [table] + ([table] if with_r else []) + [pl.BlockSpec((tok, d), lambda s, *_: (s, 0))]
    out_shape = [jax.ShapeDtypeStruct((rows, d), BF16)]
    scratch = [pltpu.VMEM((scr, tok), BF16), pltpu.VMEM((scr, d), BF16), pltpu.VMEM((rows, d), BF16)]
    if with_r:
        out_shape.append(jax.ShapeDtypeStruct((rows, 128), F32))
        scratch += [pltpu.VMEM((scr, 128), F32), pltpu.VMEM((rows, 128), F32)]
    out = pl.pallas_call(
        functools.partial(gather_kernel, n_src, n_loc, region, with_r),
        out_shape=out_shape,
        grid_spec=pltpu.PrefetchScalarGridSpec(
            num_scalar_prefetch=2, grid=(n_src,), in_specs=in_specs,
            out_specs=[pl.BlockSpec(memory_space=pl.ANY)] * len(out_shape),
            scratch_shapes=scratch + [pltpu.SemaphoreType.DMA]),
        compiler_params=pltpu.CompilerParams(vmem_limit_bytes=VMEM_LIMIT, dimension_semantics=("arbitrary",)),
        cost_estimate=pl.CostEstimate(flops=2 * 12000 * tok * d, bytes_accessed=n_src * tok * d * 4, transcendentals=0),
        name="gather_r" if with_r else "gather_x",
    )(*([cnt, off, pos] + ([r] if with_r else []) + [src]))
    return out if with_r else out[0]


def expert_kernel(n_fs, info, x_ref, dy_ref, r_ref, w1_ref, w3_ref, w2s_ref, dx_ref, dr_ref, *refs):
    outs, (w2, a_buf, dh1_buf, dh3_buf, dw1, dw3, dw2t) = refs[:n_fs], refs[n_fs:]
    i = pl.program_id(0)
    d, f = w1_ref.shape
    dsl = d // n_fs

    @pl.when(i == 0)
    def _():
        dw1[...] = jnp.zeros_like(dw1)
        dw3[...] = jnp.zeros_like(dw3)
        dw2t[...] = jnp.zeros_like(dw2t)
        for q in range(n_fs):
            w2[:, q * dsl:(q + 1) * dsl] = w2s_ref[q]

    def tile(m):
        x, dy = x_ref[:m, :], dy_ref[:m, :]
        dy_wide = dy.astype(F32)
        g = (r_ref[:m, 0:1] * dy_wide).astype(BF16)
        step = 256
        for c in range(0, f, step):
            cs = slice(c, c + step)
            h1 = dot(x, w1_ref[:, cs])
            h3 = dot(x, w3_ref[:, cs])
            da = dot_nt(g, w2[cs, :])
            s = jax.nn.sigmoid(h1)
            hs = h1 * s
            a_buf[:m, cs] = (hs * h3).astype(BF16)
            dh1_buf[:m, cs] = (da * h3 * s * (1.0 + h1 * (1.0 - s))).astype(BF16)
            dh3_buf[:m, cs] = (da * hs).astype(BF16)
        y = dot(a_buf[:m, :], w2[...])
        dr = jnp.sum(dy_wide * y, axis=1, keepdims=True)
        dr_ref[:m, :] = jnp.broadcast_to(dr, (m, 128))
        dx_ref[:m, :] = (dot_nt(dh1_buf[:m, :], w1_ref[...]) + dot_nt(dh3_buf[:m, :], w3_ref[...])).astype(BF16)
        dw1[...] += dot_tn(x, dh1_buf[:m, :])
        dw3[...] += dot_tn(x, dh3_buf[:m, :])
        dw2t[...] += dot_tn(g, a_buf[:m, :])

    left = info[0] - i * TILE

    @pl.when(left > TILE // 2)
    def _():
        tile(TILE)

    @pl.when((i < info[1]) & (left <= TILE // 2))
    def _():
        tile(TILE // 2)
        dx_ref[TILE // 2:, :] = jnp.zeros((TILE // 2, d), BF16)
        dr_ref[TILE // 2:, :] = jnp.zeros((TILE // 2, 128), F32)

    @pl.when(i == info[1] - 1)
    def _():
        for m in range(n_fs):
            at = pl.ds(aligned((info[2] ^ m) * dsl, dsl), dsl)
            for t, acc in enumerate((dw1, dw3, dw2t)):
                outs[m][t] = acc[at, :]


def expert_call(k, info, x_pool, dy_pool, r_pool, w1, w3, w2s, region):
    n_fs, f, dsl = w2s.shape
    d = w1.shape[0]
    first = k * (region // TILE)
    row_map = lambda i, info: (first + jnp.minimum(i, info[1] - 1), 0)
    out_map = lambda i, info: (jnp.minimum(i, info[1] - 1), 0)
    whole = lambda i, info: (0, 0)
    whole3 = lambda i, info: (0, 0, 0)
    return pl.pallas_call(
        functools.partial(expert_kernel, n_fs),
        out_shape=[jax.ShapeDtypeStruct((region, d), BF16), jax.ShapeDtypeStruct((region, 128), F32)]
        + [jax.ShapeDtypeStruct((3, dsl, f), F32)] * n_fs,
        grid_spec=pltpu.PrefetchScalarGridSpec(
            num_scalar_prefetch=1, grid=(region // TILE - 1,),
            in_specs=[pl.BlockSpec((TILE, d), row_map), pl.BlockSpec((TILE, d), row_map), pl.BlockSpec((TILE, 128), row_map),
                      pl.BlockSpec((d, f), whole), pl.BlockSpec((d, f), whole),
                      pl.BlockSpec((n_fs, f, dsl), whole3)],
            out_specs=[pl.BlockSpec((TILE, d), out_map), pl.BlockSpec((TILE, 128), out_map)]
            + [pl.BlockSpec((3, dsl, f), whole3)] * n_fs,
            scratch_shapes=[pltpu.VMEM((f, d), BF16)] + [pltpu.VMEM((TILE, f), BF16)] * 3 + [pltpu.VMEM((d, f), F32)] * 3),
        compiler_params=pltpu.CompilerParams(vmem_limit_bytes=VMEM_LIMIT, dimension_semantics=("arbitrary",)),
        cost_estimate=pl.CostEstimate(flops=18 * 3000 * d * f, bytes_accessed=24 * d * f, transcendentals=3000 * f),
    )(info, x_pool, dy_pool, r_pool, w1, w3, w2s)


def place_kernel(n_fs, n_loc, k, first, me, *refs):
    pieces = refs[:n_fs]
    n_in = n_fs if first else n_fs + 3
    outs, (turned, sem) = refs[n_in:n_in + 3], refs[n_in + 3:]
    copies = []
    for m in range(n_fs):
        to = (me[0] ^ m) * n_loc + k
        copies.append(pltpu.make_async_copy(pieces[m].at[0], outs[0].at[to], sem))
        copies.append(pltpu.make_async_copy(pieces[m].at[1], outs[1].at[to], sem))
    for copy in copies:
        copy.start()
    for m in range(n_fs):
        turned[m] = pieces[m][2].T
        copies.append(pltpu.make_async_copy(turned.at[m], outs[2].at[(me[0] ^ m) * n_loc + k], sem))
        copies[-1].start()
    for copy in copies:
        copy.wait()


def place(k, n_loc, me, pieces, grads):
    n_fs = len(pieces)
    _, dsl, f = pieces[0].shape
    vmem, hbm = pl.BlockSpec(memory_space=pltpu.VMEM), pl.BlockSpec(memory_space=pl.ANY)
    first = grads is None
    shapes = [(n_fs * n_loc, dsl, f)] * 2 + [(n_fs * n_loc, f, dsl)]
    return pl.pallas_call(
        functools.partial(place_kernel, n_fs, n_loc, k, first),
        out_shape=[jax.ShapeDtypeStruct(v, F32) for v in shapes],
        in_specs=[pl.BlockSpec(memory_space=pltpu.SMEM)] + [vmem] * n_fs + ([] if first else [hbm] * 3),
        out_specs=[hbm] * 3,
        scratch_shapes=[pltpu.VMEM((n_fs, f, dsl), F32), pltpu.SemaphoreType.DMA],
        input_output_aliases={} if first else {n_fs + 1 + t: t for t in range(3)},
        compiler_params=pltpu.CompilerParams(vmem_limit_bytes=VMEM_LIMIT),
        cost_estimate=pl.CostEstimate(flops=0, bytes_accessed=6 * 4 * n_fs * dsl * f, transcendentals=0),
    )(me, *pieces, *([] if first else grads))


def combine_kernel(n_src, n_loc, cnt, off, pos_ref, *refs):
    dx_in, dr_in = refs[:n_loc], refs[n_loc:2 * n_loc]
    out, dr_out, hot, stage, pool, rpool, sem = refs[2 * n_loc:]
    s = pl.program_id(0)
    tok = pos_ref.shape[2]
    d = pool.shape[2]

    @pl.when(s == 0)
    def _():
        def copies(k, i):
            at = pl.ds(aligned(i * TILE, TILE), TILE)
            return [pltpu.make_async_copy(dx_in[k].at[at], pool.at[k, at], sem),
                    pltpu.make_async_copy(dr_in[k].at[at], rpool.at[k, at], sem)]

        tiles = []
        for k in range(n_loc):
            last = (n_src - 1) * n_loc + k
            end = off[last] + blocks(cnt[last], 16) * 16
            tiles.append(jnp.maximum(1, blocks(end, TILE)))
        for k in range(n_loc):
            def start(i, carry, k=k):
                for copy in copies(k, i):
                    copy.start()
                return carry

            lax.fori_loop(0, tiles[k], start, 0)
            at = pl.ds(aligned(tiles[k] * TILE), CHUNK)
            pool[k, at, :] = jnp.zeros((CHUNK, d), BF16)
            rpool[k, at, :] = jnp.zeros((CHUNK, 128), F32)
        for k in range(n_loc):
            def wait(i, carry, k=k):
                for copy in copies(k, i):
                    copy.wait()
                return carry

            lax.fori_loop(0, tiles[k], wait, 0)

    dr_out[...] = jnp.zeros_like(dr_out)
    base = jnp.int32(0)
    for k in range(n_loc):
        n = cnt[s * n_loc + k]
        frm = off[s * n_loc + k]
        pos_row = pos_ref[0, k:k + 1, :]

        def build(c, carry, base=base, frm=frm, pos_row=pos_row, k=k):
            m = one_hot_block(pos_row, c)
            at = pl.ds(aligned(base + c * CHUNK), CHUNK)
            src = pl.ds(aligned(frm + c * CHUNK), CHUNK)
            hot[at, :] = jnp.where(m, 1.0, 0.0).astype(BF16)
            stage[at, :] = pool[k, src, :]
            r = jnp.concatenate([rpool[k, src, :]] * (tok // 128), axis=1)
            dr_out[0, k:k + 1, :] += jnp.sum(jnp.where(m, r, 0.0), axis=0, keepdims=True)
            return carry

        lax.fori_loop(0, blocks(n, CHUNK), build, 0)
        base = base + blocks(n, 16) * 16
    tail = pl.ds(aligned(base), MM)
    hot[tail, :] = jnp.zeros((MM, tok), BF16)
    stage[tail, :] = jnp.zeros((MM, d), BF16)
    out[...] = jnp.zeros_like(out)

    def mm(c, carry):
        at = pl.ds(aligned(c * MM), MM)
        out[...] += dot_tn(hot[at, :], stage[at, :])
        return carry

    lax.fori_loop(0, blocks(base, MM), mm, 0)


def combine_rows(cnt, off, pos, dx_pools, dr_pools, region):
    n_src, n_loc, tok = pos.shape
    d = dx_pools[0].shape[1]
    scr = up(n_loc * ((region - TILE) // n_src) + MM, MM)
    hbm = pl.BlockSpec(memory_space=pl.ANY)
    return pl.pallas_call(
        functools.partial(combine_kernel, n_src, n_loc),
        out_shape=[jax.ShapeDtypeStruct((n_src * tok, d), F32), jax.ShapeDtypeStruct((n_src, n_loc, tok), F32)],
        grid_spec=pltpu.PrefetchScalarGridSpec(
            num_scalar_prefetch=2, grid=(n_src,),
            in_specs=[pl.BlockSpec((1, n_loc, tok), lambda s, *_: (s, 0, 0))] + [hbm] * (2 * n_loc),
            out_specs=[pl.BlockSpec((tok, d), lambda s, *_: (s, 0)),
                       pl.BlockSpec((1, n_loc, tok), lambda s, *_: (s, 0, 0))],
            scratch_shapes=[pltpu.VMEM((scr, tok), BF16), pltpu.VMEM((scr, d), BF16),
                            pltpu.VMEM((n_loc, region, d), BF16), pltpu.VMEM((n_loc, region, 128), F32),
                            pltpu.SemaphoreType.DMA]),
        compiler_params=pltpu.CompilerParams(vmem_limit_bytes=VMEM_LIMIT, dimension_semantics=("arbitrary",)),
        cost_estimate=pl.CostEstimate(flops=2 * 12000 * tok * d, bytes_accessed=n_src * tok * d * 4, transcendentals=0),
        name="combine",
    )(cnt, off, pos, *dx_pools, *dr_pools)


def solution(mesh):
    n_ep, n_fs = mesh.shape["ep"], mesh.shape["fsdp"]
    n_dev = n_ep * n_fs
    both = ("fsdp", "ep")
    tok_spec = P(both, None)
    spec_in = P("ep", "fsdp", None)
    spec_out = P("ep", None, "fsdp")

    def body(x_tok, dy_tok, expert_ids, route_w, w_gate, w_up, w_down):
        tok, top_k = expert_ids.shape
        d = x_tok.shape[1]
        exp_local, _, f = w_gate.shape
        n_loc = exp_local // n_fs
        experts = exp_local * n_ep
        capacity = capacity_of(tok, top_k, experts)
        region = n_dev * up(capacity, 16) + TILE

        position, weight = route_tables(expert_ids, route_w, experts, capacity)
        table = jnp.stack([position, weight], axis=1).reshape(n_ep, n_fs, n_loc, 2, tok)
        table = table.transpose(1, 0, 2, 3, 4).reshape(n_dev, n_loc * 2, tok)
        table = lax.all_to_all(table, both, 0, 0, tiled=True).reshape(n_dev, n_loc, 2, tok)
        x_all = lax.all_gather(x_tok, both, axis=0, tiled=True)
        dy_all = lax.all_gather(dy_tok, both, axis=0, tiled=True)

        def to_owner(w):
            return lax.all_to_all(w.reshape(n_fs, n_loc, *w.shape[1:]), "fsdp", 0, 0, tiled=True)

        wg, wu, wd = to_owner(w_gate), to_owner(w_up), to_owner(w_down)

        pos = table[:, :, 0, :].astype(jnp.int32)
        r = table[:, :, 1, :]
        cnt = jnp.max(pos, axis=2) + 1
        padded = blocks(cnt, 16) * 16
        off = jnp.cumsum(padded, axis=0) - padded
        rows = jnp.sum(padded, axis=0)
        cnt_flat, off_flat = cnt.reshape(-1), off.reshape(-1)
        x_pool = gather_rows(x_all, cnt_flat, off_flat, pos, None, region)
        dy_pool, r_pool = gather_rows(dy_all, cnt_flat, off_flat, pos, r, region)

        me = lax.axis_index("fsdp").astype(jnp.int32)
        dx_pools, dr_pools, pieces = [], [], []
        for k in range(n_loc):
            info = jnp.stack([rows[k], jnp.maximum(1, blocks(rows[k], TILE)), me])
            w1, w3, w2s = wg[:, k].reshape(d, f), wu[:, k].reshape(d, f), wd[:, k]
            dxk, drk, *slices = expert_call(k, info, x_pool, dy_pool, r_pool, w1, w3, w2s, region)
            dx_pools.append(dxk)
            dr_pools.append(drk)
            pieces.append([slices[0]] + [lax.ppermute(slices[m], "fsdp", [(i, i ^ m) for i in range(n_fs)])
                                         for m in range(1, n_fs)])
        dx_part, dr_part = combine_rows(cnt_flat, off_flat, pos, dx_pools, dr_pools, region)
        grad_x = lax.psum_scatter(dx_part, both, scatter_dimension=0, tiled=True).astype(BF16)
        dr_home = lax.all_to_all(dr_part, both, 0, 0, tiled=True)
        dr_home = dr_home.reshape(n_fs, n_ep, n_loc, tok).transpose(1, 0, 2, 3).reshape(experts, tok)
        hit = expert_ids.T[:, None, :] == jnp.arange(experts, dtype=jnp.int32)[None, :, None]
        route_grad = jnp.sum(jnp.where(hit, dr_home[None], 0.0), axis=1).T
        grads = None
        for k in range(n_loc):
            grads = place(k, n_loc, me.reshape(1), pieces[k], grads)
        return grad_x, route_grad, *grads

    return jax.shard_map(
        body, mesh=mesh,
        in_specs=(tok_spec, tok_spec, tok_spec, tok_spec, spec_in, spec_in, spec_out),
        out_specs=(tok_spec, tok_spec, spec_in, spec_in, spec_out),
        check_vma=False)
```

time: 2390 us -> 1090 us (0.46)
  the two profiles are of different devices: /device:TPU:0 before, /device:TPU:15 now
where the time goes in v1:
time: 1090 us
  blocking collectives  593 us (54%)
  Pallas kernels  231 us (21%)
  waiting for transfers between devices  129 us (12%)
  starting transfers between devices  91.1 us (8%)
  between operations  16.9 us (2%)
  local copies, waits for them, and re-layouts  16.8 us (2%)
    all_to_all x1, blocking collectives, body(): dr_home = lax.all_to_all(dr_part, both, 0, 0, tiled=True)  403 us
    all_to_all x2, blocking collectives, to_owner(): lax.all_to_all(w.reshape(n_fs, n_loc, *w.shape[1:]), 'fsdp', 0, 0, tiled=...  177 us
    pallas_call x4, Pallas kernels, expert_call(): pl.pallas_call(functools.partial(expert_kernel, n_fs), out_shape=[jax.Sha...  117 us
    ppermute x12, starting transfers between devices, body(): lax.ppermute(slices[m], 'fsdp', [(i, i ^ m) for i in range(n_fs)])  84.5 us
    ppermute x12, waiting for transfers between devices, body(): lax.ppermute(slices[m], 'fsdp', [(i, i ^ m) for i in range(n_fs)])  66.9 us
    all_to_all x1, waiting for transfers between devices, to_owner(): lax.all_to_all(w.reshape(n_fs, n_loc, *w.shape[1:]), 'fsdp', 0, 0, tiled=...  60.5 us
    pallas_call x2, Pallas kernels, gather_rows(): pl.pallas_call(functools.partial(gather_kernel, n_src, n_loc, region, wit...  56.9 us
    pallas_call x1, Pallas kernels, combine_rows(): pl.pallas_call(functools.partial(combine_kernel, n_src, n_loc), out_shape...  31.8 us
  transfers between devices with their start and end apart: 16, of which 5 were waited for; matrix products, arithmetic and copies ran while one was open for 2% of the time, Pallas kernels for 5%

profile of v1, /device:TPU:15, one launch (start us, length us, event | category | flops | bytes accessed | tf_op | source)
XLA Modules:
  0.0 1088.2 jit_solution(8486392006864842221)
XLA Ops:
  7.2 0.7 all-gather.3.cloned.1.call-update
  8.0 0.7 all-gather.5.cloned.1.call-update
  9.0 0.4 and_select_fusion
  10.0 0.4 copy.48
  10.4 0.4 reshape.58
  10.8 12.5 %all_to_all.25 = f32[16,8,1024]{2,1,0:T(8,128)S(1)} all-to-all(f32[16,8,1024]{2,1,0:T(8,128)S(1)} %reshape.58), channel_id=1, replica_groups=mesh['fsdp'=4,'ep'=4] {'fsdp','ep'}, dimensions={0} | all-to-all | bytes 1048576 | tf_op jit(solution)/shard_map/all_to_all | solution.py:403
  23.3 96.0 %all_to_all.26 = bf16[4,4,128,1280]{3,2,1,0:T(8,128)(2,1)} all-to-all(bf16[4,4,128,1280]{3,2,1,0:T(8,128)(2,1)} %bitcast.54), channel_id=1, replica_groups=mesh['fsdp'=4,'ep'=4] {'fsdp'}, dimensions={0} | all-to-all | bytes 10485760 | tf_op jit(solution)/shard_map/all_to_all | solution.py:408
  119.3 81.4 %all_to_all.27 = bf16[4,4,128,1280]{3,2,1,0:T(8,128)(2,1)} all-to-all(bf16[4,4,128,1280]{3,2,1,0:T(8,128)(2,1)S(1)} %bitcast.57), channel_id=1, replica_groups=mesh['fsdp'=4,'ep'=4] {'fsdp'}, dimensions={0} | all-to-all | bytes 10485760 | tf_op jit(solution)/shard_map/all_to_all | solution.py:408
  200.7 6.5 all-to-all-start.3
  207.2 0.3 copy.49
  207.6 0.4 fusion.3
  208.0 0.6 fusion.13
  211.2 0.9 copy.70
  212.1 0.6 add.56.refs_0_.cnt
  212.9 1.9 add_add_fusion.2
  214.9 1.9 add_add_fusion
  216.8 0.6 fusion.8.refs_1_.off
  217.4 0.9 fusion.2.refs_2_.pos_ref
  218.2 5.4 fusion.11
  223.7 2.4 fusion.10
  226.1 60.5 %all-to-all-done.3 = bf16[4,4,1280,128]{3,2,1,0:T(8,128)(2,1)} async-done(((bf16[4,4,1280,128]{3,2,1,0:T(8,128)(2,1)}), bf16[4,4,1280,128]{3,2,1,0:T(8,128)(2,1)}, u32[]{:S(2)}, u32[]{:S(2)}) %all-to-all-start.3) | async-done | bytes 5242912 | tf_op jit(solution)/shard_map/all_to_all | solution.py:408
  286.7 4.9 slice_bitcast_fusion
  291.6 24.7 %gather_x.1.x_ref = bf16[26624,512]{1,0:T(8,128)(2,1)} custom-call(s32[64]{0:T(128)} %add.56.refs_0_.cnt, s32[64]{0:T(128)} %fusion.8.refs_1_.off, s32[16,4,1024]{2,1,0:T(4,128)} %fusion.2.refs_2_.pos_ref, bf16[16384,512]{1,0:T(8,128)(2,1)} %all-gather.3.cloned.1.call-done.refs_3_), custom_call_target="tpu_custom_call" | custom-call | flops 12582912000 | bytes 33554432 | tf_op jit(solution)/shard_map/gather_x/pallas_call | solution.py:159
  316.3 32.2 %gather_r.1 = (bf16[26624,512]{1,0:T(8,128)(2,1)}, f32[26624,128]{1,0:T(8,128)}) custom-call(s32[64]{0:T(128)} %add.56.refs_0_.cnt, s32[64]{0:T(128)} %fusion.8.refs_1_.off, s32[16,4,1024]{2,1,0:T(4,128)} %fusion.2.refs_2_.pos_ref, f32[16,4,1024]{2,1,0:T(4,128)} %bitcast.73, bf16[16384,512]{1,0:T(8,128)(2,1)} %all-gather.5.cloned.1.call-done.refs_4_), custom_call_target="tpu_custom_call" | custom-call | flops 12582912000 | bytes 33554432 | tf_op jit(solution)/shard_map/gather_r/pallas_call | solution.py:159
  348.5 29.0 %shard_map.113 = (bf16[6656,512]{1,0:T(8,128)(2,1)}, f32[6656,128]{1,0:T(8,128)}, f32[3,128,1280]{2,1,0:T(8,128)}, f32[3,128,1280]{2,1,0:T(8,128)}, f32[3,128,1280]{2,1,0:T(8,128)}, /*index=5*/f32[3,128,1280]{2,1,0:T(8,128)}) custom-call(s32[3]{0:T(128)} %get-tuple-element.110.info, bf16[26624,512]{1,0:T(8,128)(2,1)} %gather_x.1.x_ref, ...), custom_call_target="tpu_custom_call" | custom-call | flops 35389440000 | bytes 15728640 | tf_op jit(solution)/shard_map/pallas_call | solution.py:238
  377.5 29.1 %shard_map.112 = (bf16[6656,512]{1,0:T(8,128)(2,1)}, f32[6656,128]{1,0:T(8,128)}, f32[3,128,1280]{2,1,0:T(8,128)}, f32[3,128,1280]{2,1,0:T(8,128)}, f32[3,128,1280]{2,1,0:T(8,128)}, /*index=5*/f32[3,128,1280]{2,1,0:T(8,128)}) custom-call(s32[3]{0:T(128)} %get-tuple-element.109.info, bf16[26624,512]{1,0:T(8,128)(2,1)} %gather_x.1.x_ref, ...), custom_call_target="tpu_custom_call" | custom-call | flops 35389440000 | bytes 15728640 | tf_op jit(solution)/shard_map/pallas_call | solution.py:238
  406.6 29.4 %shard_map.111 = (bf16[6656,512]{1,0:T(8,128)(2,1)}, f32[6656,128]{1,0:T(8,128)}, f32[3,128,1280]{2,1,0:T(8,128)}, f32[3,128,1280]{2,1,0:T(8,128)}, f32[3,128,1280]{2,1,0:T(8,128)}, /*index=5*/f32[3,128,1280]{2,1,0:T(8,128)}) custom-call(s32[3]{0:T(128)} %get-tuple-element.108.info, bf16[26624,512]{1,0:T(8,128)(2,1)} %gather_x.1.x_ref, ...), custom_call_target="tpu_custom_call" | custom-call | flops 35389440000 | bytes 15728640 | tf_op jit(solution)/shard_map/pallas_call | solution.py:238
  436.0 29.1 %shard_map.110 = (bf16[6656,512]{1,0:T(8,128)(2,1)}, f32[6656,128]{1,0:T(8,128)}, f32[3,128,1280]{2,1,0:T(8,128)}, f32[3,128,1280]{2,1,0:T(8,128)}, f32[3,128,1280]{2,1,0:T(8,128)}, /*index=5*/f32[3,128,1280]{2,1,0:T(8,128)}) custom-call(s32[3]{0:T(128)} %get-tuple-element.107.info, bf16[26624,512]{1,0:T(8,128)(2,1)} %gather_x.1.x_ref, ...), custom_call_target="tpu_custom_call" | custom-call | flops 35389440000 | bytes 15728640 | tf_op jit(solution)/shard_map/pallas_call | solution.py:238
  465.1 31.8 %combine.1 = (f32[16384,512]{1,0:T(8,128)}, f32[16,4,1024]{2,1,0:T(4,128)}) custom-call(s32[64]{0:T(128)} %add.56.refs_0_.cnt, s32[64]{0:T(128)} %fusion.8.refs_1_.off, s32[16,4,1024]{2,1,0:T(4,128)} %fusion.2.refs_2_.pos_ref, bf16[6656,512]{1,0:T(8,128)(2,1)} %get-tuple-element.47.refs_0_, bf16[6656,512]{1,0:T(8,128)(2,1)} %get-tuple-element.48.refs_1_, ...), custom_call_target="tpu_custom_call" | custom-call | flops 12582912000 | bytes 33554432 | tf_op jit(solution)/shard_map/combine/pallas_call | solution.py:366
  496.9 1.8 collective-permute-start.3
  498.8 1.4 collective-permute-start.7
  500.2 1.2 collective-permute-start.8
  501.4 19.5 %collective-permute-done.3.refs_1_ = f32[3,128,1280]{2,1,0:T(8,128)S(1)} collective-permute-done((f32[3,128,1280]{2,1,0:T(8,128)}, f32[3,128,1280]{2,1,0:T(8,128)S(1)}, u32[]{:S(2)}, u32[]{:S(2)}) %collective-permute-start.3) | collective-permute-done | bytes 1966112 | tf_op jit(solution)/shard_map/ppermute | solution.py:430
  521.0 18.1 %collective-permute-start.10 = (f32[3,128,1280]{2,1,0:T(8,128)}, f32[3,128,1280]{2,1,0:T(8,128)}, u32[]{:S(2)}, u32[]{:S(2)}) collective-permute-start(f32[3,128,1280]{2,1,0:T(8,128)} %get-tuple-element.71), channel_id=1, source_target_pairs={{0,8},{4,12},{8,0},{12,4},{1,9},{5,13},{9,1},{13,5},{2,10},{6,14},... | collective-permute-start | bytes 5898248 | tf_op jit(solution)/shard_map/ppermute | solution.py:430
  539.0 3.0 collective-permute-done.6.refs_1_
  542.0 40.2 %collective-permute-start.11 = (f32[3,128,1280]{2,1,0:T(8,128)}, f32[3,128,1280]{2,1,0:T(8,128)}, u32[]{:S(2)}, u32[]{:S(2)}) collective-permute-start(f32[3,128,1280]{2,1,0:T(8,128)} %get-tuple-element.72), channel_id=1, source_target_pairs={{0,12},{4,8},{8,4},{12,0},{1,13},{5,9},{9,5},{13,1},{2,14},{6,10},... | collective-permute-start | bytes 5898248 | tf_op jit(solution)/shard_map/ppermute | solution.py:430
  582.2 24.3 %collective-permute-done.8.refs_3_ = f32[3,128,1280]{2,1,0:T(8,128)S(1)} collective-permute-done((f32[3,128,1280]{2,1,0:T(8,128)}, f32[3,128,1280]{2,1,0:T(8,128)S(1)}, u32[]{:S(2)}, u32[]{:S(2)}) %collective-permute-start.8) | collective-permute-done | bytes 1966112 | tf_op jit(solution)/shard_map/ppermute | solution.py:430
  606.5 0.9 collective-permute-start
  607.4 0.4 copy-done.4
  607.8 20.9 %collective-permute-start.1 = (f32[3,128,1280]{2,1,0:T(8,128)}, f32[3,128,1280]{2,1,0:T(8,128)}, u32[]{:S(2)}, u32[]{:S(2)}) collective-permute-start(f32[3,128,1280]{2,1,0:T(8,128)} %get-tuple-element.59), channel_id=1, source_target_pairs={{0,8},{4,12},{8,0},{12,4},{1,9},{5,13},{9,1},{13,5},{2,10},{6,14},... | collective-permute-start | bytes 5898248 | tf_op jit(solution)/shard_map/ppermute | solution.py:430
  628.7 20.1 %collective-permute-done.11.refs_3_ = f32[3,128,1280]{2,1,0:T(8,128)} collective-permute-done((f32[3,128,1280]{2,1,0:T(8,128)}, f32[3,128,1280]{2,1,0:T(8,128)}, u32[]{:S(2)}, u32[]{:S(2)}) %collective-permute-start.11) | collective-permute-done | bytes 1966112 | tf_op jit(solution)/shard_map/ppermute | solution.py:430
  648.8 403.0 %all_to_all.28 = f32[16,4,1024]{2,1,0:T(4,128)S(1)} all-to-all(f32[16,4,1024]{2,1,0:T(4,128)S(1)} %copy-done.7), channel_id=1, replica_groups=mesh['fsdp'=4,'ep'=4] {'fsdp','ep'}, dimensions={0} | all-to-all | bytes 524288 | tf_op jit(solution)/shard_map/all_to_all | solution.py:434
  1051.9 0.9 select_reduce_fusion
  1052.9 6.4 shard_map.114
  1059.3 6.5 shard_map.115
  1065.8 6.5 shard_map.116
  1072.3 6.5 shard_map.117
  1078.8 2.7 convert_element_type.12
  (59 shorter events, 1.6 us)
Async XLA Ops:
  7.2 1.5 copy-start.5
  7.2 284.4 %all-gather.3.cloned.1.call-start = ((), (), s32[]{:S(2)}) async-start(), calls=%async_computation.6 | async-start | bytes 17825792 | tf_op jit(solution)/shard_map/all_gather | solution.py:404
  7.9 1.6 copy-start.8
  7.9 308.4 %all-gather.5.cloned.1.call-start = ((), (), s32[]{:S(2)}) async-start(), calls=%async_computation.7 | async-start | bytes 17825792 | tf_op jit(solution)/shard_map/all_gather | solution.py:405
  10.8 108.5 %slice-start.2 = ((s8[5242880]{0:T(1024)(128)(4,1)}), s8[4194304]{0:T(1024)(128)(4,1)S(1)}, s32[]{:S(2)}) async-start(s8[5242880]{0:T(1024)(128)(4,1)} %bitcast.55), calls=%async_computation.11 | async-start | bytes 8388608
  23.3 96.0 %slice-start.3 = ((s8[5242880]{0:T(1024)(128)(4,1)}), s8[1048576]{0:T(1024)(128)(4,1)S(1)}, s32[]{:S(2)}) async-start(s8[5242880]{0:T(1024)(128)(4,1)} %bitcast.55), calls=%async_computation.12 | async-start | bytes 2097152
  200.7 86.0 %all-to-all-start.3 = ((bf16[4,4,1280,128]{3,2,1,0:T(8,128)(2,1)}), bf16[4,4,1280,128]{3,2,1,0:T(8,128)(2,1)}, u32[]{:S(2)}, u32[]{:S(2)}) async-start(bf16[4,4,1280,128]{3,2,1,0:T(8,128)(2,1)} %bitcast.58), calls=%async_computation.3 | async-start | bytes 10485760 | tf_op jit(solution)/shard_map/all_to_all | solution.py:408
  207.2 871.5 %reduce-scatter.2.cloned.1.call-start = ((), (), s32[]{:S(2)}) async-start(), calls=%async_computation.8 | async-start | bytes 35651584 | tf_op jit(solution)/shard_map/reduce_scatter | solution.py:433
  217.4 6.3 slice-start
  218.2 5.4 slice-start.1
  496.9 151.9 %copy-start.7 = (f32[16,4,1024]{2,1,0:T(4,128)S(1)}, f32[16,4,1024]{2,1,0:T(4,128)}, u32[]{:S(2)}) copy-start(f32[16,4,1024]{2,1,0:T(4,128)} %get-tuple-element.56) | copy-start | bytes 786436
  496.9 555.0 %copy-start.6 = (s32[1024,8]{0,1:T(8,128)S(1)}, s32[1024,8]{0,1:T(8,128)}, u32[]{:S(2)}) copy-start(s32[1024,8]{0,1:T(8,128)} %param.9) | copy-start | bytes 98308
  496.9 24.0 %collective-permute-start.3 = (f32[3,128,1280]{2,1,0:T(8,128)}, f32[3,128,1280]{2,1,0:T(8,128)S(1)}, u32[]{:S(2)}, u32[]{:S(2)}) collective-permute-start(f32[3,128,1280]{2,1,0:T(8,128)} %get-tuple-element.62), channel_id=1, source_target_pairs={{0,4},{4,0},{8,12},{12,8},{1,5},{5,1},{9,13},{13,9},{2,6},{6,2},{1... | collective-permute-start | bytes 5898248 | tf_op jit(solution)/shard_map/ppermute | solution.py:430
  498.7 43.3 %collective-permute-start.6 = (f32[3,128,1280]{2,1,0:T(8,128)}, f32[3,128,1280]{2,1,0:T(8,128)S(1)}, u32[]{:S(2)}, u32[]{:S(2)}) collective-permute-start(f32[3,128,1280]{2,1,0:T(8,128)} %get-tuple-element.66), channel_id=1, source_target_pairs={{0,4},{4,0},{8,12},{12,8},{1,5},{5,1},{9,13},{13,9},{2,6},{6,2},{1... | collective-permute-start | bytes 5898248 | tf_op jit(solution)/shard_map/ppermute | solution.py:430
  498.8 83.4 %collective-permute-start.7 = (f32[3,128,1280]{2,1,0:T(8,128)}, f32[3,128,1280]{2,1,0:T(8,128)S(1)}, u32[]{:S(2)}, u32[]{:S(2)}) collective-permute-start(f32[3,128,1280]{2,1,0:T(8,128)} %get-tuple-element.67), channel_id=1, source_target_pairs={{0,8},{4,12},{8,0},{12,4},{1,9},{5,13},{9,1},{13,5},{2,10},{6,14},... | collective-permute-start | bytes 5898248 | tf_op jit(solution)/shard_map/ppermute | solution.py:430
  500.2 106.3 %collective-permute-start.8 = (f32[3,128,1280]{2,1,0:T(8,128)}, f32[3,128,1280]{2,1,0:T(8,128)S(1)}, u32[]{:S(2)}, u32[]{:S(2)}) collective-permute-start(f32[3,128,1280]{2,1,0:T(8,128)} %get-tuple-element.68), channel_id=1, source_target_pairs={{0,12},{4,8},{8,4},{12,0},{1,13},{5,9},{9,5},{13,1},{2,14},{6,10},... | collective-permute-start | bytes 5898248 | tf_op jit(solution)/shard_map/ppermute | solution.py:430
  501.4 105.1 %collective-permute-start.9 = (f32[3,128,1280]{2,1,0:T(8,128)}, f32[3,128,1280]{2,1,0:T(8,128)S(1)}, u32[]{:S(2)}, u32[]{:S(2)}) collective-permute-start(f32[3,128,1280]{2,1,0:T(8,128)} %get-tuple-element.70), channel_id=1, source_target_pairs={{0,4},{4,0},{8,12},{12,8},{1,5},{5,1},{9,13},{13,9},{2,6},{6,2},{1... | collective-permute-start | bytes 5898248 | tf_op jit(solution)/shard_map/ppermute | solution.py:430
  521.0 85.5 %copy-start.1 = (f32[3,128,1280]{2,1,0:T(8,128)}, f32[3,128,1280]{2,1,0:T(8,128)S(1)}, u32[]{:S(2)}) copy-start(f32[3,128,1280]{2,1,0:T(8,128)S(1)} %collective-permute-done.3.refs_1_) | copy-start | bytes 5898244
  521.0 86.4 %collective-permute-start.10 = (f32[3,128,1280]{2,1,0:T(8,128)}, f32[3,128,1280]{2,1,0:T(8,128)}, u32[]{:S(2)}, u32[]{:S(2)}) collective-permute-start(f32[3,128,1280]{2,1,0:T(8,128)} %get-tuple-element.71), channel_id=1, source_target_pairs={{0,8},{4,12},{8,0},{12,4},{1,9},{5,13},{9,1},{13,5},{2,10},{6,14},... | collective-permute-start | bytes 5898248 | tf_op jit(solution)/shard_map/ppermute | solution.py:430
  542.0 64.5 %copy-start.2 = (f32[3,128,1280]{2,1,0:T(8,128)}, f32[3,128,1280]{2,1,0:T(8,128)S(1)}, u32[]{:S(2)}) copy-start(f32[3,128,1280]{2,1,0:T(8,128)S(1)} %collective-permute-done.6.refs_1_) | copy-start | bytes 5898244
  542.0 106.7 %collective-permute-start.11 = (f32[3,128,1280]{2,1,0:T(8,128)}, f32[3,128,1280]{2,1,0:T(8,128)}, u32[]{:S(2)}, u32[]{:S(2)}) collective-permute-start(f32[3,128,1280]{2,1,0:T(8,128)} %get-tuple-element.72), channel_id=1, source_target_pairs={{0,12},{4,8},{8,4},{12,0},{1,13},{5,9},{9,5},{13,1},{2,14},{6,10},... | collective-permute-start | bytes 5898248 | tf_op jit(solution)/shard_map/ppermute | solution.py:430
  582.2 25.2 %copy-start.3 = (f32[3,128,1280]{2,1,0:T(8,128)}, f32[3,128,1280]{2,1,0:T(8,128)S(1)}, u32[]{:S(2)}) copy-start(f32[3,128,1280]{2,1,0:T(8,128)S(1)} %collective-permute-done.7.refs_2_) | copy-start | bytes 5898244
  582.2 483.6 %collective-permute-start.4 = (f32[3,128,1280]{2,1,0:T(8,128)}, f32[3,128,1280]{2,1,0:T(8,128)}, u32[]{:S(2)}, u32[]{:S(2)}) collective-permute-start(f32[3,128,1280]{2,1,0:T(8,128)} %get-tuple-element.63), channel_id=1, source_target_pairs={{0,8},{4,12},{8,0},{12,4},{1,9},{5,13},{9,1},{13,5},{2,10},{6,14},... | collective-permute-start | bytes 5898248 | tf_op jit(solution)/shard_map/ppermute | solution.py:430
  606.5 1.3 copy-start.4
  606.5 459.3 %collective-permute-start.5 = (f32[3,128,1280]{2,1,0:T(8,128)}, f32[3,128,1280]{2,1,0:T(8,128)}, u32[]{:S(2)}, u32[]{:S(2)}) collective-permute-start(f32[3,128,1280]{2,1,0:T(8,128)} %get-tuple-element.64), channel_id=1, source_target_pairs={{0,12},{4,8},{8,4},{12,0},{1,13},{5,9},{9,5},{13,1},{2,14},{6,10},... | collective-permute-start | bytes 5898248 | tf_op jit(solution)/shard_map/ppermute | solution.py:430
  606.5 446.3 %copy-start = (f32[3,128,1280]{2,1,0:T(8,128)}, f32[3,128,1280]{2,1,0:T(8,128)S(1)}, u32[]{:S(2)}) copy-start(f32[3,128,1280]{2,1,0:T(8,128)S(1)} %collective-permute-done.9.refs_1_) | copy-start | bytes 5898244
  606.5 465.7 %collective-permute-start = (f32[3,128,1280]{2,1,0:T(8,128)}, f32[3,128,1280]{2,1,0:T(8,128)}, u32[]{:S(2)}, u32[]{:S(2)}) collective-permute-start(f32[3,128,1280]{2,1,0:T(8,128)} %get-tuple-element.58), channel_id=1, source_target_pairs={{0,4},{4,0},{8,12},{12,8},{1,5},{5,1},{9,13},{13,9},{2,6},{6,2},{1... | collective-permute-start | bytes 5898248 | tf_op jit(solution)/shard_map/ppermute | solution.py:430
  607.8 464.5 %collective-permute-start.1 = (f32[3,128,1280]{2,1,0:T(8,128)}, f32[3,128,1280]{2,1,0:T(8,128)}, u32[]{:S(2)}, u32[]{:S(2)}) collective-permute-start(f32[3,128,1280]{2,1,0:T(8,128)} %get-tuple-element.59), channel_id=1, source_target_pairs={{0,8},{4,12},{8,0},{12,4},{1,9},{5,13},{9,1},{13,5},{2,10},{6,14},... | collective-permute-start | bytes 5898248 | tf_op jit(solution)/shard_map/ppermute | solution.py:430
  648.8 423.5 %collective-permute-start.2 = (f32[3,128,1280]{2,1,0:T(8,128)}, f32[3,128,1280]{2,1,0:T(8,128)}, u32[]{:S(2)}, u32[]{:S(2)}) collective-permute-start(f32[3,128,1280]{2,1,0:T(8,128)} %get-tuple-element.60), channel_id=1, source_target_pairs={{0,12},{4,8},{8,4},{12,0},{1,13},{5,9},{9,5},{13,1},{2,14},{6,10},... | collective-permute-start | bytes 5898248 | tf_op jit(solution)/shard_map/ppermute | solution.py:430
Sparse Core Ops, SparseCore 0:
  10.2 139.9 all-gather.2
  152.5 148.9 all-gather.4
  497.1 543.8 reduce-scatter.1

commit v2 on v1

--- a/solution.py
+++ b/solution.py
@@ -170,8 +170,9 @@
     return out if with_r else out[0]
 
 
-def expert_kernel(n_fs, info, x_ref, dy_ref, r_ref, w1_ref, w3_ref, w2s_ref, dx_ref, dr_ref, *refs):
-    outs, (w2, a_buf, dh1_buf, dh3_buf, dw1, dw3, dw2t) = refs[:n_fs], refs[n_fs:]
+def expert_kernel(n_fs, info, x_ref, dy_ref, r_ref, *refs):
+    gu_refs, down_refs, (dx_ref, dr_ref) = refs[:n_fs], refs[n_fs:2 * n_fs], refs[2 * n_fs:2 * n_fs + 2]
+    outs, (w1_ref, w3_ref, w2, a_buf, dh1_buf, dh3_buf, dw1, dw3, dw2t) = refs[2 * n_fs + 2:3 * n_fs + 2], refs[3 * n_fs + 2:]
     i = pl.program_id(0)
     d, f = w1_ref.shape
     dsl = d // n_fs
@@ -181,8 +182,11 @@
         dw1[...] = jnp.zeros_like(dw1)
         dw3[...] = jnp.zeros_like(dw3)
         dw2t[...] = jnp.zeros_like(dw2t)
-        for q in range(n_fs):
-            w2[:, q * dsl:(q + 1) * dsl] = w2s_ref[q]
+        for m in range(n_fs):
+            at = pl.ds(aligned((info[2] ^ m) * dsl, dsl), dsl)
+            w1_ref[at, :] = gu_refs[m][0]
+            w3_ref[at, :] = gu_refs[m][1]
+            w2[:, at] = down_refs[m][...]
 
     def tile(m):
         x, dy = x_ref[:m, :], dy_ref[:m, :]
@@ -227,9 +231,9 @@
                 outs[m][t] = acc[at, :]
 
 
-def expert_call(k, info, x_pool, dy_pool, r_pool, w1, w3, w2s, region):
-    n_fs, f, dsl = w2s.shape
-    d = w1.shape[0]
+def expert_call(k, info, x_pool, dy_pool, r_pool, gate_up, down, region):
+    n_fs, (f, dsl) = len(down), down[0].shape
+    d = n_fs * dsl
     first = k * (region // TILE)
     row_map = lambda i, info: (first + jnp.minimum(i, info[1] - 1), 0)
     out_map = lambda i, info: (jnp.minimum(i, info[1] - 1), 0)
@@ -242,14 +246,13 @@
         grid_spec=pltpu.PrefetchScalarGridSpec(
             num_scalar_prefetch=1, grid=(region // TILE - 1,),
             in_specs=[pl.BlockSpec((TILE, d), row_map), pl.BlockSpec((TILE, d), row_map), pl.BlockSpec((TILE, 128), row_map),
-                      pl.BlockSpec((d, f), whole), pl.BlockSpec((d, f), whole),
-                      pl.BlockSpec((n_fs, f, dsl), whole3)],
+                      *[pl.BlockSpec((2, dsl, f), whole3)] * n_fs, *[pl.BlockSpec((f, dsl), whole)] * n_fs],
             out_specs=[pl.BlockSpec((TILE, d), out_map), pl.BlockSpec((TILE, 128), out_map)]
             + [pl.BlockSpec((3, dsl, f), whole3)] * n_fs,
-            scratch_shapes=[pltpu.VMEM((f, d), BF16)] + [pltpu.VMEM((TILE, f), BF16)] * 3 + [pltpu.VMEM((d, f), F32)] * 3),
+            scratch_shapes=[pltpu.VMEM((d, f), BF16)] * 2 + [pltpu.VMEM((f, d), BF16)] + [pltpu.VMEM((TILE, f), BF16)] * 3 + [pltpu.VMEM((d, f), F32)] * 3),
         compiler_params=pltpu.CompilerParams(vmem_limit_bytes=VMEM_LIMIT, dimension_semantics=("arbitrary",)),
         cost_estimate=pl.CostEstimate(flops=18 * 3000 * d * f, bytes_accessed=24 * d * f, transcendentals=3000 * f),
-    )(info, x_pool, dy_pool, r_pool, w1, w3, w2s)
+    )(info, x_pool, dy_pool, r_pool, *gate_up, *down)
 
 
 def place_kernel(n_fs, n_loc, k, first, me, *refs):
@@ -380,6 +383,229 @@
     )(cnt, off, pos, *dx_pools, *dr_pools)
 
 
+MESH = pl.DeviceIdType.MESH
+HOPS = ((0, 2), (1, 0), (2, 0))
+SIBLING = (0, 1)
+ORDERS = ((0, 1, 2), (1, 2, 0), (2, 0, 1))
+
+
+def here():
+    return lax.axis_index("fsdp"), lax.axis_index("ep")
+
+
+def peer_of(hop):
+    f, p = here()
+    return {"fsdp": f ^ hop[0], "ep": p ^ hop[1]}
+
+
+def block_of(bits, core=0):
+    f, p = here()
+    for axis in range(3):
+        if bits >> axis & 1:
+            f, p = f ^ HOPS[axis][0], p ^ HOPS[axis][1]
+    return f * 4 + (p ^ core)
+
+
+def enter(n_fs, n_ep):
+    barrier = pltpu.get_barrier_semaphore()
+    for df in range(n_fs):
+        for dp in range(n_ep):
+            if df or dp:
+                pl.semaphore_signal(barrier, inc=1, device_id=peer_of((df, dp)), device_id_type=MESH)
+    pl.semaphore_wait(barrier, n_fs * n_ep - 1)
+
+
+def exchange(n_fs, n_ep, src, dst, send, recv):
+    f, p = here()
+    copies = []
+    for df in range(n_fs):
+        for dp in range(n_ep):
+            if df or dp:
+                n = df * n_ep + dp
+                copies.append(pltpu.make_async_remote_copy(
+                    src_ref=src.at[(f ^ df) * n_ep + (p ^ dp)], dst_ref=dst.at[f * n_ep + p],
+                    send_sem=send.at[n], recv_sem=recv.at[n], device_id=peer_of((df, dp)), device_id_type=MESH))
+                copies[-1].start()
+    return copies
+
+
+def spread_kernel(n_fs, n_ep, parts, x_ref, dy_ref, table_ref, x_all, dy_all, table_all,
+                  send, recv, c_send, c_recv, t_send, t_recv, own_sem):
+    tok = x_ref.shape[0]
+    mine = block_of(0)
+    enter(n_fs, n_ep)
+    pending = []
+    local = []
+    for n, (src, dst) in enumerate(((x_ref, x_all), (dy_ref, dy_all))):
+        local.append(pltpu.make_async_copy(src, dst.at[pl.ds(aligned(mine * tok, tok), tok)], own_sem.at[n]))
+    local.append(pltpu.make_async_copy(table_ref.at[mine], table_all.at[mine], own_sem.at[2]))
+    for copy in local:
+        copy.start()
+    pending += exchange(n_fs, n_ep, table_ref, table_all, t_send, t_recv)
+    arrays = ((x_ref, x_all), (dy_ref, dy_all))
+    starts = [sum(parts[:q]) for q in range(3)]
+    sem_at = {}
+    inbound = {}
+
+    def send_on(a, q, phase, bits):
+        own, full = arrays[a]
+        to = pl.ds(aligned(block_of(bits) * tok + starts[q], 16), parts[q])
+        src = own.at[pl.ds(starts[q], parts[q])] if bits == 0 else full.at[to]
+        n = sem_at.setdefault((a, q, phase, bits), len(sem_at))
+        copy = pltpu.make_async_remote_copy(
+            src_ref=src, dst_ref=full.at[to], send_sem=send.at[n], recv_sem=recv.at[n],
+            device_id=peer_of(HOPS[ORDERS[q][phase]]), device_id_type=MESH)
+        copy.start()
+        inbound[(a, q, phase, bits)] = copy
+
+    shared = []
+
+    def share(a, q, bits):
+        own, full = arrays[a]
+        to = pl.ds(aligned(block_of(bits) * tok + starts[q], 16), parts[q])
+        src = own.at[pl.ds(starts[q], parts[q])] if bits == 0 else full.at[to]
+        n = len(shared)
+        copy = pltpu.make_async_remote_copy(
+            src_ref=src, dst_ref=full.at[to], send_sem=c_send.at[n], recv_sem=c_recv.at[n],
+            device_id=peer_of(SIBLING), device_id_type=MESH)
+        copy.start()
+        shared.append(copy)
+
+    for phase in range(3):
+        for a in range(2):
+            for q in range(3):
+                send_on(a, q, phase, 0)
+    for a in range(2):
+        for q in range(3):
+            share(a, q, 0)
+    for phase in range(3):
+        for a in range(2):
+            for q in range(3):
+                held = [0]
+                for axis in ORDERS[q][:phase]:
+                    held += [b | 1 << axis for b in held]
+                for b in held:
+                    inbound[(a, q, phase, b)].wait_recv()
+                    got = b | 1 << ORDERS[q][phase]
+                    for later in range(phase + 1, 3):
+                        send_on(a, q, later, got)
+                    share(a, q, got)
+    for copy in inbound.values():
+        copy.wait_send()
+    for copy in shared:
+        copy.wait()
+    for copy in pending:
+        copy.wait()
+    for copy in local:
+        copy.wait()
+
+
+def spread(x_tok, dy_tok, table, n_fs, n_ep):
+    n_dev = n_fs * n_ep
+    tok, d = x_tok.shape
+    third = tok // 3 // 16 * 16
+    parts = (tok - 2 * third, third, third)
+    vmem, hbm = pl.BlockSpec(memory_space=pltpu.VMEM), pl.BlockSpec(memory_space=pl.ANY)
+    full = jax.ShapeDtypeStruct((n_dev * tok, d), x_tok.dtype)
+    dma = pltpu.SemaphoreType.DMA
+    return pl.pallas_call(
+        functools.partial(spread_kernel, n_fs, n_ep, parts),
+        out_shape=[full, full, jax.ShapeDtypeStruct(table.shape, table.dtype)],
+        in_specs=[vmem] * 3, out_specs=[hbm] * 3,
+        scratch_shapes=[dma((42,)), dma((42,)), dma((48,)), dma((48,)), dma((n_dev,)), dma((n_dev,)), dma((3,))],
+        compiler_params=pltpu.CompilerParams(collective_id=0, has_side_effects=True, vmem_limit_bytes=VMEM_LIMIT),
+        cost_estimate=pl.CostEstimate(flops=0, bytes_accessed=8 * n_dev * tok * d, transcendentals=0),
+        name="spread",
+    )(x_tok, dy_tok, table)
+
+
+def collect_kernel(n_fs, n_ep, parts, part_ref, dr_ref, gx_ref, dr_home, acc, sib, got,
+                   c_send, c_recv, send, recv, t_send, t_recv, own_sem):
+    tok = gx_ref.shape[0]
+    mine = block_of(0)
+    enter(n_fs, n_ep)
+    drs = exchange(n_fs, n_ep, dr_ref, dr_home, t_send, t_recv)
+    local_dr = pltpu.make_async_copy(dr_ref.at[mine], dr_home.at[mine], own_sem.at[8])
+    local_dr.start()
+    order = (7, 3, 5, 6, 1, 2, 4, 0)
+    loads, shares = {}, {}
+    for bits in order:
+        theirs = pl.ds(aligned(block_of(bits, 1) * tok, tok), tok)
+        shares[bits] = pltpu.make_async_remote_copy(
+            src_ref=part_ref.at[theirs], dst_ref=sib.at[bits], send_sem=c_send.at[bits], recv_sem=c_recv.at[bits],
+            device_id=peer_of(SIBLING), device_id_type=MESH)
+        shares[bits].start()
+        ours = pl.ds(aligned(block_of(bits) * tok, tok), tok)
+        loads[bits] = pltpu.make_async_copy(part_ref.at[ours], acc.at[bits], own_sem.at[bits])
+        loads[bits].start()
+    starts = [sum(parts[:q]) for q in range(3)]
+    slots = [(q, bits) for q in range(3) for bits in range(1, 8)]
+    hops = {}
+
+    def phase_of(q, bits):
+        return next(n for n in range(3) if bits >> ORDERS[q][n] & 1)
+
+    def send_off(q, bits):
+        n = slots.index((q, bits))
+        rows = pl.ds(starts[q], parts[q])
+        hops[(q, bits)] = pltpu.make_async_remote_copy(
+            src_ref=acc.at[bits, rows], dst_ref=got.at[bits - 1, rows], send_sem=send.at[n], recv_sem=recv.at[n],
+            device_id=peer_of(HOPS[ORDERS[q][phase_of(q, bits)]]), device_id_type=MESH)
+        hops[(q, bits)].start()
+
+    def add_arrival(q, bits, phase):
+        frm = bits | 1 << ORDERS[q][phase]
+        hops[(q, frm)].wait_recv()
+        rows = slice(starts[q], starts[q] + parts[q])
+        acc[bits, rows, :] = acc[bits, rows, :] + got[frm - 1, rows, :]
+
+    for bits in order:
+        loads[bits].wait()
+        shares[bits].wait_recv()
+        acc[bits] = acc[bits] + sib[bits]
+        for q in range(3):
+            if bits and phase_of(q, bits) == 0:
+                send_off(q, bits)
+    for phase in (1, 2):
+        for q in range(3):
+            for bits in range(1, 8):
+                if phase_of(q, bits) == phase:
+                    for earlier in range(phase):
+                        add_arrival(q, bits, earlier)
+                    send_off(q, bits)
+    for q in range(3):
+        for phase in range(3):
+            add_arrival(q, 0, phase)
+        rows = slice(starts[q], starts[q] + parts[q])
+        gx_ref[rows, :] = acc[0, rows, :].astype(gx_ref.dtype)
+    for bits in order:
+        shares[bits].wait_send()
+    for copy in hops.values():
+        copy.wait_send()
+    for copy in drs:
+        copy.wait()
+    local_dr.wait()
+
+
+def collect(dx_part, dr_part, n_fs, n_ep):
+    n_dev = n_fs * n_ep
+    tok, d = dx_part.shape[0] // n_dev, dx_part.shape[1]
+    quarter = tok // 4 // 8 * 8
+    parts = (tok - 2 * quarter, quarter, quarter)
+    vmem, hbm = pl.BlockSpec(memory_space=pltpu.VMEM), pl.BlockSpec(memory_space=pl.ANY)
+    dma = pltpu.SemaphoreType.DMA
+    return pl.pallas_call(
+        functools.partial(collect_kernel, n_fs, n_ep, parts),
+        out_shape=[jax.ShapeDtypeStruct((tok, d), BF16), jax.ShapeDtypeStruct(dr_part.shape, F32)],
+        in_specs=[hbm, vmem], out_specs=[vmem, vmem],
+        scratch_shapes=[pltpu.VMEM((8, tok, d), F32), pltpu.VMEM((8, tok, d), F32), pltpu.VMEM((7, tok, d), F32),
+                        dma((8,)), dma((8,)), dma((21,)), dma((21,)), dma((n_dev,)), dma((n_dev,)), dma((9,))],
+        compiler_params=pltpu.CompilerParams(collective_id=1, has_side_effects=True, vmem_limit_bytes=VMEM_LIMIT),
+        cost_estimate=pl.CostEstimate(flops=0, bytes_accessed=8 * n_dev * tok * d, transcendentals=0),
+        name="collect",
+    )(dx_part, dr_part)
+
+
 def solution(mesh):
     n_ep, n_fs = mesh.shape["ep"], mesh.shape["fsdp"]
     n_dev = n_ep * n_fs
@@ -390,8 +616,7 @@
 
     def body(x_tok, dy_tok, expert_ids, route_w, w_gate, w_up, w_down):
         tok, top_k = expert_ids.shape
-        d = x_tok.shape[1]
-        exp_local, _, f = w_gate.shape
+        exp_local, _, _ = w_gate.shape
         n_loc = exp_local // n_fs
         experts = exp_local * n_ep
         capacity = capacity_of(tok, top_k, experts)
@@ -400,14 +625,23 @@
         position, weight = route_tables(expert_ids, route_w, experts, capacity)
         table = jnp.stack([position, weight], axis=1).reshape(n_ep, n_fs, n_loc, 2, tok)
         table = table.transpose(1, 0, 2, 3, 4).reshape(n_dev, n_loc * 2, tok)
-        table = lax.all_to_all(table, both, 0, 0, tiled=True).reshape(n_dev, n_loc, 2, tok)
-        x_all = lax.all_gather(x_tok, both, axis=0, tiled=True)
-        dy_all = lax.all_gather(dy_tok, both, axis=0, tiled=True)
-
-        def to_owner(w):
-            return lax.all_to_all(w.reshape(n_fs, n_loc, *w.shape[1:]), "fsdp", 0, 0, tiled=True)
-
-        wg, wu, wd = to_owner(w_gate), to_owner(w_up), to_owner(w_down)
+        x_all, dy_all, table = spread(x_tok, dy_tok, table, n_fs, n_ep)
+        table = table.reshape(n_dev, n_loc, 2, tok)
+        me = lax.axis_index("fsdp").astype(jnp.int32)
+
+        def to_owners(k):
+            gate_up, down = [], []
+            for m in range(n_fs):
+                at = (me ^ m) * n_loc + k
+                gu = jnp.stack([lax.dynamic_index_in_dim(w, at, 0, keepdims=False) for w in (w_gate, w_up)])
+                dn = lax.dynamic_index_in_dim(w_down, at, 0, keepdims=False)
+                if m:
+                    gu, dn = [lax.ppermute(v, "fsdp", [(i, i ^ m) for i in range(n_fs)]) for v in (gu, dn)]
+                gate_up.append(gu)
+                down.append(dn)
+            return gate_up, down
+
+        weights = [to_owners(k) for k in range(n_loc)]
 
         pos = table[:, :, 0, :].astype(jnp.int32)
         r = table[:, :, 1, :]
@@ -419,19 +653,16 @@
         x_pool = gather_rows(x_all, cnt_flat, off_flat, pos, None, region)
         dy_pool, r_pool = gather_rows(dy_all, cnt_flat, off_flat, pos, r, region)
 
-        me = lax.axis_index("fsdp").astype(jnp.int32)
         dx_pools, dr_pools, pieces = [], [], []
         for k in range(n_loc):
             info = jnp.stack([rows[k], jnp.maximum(1, blocks(rows[k], TILE)), me])
-            w1, w3, w2s = wg[:, k].reshape(d, f), wu[:, k].reshape(d, f), wd[:, k]
-            dxk, drk, *slices = expert_call(k, info, x_pool, dy_pool, r_pool, w1, w3, w2s, region)
+            dxk, drk, *slices = expert_call(k, info, x_pool, dy_pool, r_pool, *weights[k], region)
             dx_pools.append(dxk)
             dr_pools.append(drk)
             pieces.append([slices[0]] + [lax.ppermute(slices[m], "fsdp", [(i, i ^ m) for i in range(n_fs)])
                                          for m in range(1, n_fs)])
         dx_part, dr_part = combine_rows(cnt_flat, off_flat, pos, dx_pools, dr_pools, region)
-        grad_x = lax.psum_scatter(dx_part, both, scatter_dimension=0, tiled=True).astype(BF16)
-        dr_home = lax.all_to_all(dr_part, both, 0, 0, tiled=True)
+        grad_x, dr_home = collect(dx_part, dr_part, n_fs, n_ep)
         dr_home = dr_home.reshape(n_fs, n_ep, n_loc, tok).transpose(1, 0, 2, 3).reshape(experts, tok)
         hit = expert_ids.T[:, None, :] == jnp.arange(experts, dtype=jnp.int32)[None, :, None]
         route_grad = jnp.sum(jnp.where(hit, dr_home[None], 0.0), axis=1).T

time: 1090 us -> 898 us (0.82)
  the two profiles are of different devices: /device:TPU:15 before, /device:TPU:0 now
where the time goes in v2:
time: 898 us; the launch traced here: 890 us
  Pallas kernels  691 us (77%)
  waiting for transfers between devices  106 us (12%)
  starting transfers between devices  49.8 us (6%)
  other arithmetic  21.2 us (2%)
  local copies, waits for them, and re-layouts  17.1 us (2%)
    pallas_call x1, Pallas kernels, collect(): pl.pallas_call(functools.partial(collect_kernel, n_fs, n_ep, parts), out_...  322 us
    pallas_call x1, Pallas kernels, spread(): pl.pallas_call(functools.partial(spread_kernel, n_fs, n_ep, parts), out_s...  137 us
    pallas_call x4, Pallas kernels, expert_call(): pl.pallas_call(functools.partial(expert_kernel, n_fs), out_shape=[jax.Sha...  118 us
    ppermute x12, waiting for transfers between devices, body(): lax.ppermute(slices[m], 'fsdp', [(i, i ^ m) for i in range(n_fs)])  88.8 us
    pallas_call x2, Pallas kernels, gather_rows(): pl.pallas_call(functools.partial(gather_kernel, n_src, n_loc, region, wit...  56.8 us
    ppermute x24, starting transfers between devices, to_owners(): lax.ppermute(v, 'fsdp', [(i, i ^ m) for i in range(n_fs)])  33.1 us
    pallas_call x1, Pallas kernels, combine_rows(): pl.pallas_call(functools.partial(combine_kernel, n_src, n_loc), out_shape...  31.9 us
    pallas_call x4, Pallas kernels, place(): pl.pallas_call(functools.partial(place_kernel, n_fs, n_loc, k, first), ou...  25.9 us
  transfers between devices with their start and end apart: 36, of which 8 were waited for; matrix products, arithmetic and copies ran while one was open for 4% of the time, Pallas kernels for 77%

profile of v2, /device:TPU:0, one launch (start us, length us, event | category | flops | bytes accessed | tf_op | source)
XLA Modules:
  0.0 890.3 jit_solution(15809875134110198691)
XLA Ops:
  0.7 4.7 dynamic-slice_bitcast_fusion
  5.5 4.3 collective-permute-start.23
  10.2 1.4 collective-permute-start.17
  11.6 1.6 collective-permute-start.16
  16.6 136.5 %spread.1 = (bf16[16384,512]{1,0:T(8,128)(2,1)}, bf16[16384,512]{1,0:T(8,128)(2,1)}, f32[16,8,1024]{2,1,0:T(8,128)}) custom-call(bf16[1024,512]{1,0:T(8,128)(2,1)} %x_ref.1, bf16[1024,512]{1,0:T(8,128)(2,1)} %dy_ref.1, f32[16,8,1024]{2,1,0:T(8,128)} %reshape.49.table_ref), custom_call_target="tpu_custom_call" | custom-call | bytes 67108864 | tf_op jit(solution)/shard_map/spread/pallas_call | solution.py:511
  153.1 1.4 copy.28
  160.1 4.9 constant_dynamic-slice_fusion
  175.1 1.2 add_add_fusion.3.info
  176.8 24.5 %gather_x.1.x_ref = bf16[26624,512]{1,0:T(8,128)(2,1)} custom-call(s32[64]{0:T(128)} %add.196.refs_0_.cnt, s32[64]{0:T(128)} %fusion.8.refs_1_.off, s32[16,4,1024]{2,1,0:T(4,128)} %fusion.2.refs_2_.pos_ref, bf16[16384,512]{1,0:T(8,128)(2,1)} %get-tuple-element.51.refs_3_), custom_call_target="tpu_custom_call" | custom-call | flops 12582912000 | bytes 33554432 | tf_op jit(solution)/shard_map/gather_x/pallas_call | solution.py:159
  201.3 32.3 %gather_r.1 = (bf16[26624,512]{1,0:T(8,128)(2,1)}, f32[26624,128]{1,0:T(8,128)}) custom-call(s32[64]{0:T(128)} %add.196.refs_0_.cnt, s32[64]{0:T(128)} %fusion.8.refs_1_.off, s32[16,4,1024]{2,1,0:T(4,128)} %fusion.2.refs_2_.pos_ref, f32[16,4,1024]{2,1,0:T(4,128)} %bitcast.62, bf16[16384,512]{1,0:T(8,128)(2,1)} %get-tuple-element.52.refs_4_), custom_call_target="tpu_custom_call" | custom-call | flops 12582912000 | bytes 33554432 | tf_op jit(solution)/shard_map/gather_r/pallas_call | solution.py:159
  235.7 1.2 collective-permute-start.11
  237.9 1.3 collective-permute-start.13
  239.2 1.2 collective-permute-start.14
  240.5 1.4 add_add_fusion.1.info
  243.3 1.6 collective-permute-start.10
  244.9 3.3 collective-permute-start.9
  248.3 1.2 add_add_fusion.info
  250.4 12.3 %collective-permute-done.10.refs_6_ = bf16[1280,128]{1,0:T(8,128)(2,1)S(1)} collective-permute-done((bf16[1280,128]{1,0:T(8,128)(2,1)}, bf16[1280,128]{1,0:T(8,128)(2,1)S(1)}, u32[]{:S(2)}, u32[]{:S(2)}) %collective-permute-start.10) | collective-permute-done | bytes 327712 | tf_op jit(solution)/shard_map/ppermute | solution.py:639
  262.7 2.1 collective-permute-start.5
  264.8 2.4 collective-permute-start.4
  267.2 1.4 collective-permute-start.7
  268.6 2.1 collective-permute-start.8
  270.8 29.6 %shard_map.112 = (bf16[6656,512]{1,0:T(8,128)(2,1)}, f32[6656,128]{1,0:T(8,128)}, f32[3,128,1280]{2,1,0:T(8,128)}, f32[3,128,1280]{2,1,0:T(8,128)}, f32[3,128,1280]{2,1,0:T(8,128)}, /*index=5*/f32[3,128,1280]{2,1,0:T(8,128)}) custom-call(s32[3]{0:T(128)} %add_add_fusion.2.info, bf16[26624,512]{1,0:T(8,128)(2,1)} %gather_x.1.x_ref, ...), custom_call_target="tpu_custom_call" | custom-call | flops 35389440000 | bytes 15728640 | tf_op jit(solution)/shard_map/pallas_call | solution.py:242
  300.4 1.3 collective-permute-start.22
  302.5 4.9 collective-permute-done.7.refs_2_
  307.4 1.2 collective-permute-start.2
  308.6 29.6 %shard_map.111 = (bf16[6656,512]{1,0:T(8,128)(2,1)}, f32[6656,128]{1,0:T(8,128)}, f32[3,128,1280]{2,1,0:T(8,128)}, f32[3,128,1280]{2,1,0:T(8,128)}, f32[3,128,1280]{2,1,0:T(8,128)}, /*index=5*/f32[3,128,1280]{2,1,0:T(8,128)}) custom-call(s32[3]{0:T(128)} %add_add_fusion.1.info, bf16[26624,512]{1,0:T(8,128)(2,1)} %gather_x.1.x_ref, ...), custom_call_target="tpu_custom_call" | custom-call | flops 35389440000 | bytes 15728640 | tf_op jit(solution)/shard_map/pallas_call | solution.py:242
  338.2 2.0 collective-permute-start.19
  340.6 1.4 collective-permute-start.20
  342.5 1.6 collective-permute-start.27
  344.5 29.4 %shard_map.110 = (bf16[6656,512]{1,0:T(8,128)(2,1)}, f32[6656,128]{1,0:T(8,128)}, f32[3,128,1280]{2,1,0:T(8,128)}, f32[3,128,1280]{2,1,0:T(8,128)}, f32[3,128,1280]{2,1,0:T(8,128)}, /*index=5*/f32[3,128,1280]{2,1,0:T(8,128)}) custom-call(s32[3]{0:T(128)} %add_add_fusion.info, bf16[26624,512]{1,0:T(8,128)(2,1)} %gather_x.1.x_ref, ...), custom_call_target="tpu_custom_call" | custom-call | flops 35389440000 | bytes 15728640 | tf_op jit(solution)/shard_map/pallas_call | solution.py:242
  373.9 1.3 collective-permute-start.31
  375.2 1.7 collective-permute-start.32
  377.4 1.6 collective-permute-done.27.refs_1_
  379.1 3.7 collective-permute-start.34
  382.8 17.3 %collective-permute-done.30.refs_1_ = f32[3,128,1280]{2,1,0:T(8,128)} collective-permute-done((f32[3,128,1280]{2,1,0:T(8,128)}, f32[3,128,1280]{2,1,0:T(8,128)}, u32[]{:S(2)}, u32[]{:S(2)}) %collective-permute-start.30) | collective-permute-done | bytes 1966112 | tf_op jit(solution)/shard_map/ppermute | solution.py:662
  400.1 4.9 collective-permute-start.35
  405.0 29.5 %shard_map.113 = (bf16[6656,512]{1,0:T(8,128)(2,1)}, f32[6656,128]{1,0:T(8,128)}, f32[3,128,1280]{2,1,0:T(8,128)}, f32[3,128,1280]{2,1,0:T(8,128)}, f32[3,128,1280]{2,1,0:T(8,128)}, /*index=5*/f32[3,128,1280]{2,1,0:T(8,128)}) custom-call(s32[3]{0:T(128)} %add_add_fusion.3.info, bf16[26624,512]{1,0:T(8,128)(2,1)} %gather_x.1.x_ref, ...), custom_call_target="tpu_custom_call" | custom-call | flops 35389440000 | bytes 15728640 | tf_op jit(solution)/shard_map/pallas_call | solution.py:242
  434.6 3.8 collective-permute-done.32.refs_3_
  438.4 1.6 collective-permute-start.29
  440.0 19.7 %collective-permute-done.33.refs_1_ = f32[3,128,1280]{2,1,0:T(8,128)S(1)} collective-permute-done((f32[3,128,1280]{2,1,0:T(8,128)}, f32[3,128,1280]{2,1,0:T(8,128)S(1)}, u32[]{:S(2)}, u32[]{:S(2)}) %collective-permute-start.33) | collective-permute-done | bytes 1966112 | tf_op jit(solution)/shard_map/ppermute | solution.py:662
  460.1 46.2 %collective-permute-done.34.refs_2_ = f32[3,128,1280]{2,1,0:T(8,128)} collective-permute-done((f32[3,128,1280]{2,1,0:T(8,128)}, f32[3,128,1280]{2,1,0:T(8,128)}, u32[]{:S(2)}, u32[]{:S(2)}) %collective-permute-start.34) | collective-permute-done | bytes 1966112 | tf_op jit(solution)/shard_map/ppermute | solution.py:662
  506.9 31.9 %combine.1 = (f32[16384,512]{1,0:T(8,128)}, f32[16,4,1024]{2,1,0:T(4,128)}) custom-call(s32[64]{0:T(128)} %add.196.refs_0_.cnt, s32[64]{0:T(128)} %fusion.8.refs_1_.off, s32[16,4,1024]{2,1,0:T(4,128)} %fusion.2.refs_2_.pos_ref, bf16[6656,512]{1,0:T(8,128)(2,1)} %get-tuple-element.55.refs_0_, bf16[6656,512]{1,0:T(8,128)(2,1)} %get-tuple-element.56.refs_1_, ...), custom_call_target="tpu_custom_call" | custom-call | flops 12582912000 | bytes 33554432 | tf_op jit(solution)/shard_map/combine/pallas_call | solution.py:369
  538.8 322.1 %collect.1 = (bf16[1024,512]{1,0:T(8,128)(2,1)}, f32[16,4,1024]{2,1,0:T(4,128)}) custom-call(f32[16384,512]{1,0:T(8,128)} %get-tuple-element.63.part_ref, f32[16,4,1024]{2,1,0:T(4,128)} %get-tuple-element.64.dr_ref), custom_call_target="tpu_custom_call" | custom-call | bytes 67108864 | tf_op jit(solution)/shard_map/collect/pallas_call | solution.py:597
  862.9 6.4 shard_map.114
  869.4 6.5 shard_map.115
  875.9 6.5 shard_map.116
  882.4 6.5 shard_map.117
  (111 shorter events, 29.4 us)
Async XLA Ops:
  0.7 13.0 %copy-start.6 = (s32[1024,8]{0,1:T(8,128)S(1)}, s32[1024,8]{0,1:T(8,128)}, u32[]{:S(2)}) copy-start(s32[1024,8]{0,1:T(8,128)} %param.9) | copy-start | bytes 98308
  5.4 9.1 %copy-start.8 = (f32[1024,8]{0,1:T(8,128)S(1)}, f32[1024,8]{0,1:T(8,128)}, u32[]{:S(2)}) copy-start(f32[1024,8]{0,1:T(8,128)} %param.10) | copy-start | bytes 98308
  5.5 230.3 %collective-permute-start.23 = (bf16[1280,128]{1,0:T(8,128)(2,1)}, bf16[1280,128]{1,0:T(8,128)(2,1)}, u32[]{:S(2)}, u32[]{:S(2)}) collective-permute-start(bf16[1280,128]{1,0:T(8,128)(2,1)} %get-tuple-element.95), channel_id=1, source_target_pairs={{0,12},{4,8},{8,4},{12,0},{1,13},{5,9},{9,5},{13,1},{2,14},{6,10},... | collective-permute-start | bytes 983048 | tf_op jit(solution)/shard_map/ppermute | solution.py:639
  9.7 227.2 %collective-permute-start.21 = (bf16[1280,128]{1,0:T(8,128)(2,1)}, bf16[1280,128]{1,0:T(8,128)(2,1)}, u32[]{:S(2)}, u32[]{:S(2)}) collective-permute-start(bf16[1280,128]{1,0:T(8,128)(2,1)} %get-tuple-element.96), channel_id=1, source_target_pairs={{0,4},{4,0},{8,12},{12,8},{1,5},{5,1},{9,13},{13,9},{2,6},{6,2},{1... | collective-permute-start | bytes 983048 | tf_op jit(solution)/shard_map/ppermute | solution.py:639
  10.2 227.7 %collective-permute-start.17 = (bf16[1280,128]{1,0:T(8,128)(2,1)}, bf16[1280,128]{1,0:T(8,128)(2,1)}, u32[]{:S(2)}, u32[]{:S(2)}) collective-permute-start(bf16[1280,128]{1,0:T(8,128)(2,1)} %get-tuple-element.98), channel_id=1, source_target_pairs={{0,12},{4,8},{8,4},{12,0},{1,13},{5,9},{9,5},{13,1},{2,14},{6,10},... | collective-permute-start | bytes 983048 | tf_op jit(solution)/shard_map/ppermute | solution.py:639
  11.6 227.6 %collective-permute-start.16 = (bf16[1280,128]{1,0:T(8,128)(2,1)}, bf16[1280,128]{1,0:T(8,128)(2,1)}, u32[]{:S(2)}, u32[]{:S(2)}) collective-permute-start(bf16[1280,128]{1,0:T(8,128)(2,1)} %get-tuple-element.99), channel_id=1, source_target_pairs={{0,8},{4,12},{8,0},{12,4},{1,9},{5,13},{9,1},{13,5},{2,10},{6,14},... | collective-permute-start | bytes 983048 | tf_op jit(solution)/shard_map/ppermute | solution.py:639
  13.2 230.1 %collective-permute-start.15 = (bf16[1280,128]{1,0:T(8,128)(2,1)}, bf16[1280,128]{1,0:T(8,128)(2,1)}, u32[]{:S(2)}, u32[]{:S(2)}) collective-permute-start(bf16[1280,128]{1,0:T(8,128)(2,1)} %get-tuple-element.100), channel_id=1, source_target_pairs={{0,4},{4,0},{8,12},{12,8},{1,5},{5,1},{9,13},{13,9},{2,6},{6,2},{1... | collective-permute-start | bytes 983048 | tf_op jit(solution)/shard_map/ppermute | solution.py:639
  235.7 9.2 %collective-permute-start.11 = (bf16[1280,128]{1,0:T(8,128)(2,1)}, bf16[1280,128]{1,0:T(8,128)(2,1)S(1)}, u32[]{:S(2)}, u32[]{:S(2)}) collective-permute-start(bf16[1280,128]{1,0:T(8,128)(2,1)} %get-tuple-element.102), channel_id=1, source_target_pairs={{0,12},{4,8},{8,4},{12,0},{1,13},{5,9},{9,5},{13,1},{2,14},{6,10},... | collective-permute-start | bytes 983048 | tf_op jit(solution)/shard_map/ppermute | solution.py:639
  237.0 30.3 %collective-permute-start.12 = (bf16[2,128,1280]{2,1,0:T(8,128)(2,1)}, bf16[2,128,1280]{2,1,0:T(8,128)(2,1)}, u32[]{:S(2)}, u32[]{:S(2)}) collective-permute-start(bf16[2,128,1280]{2,1,0:T(8,128)(2,1)} %pad_maximum_fusion.9), channel_id=1, source_target_pairs={{0,4},{4,0},{8,12},{12,8},{1,5},{5,1},{9,13},{13,9},{2,6},{6,2},{1... | collective-permute-start | bytes 1966088 | tf_op jit(solution)/shard_map/ppermute | solution.py:639
  237.9 29.3 %collective-permute-start.13 = (bf16[2,128,1280]{2,1,0:T(8,128)(2,1)}, bf16[2,128,1280]{2,1,0:T(8,128)(2,1)}, u32[]{:S(2)}, u32[]{:S(2)}) collective-permute-start(bf16[2,128,1280]{2,1,0:T(8,128)(2,1)} %pad_maximum_fusion.10), channel_id=1, source_target_pairs={{0,8},{4,12},{8,0},{12,4},{1,9},{5,13},{9,1},{13,5},{2,10},{6,14},... | collective-permute-start | bytes 1966088 | tf_op jit(solution)/shard_map/ppermute | solution.py:639
  239.2 29.4 %collective-permute-start.14 = (bf16[2,128,1280]{2,1,0:T(8,128)(2,1)}, bf16[2,128,1280]{2,1,0:T(8,128)(2,1)}, u32[]{:S(2)}, u32[]{:S(2)}) collective-permute-start(bf16[2,128,1280]{2,1,0:T(8,128)(2,1)} %pad_maximum_fusion.11), channel_id=1, source_target_pairs={{0,12},{4,8},{8,4},{12,0},{1,13},{5,9},{9,5},{13,1},{2,14},{6,10},... | collective-permute-start | bytes 1966088 | tf_op jit(solution)/shard_map/ppermute | solution.py:639
  243.3 19.4 %collective-permute-start.10 = (bf16[1280,128]{1,0:T(8,128)(2,1)}, bf16[1280,128]{1,0:T(8,128)(2,1)S(1)}, u32[]{:S(2)}, u32[]{:S(2)}) collective-permute-start(bf16[1280,128]{1,0:T(8,128)(2,1)} %get-tuple-element.103), channel_id=1, source_target_pairs={{0,8},{4,12},{8,0},{12,4},{1,9},{5,13},{9,1},{13,5},{2,10},{6,14},... | collective-permute-start | bytes 983048 | tf_op jit(solution)/shard_map/ppermute | solution.py:639
  244.9 25.8 %copy-start.11 = (bf16[1280,128]{1,0:T(8,128)(2,1)}, bf16[1280,128]{1,0:T(8,128)(2,1)S(1)}, u32[]{:S(2)}) copy-start(bf16[1280,128]{1,0:T(8,128)(2,1)S(1)} %collective-permute-done.11.refs_7_) | copy-start | bytes 983044
  244.9 19.9 %collective-permute-start.9 = (bf16[1280,128]{1,0:T(8,128)(2,1)S(1)}, bf16[1280,128]{1,0:T(8,128)(2,1)S(1)}, u32[]{:S(2)}, u32[]{:S(2)}) collective-permute-start(bf16[1280,128]{1,0:T(8,128)(2,1)S(1)} %get-tuple-element.104), channel_id=1, source_target_pairs={{0,4},{4,0},{8,12},{12,8},{1,5},{5,1},{9,13},{13,9},{2,6},{6,2},{1... | collective-permute-start | bytes 983048 | tf_op jit(solution)/shard_map/ppermute | solution.py:639
  262.7 8.0 copy-start.12
  262.7 37.6 %collective-permute-start.5 = (bf16[1280,128]{1,0:T(8,128)(2,1)}, bf16[1280,128]{1,0:T(8,128)(2,1)}, u32[]{:S(2)}, u32[]{:S(2)}) collective-permute-start(bf16[1280,128]{1,0:T(8,128)(2,1)} %get-tuple-element.106), channel_id=1, source_target_pairs={{0,12},{4,8},{8,4},{12,0},{1,13},{5,9},{9,5},{13,1},{2,14},{6,10},... | collective-permute-start | bytes 983048 | tf_op jit(solution)/shard_map/ppermute | solution.py:639
  264.8 35.6 %collective-permute-start.4 = (bf16[1280,128]{1,0:T(8,128)(2,1)}, bf16[1280,128]{1,0:T(8,128)(2,1)}, u32[]{:S(2)}, u32[]{:S(2)}) collective-permute-start(bf16[1280,128]{1,0:T(8,128)(2,1)} %get-tuple-element.107), channel_id=1, source_target_pairs={{0,8},{4,12},{8,0},{12,4},{1,9},{5,13},{9,1},{13,5},{2,10},{6,14},... | collective-permute-start | bytes 983048 | tf_op jit(solution)/shard_map/ppermute | solution.py:639
  267.2 34.6 %collective-permute-start.6 = (bf16[2,128,1280]{2,1,0:T(8,128)(2,1)}, bf16[2,128,1280]{2,1,0:T(8,128)(2,1)}, u32[]{:S(2)}, u32[]{:S(2)}) collective-permute-start(bf16[2,128,1280]{2,1,0:T(8,128)(2,1)} %pad_maximum_fusion.5), channel_id=1, source_target_pairs={{0,4},{4,0},{8,12},{12,8},{1,5},{5,1},{9,13},{13,9},{2,6},{6,2},{1... | collective-permute-start | bytes 1966088 | tf_op jit(solution)/shard_map/ppermute | solution.py:639
  267.2 40.1 %collective-permute-start.7 = (bf16[2,128,1280]{2,1,0:T(8,128)(2,1)}, bf16[2,128,1280]{2,1,0:T(8,128)(2,1)}, u32[]{:S(2)}, u32[]{:S(2)}) collective-permute-start(bf16[2,128,1280]{2,1,0:T(8,128)(2,1)} %pad_maximum_fusion.6), channel_id=1, source_target_pairs={{0,8},{4,12},{8,0},{12,4},{1,9},{5,13},{9,1},{13,5},{2,10},{6,14},... | collective-permute-start | bytes 1966088 | tf_op jit(solution)/shard_map/ppermute | solution.py:639
  268.6 38.8 %collective-permute-start.8 = (bf16[2,128,1280]{2,1,0:T(8,128)(2,1)}, bf16[2,128,1280]{2,1,0:T(8,128)(2,1)}, u32[]{:S(2)}, u32[]{:S(2)}) collective-permute-start(bf16[2,128,1280]{2,1,0:T(8,128)(2,1)} %pad_maximum_fusion.7), channel_id=1, source_target_pairs={{0,12},{4,8},{8,4},{12,0},{1,13},{5,9},{9,5},{13,1},{2,14},{6,10},... | collective-permute-start | bytes 1966088 | tf_op jit(solution)/shard_map/ppermute | solution.py:639
  270.7 29.7 %copy-start.5 = (bf16[1280,128]{1,0:T(8,128)(2,1)S(1)}, bf16[1280,128]{1,0:T(8,128)(2,1)}, u32[]{:S(2)}) copy-start(bf16[1280,128]{1,0:T(8,128)(2,1)} %get-tuple-element.110) | copy-start | bytes 983044
  270.7 31.1 %copy-start.4 = (bf16[2,128,1280]{2,1,0:T(8,128)(2,1)S(1)}, bf16[2,128,1280]{2,1,0:T(8,128)(2,1)}, u32[]{:S(2)}) copy-start(bf16[2,128,1280]{2,1,0:T(8,128)(2,1)} %pad_maximum_fusion.1) | copy-start | bytes 1966084
  270.7 36.6 %copy-start.3 = (bf16[2,128,1280]{2,1,0:T(8,128)(2,1)S(1)}, bf16[2,128,1280]{2,1,0:T(8,128)(2,1)}, u32[]{:S(2)}) copy-start(bf16[2,128,1280]{2,1,0:T(8,128)(2,1)} %pad_maximum_fusion.2) | copy-start | bytes 1966084
  270.7 36.6 %copy-start.2 = (bf16[2,128,1280]{2,1,0:T(8,128)(2,1)S(1)}, bf16[2,128,1280]{2,1,0:T(8,128)(2,1)}, u32[]{:S(2)}) copy-start(bf16[2,128,1280]{2,1,0:T(8,128)(2,1)} %pad_maximum_fusion.3) | copy-start | bytes 1966084
  300.4 37.8 %collective-permute-start.3 = (bf16[1280,128]{1,0:T(8,128)(2,1)}, bf16[1280,128]{1,0:T(8,128)(2,1)}, u32[]{:S(2)}, u32[]{:S(2)}) collective-permute-start(bf16[1280,128]{1,0:T(8,128)(2,1)} %get-tuple-element.108), channel_id=1, source_target_pairs={{0,4},{4,0},{8,12},{12,8},{1,5},{5,1},{9,13},{13,9},{2,6},{6,2},{1... | collective-permute-start | bytes 983048 | tf_op jit(solution)/shard_map/ppermute | solution.py:639
  300.4 39.8 %collective-permute-start.22 = (bf16[1280,128]{1,0:T(8,128)(2,1)S(1)}, bf16[1280,128]{1,0:T(8,128)(2,1)}, u32[]{:S(2)}, u32[]{:S(2)}) collective-permute-start(bf16[1280,128]{1,0:T(8,128)(2,1)S(1)} %copy-done.5), channel_id=1, source_target_pairs={{0,8},{4,12},{8,0},{12,4},{1,9},{5,13},{9,1},{13,5},{2,10},{6,14},... | collective-permute-start | bytes 983048 | tf_op jit(solution)/shard_map/ppermute | solution.py:639
  301.8 38.8 %collective-permute-start = (bf16[2,128,1280]{2,1,0:T(8,128)(2,1)S(1)}, bf16[2,128,1280]{2,1,0:T(8,128)(2,1)}, u32[]{:S(2)}, u32[]{:S(2)}) collective-permute-start(bf16[2,128,1280]{2,1,0:T(8,128)(2,1)S(1)} %copy-done.4), channel_id=1, source_target_pairs={{0,4},{4,0},{8,12},{12,8},{1,5},{5,1},{9,13},{13,9},{2,6},{6,2},{1... | collective-permute-start | bytes 1966088 | tf_op jit(solution)/shard_map/ppermute | solution.py:639
  307.3 35.1 %collective-permute-start.1 = (bf16[2,128,1280]{2,1,0:T(8,128)(2,1)S(1)}, bf16[2,128,1280]{2,1,0:T(8,128)(2,1)}, u32[]{:S(2)}, u32[]{:S(2)}) collective-permute-start(bf16[2,128,1280]{2,1,0:T(8,128)(2,1)S(1)} %copy-done.3), channel_id=1, source_target_pairs={{0,8},{4,12},{8,0},{12,4},{1,9},{5,13},{9,1},{13,5},{2,10},{6,14},... | collective-permute-start | bytes 1966088 | tf_op jit(solution)/shard_map/ppermute | solution.py:639
  307.4 36.7 %collective-permute-start.2 = (bf16[2,128,1280]{2,1,0:T(8,128)(2,1)S(1)}, bf16[2,128,1280]{2,1,0:T(8,128)(2,1)}, u32[]{:S(2)}, u32[]{:S(2)}) collective-permute-start(bf16[2,128,1280]{2,1,0:T(8,128)(2,1)S(1)} %copy-done.2), channel_id=1, source_target_pairs={{0,12},{4,8},{8,4},{12,0},{1,13},{5,9},{9,5},{13,1},{2,14},{6,10},... | collective-permute-start | bytes 1966088 | tf_op jit(solution)/shard_map/ppermute | solution.py:639
  338.2 35.7 %collective-permute-start.19 = (bf16[2,128,1280]{2,1,0:T(8,128)(2,1)}, bf16[2,128,1280]{2,1,0:T(8,128)(2,1)}, u32[]{:S(2)}, u32[]{:S(2)}) collective-permute-start(bf16[2,128,1280]{2,1,0:T(8,128)(2,1)} %pad_maximum_fusion.14), channel_id=1, source_target_pairs={{0,8},{4,12},{8,0},{12,4},{1,9},{5,13},{9,1},{13,5},{2,10},{6,14},... | collective-permute-start | bytes 1966088 | tf_op jit(solution)/shard_map/ppermute | solution.py:639
  340.2 35.0 %collective-permute-start.18 = (bf16[2,128,1280]{2,1,0:T(8,128)(2,1)S(1)}, bf16[2,128,1280]{2,1,0:T(8,128)(2,1)}, u32[]{:S(2)}, u32[]{:S(2)}) collective-permute-start(bf16[2,128,1280]{2,1,0:T(8,128)(2,1)S(1)} %pad_maximum_fusion.13), channel_id=1, source_target_pairs={{0,4},{4,0},{8,12},{12,8},{1,5},{5,1},{9,13},{13,9},{2,6},{6,2},{1... | collective-permute-start | bytes 1966088 | tf_op jit(solution)/shard_map/ppermute | solution.py:639
  340.6 36.4 %collective-permute-start.20 = (bf16[2,128,1280]{2,1,0:T(8,128)(2,1)S(1)}, bf16[2,128,1280]{2,1,0:T(8,128)(2,1)S(1)}, u32[]{:S(2)}, u32[]{:S(2)}) collective-permute-start(bf16[2,128,1280]{2,1,0:T(8,128)(2,1)S(1)} %pad_maximum_fusion.15), channel_id=1, source_target_pairs={{0,12},{4,8},{8,4},{12,0},{1,13},{5,9},{9,5},{13,1},{2,14},{6,10},... | collective-permute-start | bytes 1966088 | tf_op jit(solution)/shard_map/ppermute | solution.py:639
  342.5 36.6 %collective-permute-start.27 = (f32[3,128,1280]{2,1,0:T(8,128)}, f32[3,128,1280]{2,1,0:T(8,128)}, u32[]{:S(2)}, u32[]{:S(2)}) collective-permute-start(f32[3,128,1280]{2,1,0:T(8,128)} %get-tuple-element.72), channel_id=1, source_target_pairs={{0,4},{4,0},{8,12},{12,8},{1,5},{5,1},{9,13},{13,9},{2,6},{6,2},{1... | collective-permute-start | bytes 5898248 | tf_op jit(solution)/shard_map/ppermute | solution.py:662
  344.0 56.1 %collective-permute-start.30 = (f32[3,128,1280]{2,1,0:T(8,128)}, f32[3,128,1280]{2,1,0:T(8,128)}, u32[]{:S(2)}, u32[]{:S(2)}) collective-permute-start(f32[3,128,1280]{2,1,0:T(8,128)} %get-tuple-element.76), channel_id=1, source_target_pairs={{0,4},{4,0},{8,12},{12,8},{1,5},{5,1},{9,13},{13,9},{2,6},{6,2},{1... | collective-permute-start | bytes 5898248 | tf_op jit(solution)/shard_map/ppermute | solution.py:662
  373.9 60.6 %collective-permute-start.31 = (f32[3,128,1280]{2,1,0:T(8,128)}, f32[3,128,1280]{2,1,0:T(8,128)}, u32[]{:S(2)}, u32[]{:S(2)}) collective-permute-start(f32[3,128,1280]{2,1,0:T(8,128)} %get-tuple-element.77), channel_id=1, source_target_pairs={{0,8},{4,12},{8,0},{12,4},{1,9},{5,13},{9,1},{13,5},{2,10},{6,14},... | collective-permute-start | bytes 5898248 | tf_op jit(solution)/shard_map/ppermute | solution.py:662
  375.2 63.2 %collective-permute-start.32 = (f32[3,128,1280]{2,1,0:T(8,128)}, f32[3,128,1280]{2,1,0:T(8,128)}, u32[]{:S(2)}, u32[]{:S(2)}) collective-permute-start(f32[3,128,1280]{2,1,0:T(8,128)} %get-tuple-element.78), channel_id=1, source_target_pairs={{0,12},{4,8},{8,4},{12,0},{1,13},{5,9},{9,5},{13,1},{2,14},{6,10},... | collective-permute-start | bytes 5898248 | tf_op jit(solution)/shard_map/ppermute | solution.py:662
  377.0 28.0 %copy-start.10 = (bf16[2,128,1280]{2,1,0:T(8,128)(2,1)}, bf16[2,128,1280]{2,1,0:T(8,128)(2,1)S(1)}, u32[]{:S(2)}) copy-start(bf16[2,128,1280]{2,1,0:T(8,128)(2,1)S(1)} %collective-permute-done.20.refs_3_) | copy-start | bytes 1966084
  377.0 82.8 %collective-permute-start.33 = (f32[3,128,1280]{2,1,0:T(8,128)}, f32[3,128,1280]{2,1,0:T(8,128)S(1)}, u32[]{:S(2)}, u32[]{:S(2)}) collective-permute-start(f32[3,128,1280]{2,1,0:T(8,128)} %get-tuple-element.80), channel_id=1, source_target_pairs={{0,4},{4,0},{8,12},{12,8},{1,5},{5,1},{9,13},{13,9},{2,6},{6,2},{1... | collective-permute-start | bytes 5898248 | tf_op jit(solution)/shard_map/ppermute | solution.py:662
  379.1 127.3 %collective-permute-start.34 = (f32[3,128,1280]{2,1,0:T(8,128)}, f32[3,128,1280]{2,1,0:T(8,128)}, u32[]{:S(2)}, u32[]{:S(2)}) collective-permute-start(f32[3,128,1280]{2,1,0:T(8,128)} %get-tuple-element.81), channel_id=1, source_target_pairs={{0,8},{4,12},{8,0},{12,4},{1,9},{5,13},{9,1},{13,5},{2,10},{6,14},... | collective-permute-start | bytes 5898248 | tf_op jit(solution)/shard_map/ppermute | solution.py:662
  400.1 106.8 %collective-permute-start.35 = (f32[3,128,1280]{2,1,0:T(8,128)}, f32[3,128,1280]{2,1,0:T(8,128)}, u32[]{:S(2)}, u32[]{:S(2)}) collective-permute-start(f32[3,128,1280]{2,1,0:T(8,128)} %get-tuple-element.82), channel_id=1, source_target_pairs={{0,12},{4,8},{8,4},{12,0},{1,13},{5,9},{9,5},{13,1},{2,14},{6,10},... | collective-permute-start | bytes 5898248 | tf_op jit(solution)/shard_map/ppermute | solution.py:662
  405.0 33.4 %copy-start.9 = (f32[3,128,1280]{2,1,0:T(8,128)S(1)}, f32[3,128,1280]{2,1,0:T(8,128)}, u32[]{:S(2)}) copy-start(f32[3,128,1280]{2,1,0:T(8,128)} %get-tuple-element.74) | copy-start | bytes 5898244
  434.5 441.3 %collective-permute-start.28 = (f32[3,128,1280]{2,1,0:T(8,128)}, f32[3,128,1280]{2,1,0:T(8,128)}, u32[]{:S(2)}, u32[]{:S(2)}) collective-permute-start(f32[3,128,1280]{2,1,0:T(8,128)} %get-tuple-element.73), channel_id=1, source_target_pairs={{0,8},{4,12},{8,0},{12,4},{1,9},{5,13},{9,1},{13,5},{2,10},{6,14},... | collective-permute-start | bytes 5898248 | tf_op jit(solution)/shard_map/ppermute | solution.py:662
  438.4 437.4 %collective-permute-start.29 = (f32[3,128,1280]{2,1,0:T(8,128)S(1)}, f32[3,128,1280]{2,1,0:T(8,128)}, u32[]{:S(2)}, u32[]{:S(2)}) collective-permute-start(f32[3,128,1280]{2,1,0:T(8,128)S(1)} %copy-done.9), channel_id=1, source_target_pairs={{0,12},{4,8},{8,4},{12,0},{1,13},{5,9},{9,5},{13,1},{2,14},{6,10},... | collective-permute-start | bytes 5898248 | tf_op jit(solution)/shard_map/ppermute | solution.py:662
  459.8 79.0 %copy-start = (f32[3,128,1280]{2,1,0:T(8,128)}, f32[3,128,1280]{2,1,0:T(8,128)S(1)}, u32[]{:S(2)}) copy-start(f32[3,128,1280]{2,1,0:T(8,128)S(1)} %collective-permute-done.33.refs_1_) | copy-start | bytes 5898244
  459.8 422.6 %collective-permute-start.24 = (f32[3,128,1280]{2,1,0:T(8,128)}, f32[3,128,1280]{2,1,0:T(8,128)}, u32[]{:S(2)}, u32[]{:S(2)}) collective-permute-start(f32[3,128,1280]{2,1,0:T(8,128)} %get-tuple-element.68), channel_id=1, source_target_pairs={{0,4},{4,0},{8,12},{12,8},{1,5},{5,1},{9,13},{13,9},{2,6},{6,2},{1... | collective-permute-start | bytes 5898248 | tf_op jit(solution)/shard_map/ppermute | solution.py:662
  506.3 376.0 %collective-permute-start.25 = (f32[3,128,1280]{2,1,0:T(8,128)}, f32[3,128,1280]{2,1,0:T(8,128)}, u32[]{:S(2)}, u32[]{:S(2)}) collective-permute-start(f32[3,128,1280]{2,1,0:T(8,128)} %get-tuple-element.69), channel_id=1, source_target_pairs={{0,8},{4,12},{8,0},{12,4},{1,9},{5,13},{9,1},{13,5},{2,10},{6,14},... | collective-permute-start | bytes 5898248 | tf_op jit(solution)/shard_map/ppermute | solution.py:662
  506.9 375.4 %collective-permute-start.26 = (f32[3,128,1280]{2,1,0:T(8,128)}, f32[3,128,1280]{2,1,0:T(8,128)}, u32[]{:S(2)}, u32[]{:S(2)}) collective-permute-start(f32[3,128,1280]{2,1,0:T(8,128)} %get-tuple-element.70), channel_id=1, source_target_pairs={{0,12},{4,8},{8,4},{12,0},{1,13},{5,9},{9,5},{13,1},{2,14},{6,10},... | collective-permute-start | bytes 5898248 | tf_op jit(solution)/shard_map/ppermute | solution.py:662
  538.8 323.2 %copy-start.7 = (s32[1024,8]{0,1:T(8,128)S(1)}, s32[1024,8]{0,1:T(8,128)}, u32[]{:S(2)}) copy-start(s32[1024,8]{0,1:T(8,128)} %param.9) | copy-start | bytes 98308
  (2 other events, 12.4 us)

commit v3 on v2

--- a/solution.py
+++ b/solution.py
@@ -12,7 +12,7 @@
 CHUNK = 128
 TILE = 512
 MM = 256
-COPY = 64
+HEAD = 384
 VMEM_LIMIT = 60 * 1024 * 1024
 F32 = jnp.float32
 BF16 = jnp.bfloat16
@@ -76,7 +76,7 @@
         starts.append(base)
         pos_row = pos_ref[0, k:k + 1, :]
 
-        def build(c, carry, base=base, pos_row=pos_row, k=k):
+        def build(c, carry=0, base=base, pos_row=pos_row, k=k):
             m = one_hot_block(pos_row, c)
             at = pl.ds(aligned(base + c * CHUNK), CHUNK)
             hot[at, :] = jnp.where(m, 1.0, 0.0).astype(BF16)
@@ -85,29 +85,34 @@
                 rstage[at, :] = jnp.broadcast_to(r, (CHUNK, 128))
             return carry
 
-        lax.fori_loop(0, blocks(n, CHUNK), build, 0)
+        build(0)
+        lax.fori_loop(1, blocks(n, CHUNK), build, 0)
         base = base + blocks(n, 16) * 16
 
+    head = pl.ds(0, HEAD)
+    stage[head, :] = dot(hot[head, :], src_ref[...]).astype(BF16)
+
     def mm(c, carry):
-        at = pl.ds(aligned(c * MM), MM)
+        at = pl.ds(aligned(HEAD + c * MM), MM)
         stage[at, :] = dot(hot[at, :], src_ref[...]).astype(BF16)
         return carry
 
-    lax.fori_loop(0, blocks(base, MM), mm, 0)
+    lax.fori_loop(0, blocks(jnp.maximum(base - HEAD, 0), MM), mm, 0)
 
     for k in range(n_loc):
         n = cnt[s * n_loc + k]
         to = off[s * n_loc + k] + k * region
 
-        def move(c, carry, start=starts[k], to=to):
-            dst = pl.ds(aligned(to + c * COPY), COPY)
-            frm = pl.ds(aligned(start + c * COPY), COPY)
+        def move(c, carry=0, start=starts[k], to=to):
+            dst = pl.ds(aligned(to + c * CHUNK), CHUNK)
+            frm = pl.ds(aligned(start + c * CHUNK), CHUNK)
             pool[dst, :] = stage[frm, :]
             if with_r:
                 rpool[dst, :] = rstage[frm, :]
             return carry
 
-        lax.fori_loop(0, blocks(n, COPY), move, 0)
+        move(0)
+        lax.fori_loop(1, blocks(n, CHUNK), move, 0)
 
     @pl.when(s == n_src - 1)
     def _():
@@ -147,8 +152,7 @@
     d = src.shape[1]
     with_r = r is not None
     rows = n_loc * region
-    scr = n_loc * ((region - TILE) // n_src) + CHUNK
-    scr = up(scr, MM)
+    scr = HEAD + up(n_loc * ((region - TILE) // n_src) + CHUNK - HEAD, MM)
     table = pl.BlockSpec((1, n_loc, tok), lambda s, *_: (s, 0, 0))
     in_specs = [table] + ([table] if with_r else []) + [pl.BlockSpec((tok, d), lambda s, *_: (s, 0))]
     out_shape = [jax.ShapeDtypeStruct((rows, d), BF16)]
@@ -171,8 +175,9 @@
 
 
 def expert_kernel(n_fs, info, x_ref, dy_ref, r_ref, *refs):
-    gu_refs, down_refs, (dx_ref, dr_ref) = refs[:n_fs], refs[n_fs:2 * n_fs], refs[2 * n_fs:2 * n_fs + 2]
-    outs, (w1_ref, w3_ref, w2, a_buf, dh1_buf, dh3_buf, dw1, dw3, dw2t) = refs[2 * n_fs + 2:3 * n_fs + 2], refs[3 * n_fs + 2:]
+    own, gu_refs, down_refs, refs = refs[:3], refs[3:n_fs + 2], refs[n_fs + 2:2 * n_fs + 1], refs[2 * n_fs + 1:]
+    (dx_ref, dr_ref), outs, refs = refs[:2], refs[2:n_fs + 2], refs[n_fs + 2:]
+    w1_ref, w3_ref, w2, a_buf, dh1_buf, dh3_buf, dw1, dw3, dw2t = refs
     i = pl.program_id(0)
     d, f = w1_ref.shape
     dsl = d // n_fs
@@ -184,9 +189,9 @@
         dw2t[...] = jnp.zeros_like(dw2t)
         for m in range(n_fs):
             at = pl.ds(aligned((info[2] ^ m) * dsl, dsl), dsl)
-            w1_ref[at, :] = gu_refs[m][0]
-            w3_ref[at, :] = gu_refs[m][1]
-            w2[:, at] = down_refs[m][...]
+            w1_ref[at, :] = gu_refs[m - 1][0] if m else own[0][0]
+            w3_ref[at, :] = gu_refs[m - 1][1] if m else own[1][0]
+            w2[:, at] = down_refs[m - 1][...] if m else own[2][0]
 
     def tile(m):
         x, dy = x_ref[:m, :], dy_ref[:m, :]
@@ -231,14 +236,15 @@
                 outs[m][t] = acc[at, :]
 
 
-def expert_call(k, info, x_pool, dy_pool, r_pool, gate_up, down, region):
-    n_fs, (f, dsl) = len(down), down[0].shape
+def expert_call(k, n_loc, info, x_pool, dy_pool, r_pool, own, gate_up, down, region):
+    n_fs, (f, dsl) = len(down) + 1, down[0].shape
     d = n_fs * dsl
     first = k * (region // TILE)
     row_map = lambda i, info: (first + jnp.minimum(i, info[1] - 1), 0)
     out_map = lambda i, info: (jnp.minimum(i, info[1] - 1), 0)
     whole = lambda i, info: (0, 0)
     whole3 = lambda i, info: (0, 0, 0)
+    mine = lambda i, info: (info[2] * n_loc + k, 0, 0)
     return pl.pallas_call(
         functools.partial(expert_kernel, n_fs),
         out_shape=[jax.ShapeDtypeStruct((region, d), BF16), jax.ShapeDtypeStruct((region, 128), F32)]
@@ -246,13 +252,14 @@
         grid_spec=pltpu.PrefetchScalarGridSpec(
             num_scalar_prefetch=1, grid=(region // TILE - 1,),
             in_specs=[pl.BlockSpec((TILE, d), row_map), pl.BlockSpec((TILE, d), row_map), pl.BlockSpec((TILE, 128), row_map),
-                      *[pl.BlockSpec((2, dsl, f), whole3)] * n_fs, *[pl.BlockSpec((f, dsl), whole)] * n_fs],
+                      *[pl.BlockSpec((1, dsl, f), mine)] * 2, pl.BlockSpec((1, f, dsl), mine),
+                      *[pl.BlockSpec((2, dsl, f), whole3)] * (n_fs - 1), *[pl.BlockSpec((f, dsl), whole)] * (n_fs - 1)],
             out_specs=[pl.BlockSpec((TILE, d), out_map), pl.BlockSpec((TILE, 128), out_map)]
             + [pl.BlockSpec((3, dsl, f), whole3)] * n_fs,
             scratch_shapes=[pltpu.VMEM((d, f), BF16)] * 2 + [pltpu.VMEM((f, d), BF16)] + [pltpu.VMEM((TILE, f), BF16)] * 3 + [pltpu.VMEM((d, f), F32)] * 3),
         compiler_params=pltpu.CompilerParams(vmem_limit_bytes=VMEM_LIMIT, dimension_semantics=("arbitrary",)),
         cost_estimate=pl.CostEstimate(flops=18 * 3000 * d * f, bytes_accessed=24 * d * f, transcendentals=3000 * f),
-    )(info, x_pool, dy_pool, r_pool, *gate_up, *down)
+    )(info, x_pool, dy_pool, r_pool, *own, *gate_up, *down)
 
 
 def place_kernel(n_fs, n_loc, k, first, me, *refs):
@@ -336,7 +343,7 @@
         frm = off[s * n_loc + k]
         pos_row = pos_ref[0, k:k + 1, :]
 
-        def build(c, carry, base=base, frm=frm, pos_row=pos_row, k=k):
+        def build(c, carry=0, base=base, frm=frm, pos_row=pos_row, k=k):
             m = one_hot_block(pos_row, c)
             at = pl.ds(aligned(base + c * CHUNK), CHUNK)
             src = pl.ds(aligned(frm + c * CHUNK), CHUNK)
@@ -346,25 +353,27 @@
             dr_out[0, k:k + 1, :] += jnp.sum(jnp.where(m, r, 0.0), axis=0, keepdims=True)
             return carry
 
-        lax.fori_loop(0, blocks(n, CHUNK), build, 0)
+        build(0)
+        lax.fori_loop(1, blocks(n, CHUNK), build, 0)
         base = base + blocks(n, 16) * 16
-    tail = pl.ds(aligned(base), MM)
-    hot[tail, :] = jnp.zeros((MM, tok), BF16)
-    stage[tail, :] = jnp.zeros((MM, d), BF16)
-    out[...] = jnp.zeros_like(out)
+    tail = pl.ds(aligned(base), HEAD)
+    hot[tail, :] = jnp.zeros((HEAD, tok), BF16)
+    stage[tail, :] = jnp.zeros((HEAD, d), BF16)
+    head = pl.ds(0, HEAD)
+    out[...] = dot_tn(hot[head, :], stage[head, :])
 
     def mm(c, carry):
-        at = pl.ds(aligned(c * MM), MM)
+        at = pl.ds(aligned(HEAD + c * MM), MM)
         out[...] += dot_tn(hot[at, :], stage[at, :])
         return carry
 
-    lax.fori_loop(0, blocks(base, MM), mm, 0)
+    lax.fori_loop(0, blocks(jnp.maximum(base - HEAD, 0), MM), mm, 0)
 
 
 def combine_rows(cnt, off, pos, dx_pools, dr_pools, region):
     n_src, n_loc, tok = pos.shape
     d = dx_pools[0].shape[1]
-    scr = up(n_loc * ((region - TILE) // n_src) + MM, MM)
+    scr = n_loc * ((region - TILE) // n_src) + HEAD
     hbm = pl.BlockSpec(memory_space=pl.ANY)
     return pl.pallas_call(
         functools.partial(combine_kernel, n_src, n_loc),
@@ -429,8 +438,10 @@
     return copies
 
 
-def spread_kernel(n_fs, n_ep, parts, x_ref, dy_ref, table_ref, x_all, dy_all, table_all,
-                  send, recv, c_send, c_recv, t_send, t_recv, own_sem):
+def spread_kernel(n_fs, n_ep, n_loc, parts, x_ref, dy_ref, table_ref, wg_ref, wu_ref, wd_ref, x_all, dy_all, table_all, *refs):
+    n_out = n_loc * (n_fs - 1)
+    gu_out, down_out, refs = refs[:n_out], refs[n_out:2 * n_out], refs[2 * n_out:]
+    send, recv, c_send, c_recv, t_send, t_recv, own_sem, gu_buf, down_buf, in_sem, out_sem = refs
     tok = x_ref.shape[0]
     mine = block_of(0)
     enter(n_fs, n_ep)
@@ -478,6 +489,24 @@
     for a in range(2):
         for q in range(3):
             share(a, q, 0)
+    f, _ = here()
+    packs = []
+    for k in range(n_loc):
+        for m in range(1, n_fs):
+            n = k * (n_fs - 1) + m - 1
+            at = (f ^ m) * n_loc + k
+            packs.append([pltpu.make_async_copy(wg_ref.at[at], gu_buf.at[n, 0], in_sem.at[3 * n]),
+                          pltpu.make_async_copy(wu_ref.at[at], gu_buf.at[n, 1], in_sem.at[3 * n + 1]),
+                          pltpu.make_async_copy(wd_ref.at[at], down_buf.at[n], in_sem.at[3 * n + 2])])
+            for copy in packs[-1]:
+                copy.start()
+    for n in range(n_out):
+        for copy in packs[n]:
+            copy.wait()
+        for copy in (pltpu.make_async_copy(gu_buf.at[n], gu_out[n], out_sem.at[2 * n]),
+                     pltpu.make_async_copy(down_buf.at[n], down_out[n], out_sem.at[2 * n + 1])):
+            copy.start()
+            local.append(copy)
     for phase in range(3):
         for a in range(2):
             for q in range(3):
@@ -500,23 +529,28 @@
         copy.wait()
 
 
-def spread(x_tok, dy_tok, table, n_fs, n_ep):
+def spread(x_tok, dy_tok, table, w_gate, w_up, w_down, n_fs, n_ep):
     n_dev = n_fs * n_ep
     tok, d = x_tok.shape
+    exp_local, dsl, f = w_gate.shape
+    n_loc = exp_local // n_fs
+    n_out = n_loc * (n_fs - 1)
     third = tok // 3 // 16 * 16
     parts = (tok - 2 * third, third, third)
     vmem, hbm = pl.BlockSpec(memory_space=pltpu.VMEM), pl.BlockSpec(memory_space=pl.ANY)
     full = jax.ShapeDtypeStruct((n_dev * tok, d), x_tok.dtype)
     dma = pltpu.SemaphoreType.DMA
     return pl.pallas_call(
-        functools.partial(spread_kernel, n_fs, n_ep, parts),
-        out_shape=[full, full, jax.ShapeDtypeStruct(table.shape, table.dtype)],
-        in_specs=[vmem] * 3, out_specs=[hbm] * 3,
-        scratch_shapes=[dma((42,)), dma((42,)), dma((48,)), dma((48,)), dma((n_dev,)), dma((n_dev,)), dma((3,))],
+        functools.partial(spread_kernel, n_fs, n_ep, n_loc, parts),
+        out_shape=[full, full, jax.ShapeDtypeStruct(table.shape, table.dtype)]
+        + [jax.ShapeDtypeStruct((2, dsl, f), BF16)] * n_out + [jax.ShapeDtypeStruct((f, dsl), BF16)] * n_out,
+        in_specs=[vmem] * 3 + [hbm] * 3, out_specs=[hbm] * (3 + 2 * n_out),
+        scratch_shapes=[dma((42,)), dma((42,)), dma((48,)), dma((48,)), dma((n_dev,)), dma((n_dev,)), dma((3,)),
+                        pltpu.VMEM((n_out, 2, dsl, f), BF16), pltpu.VMEM((n_out, f, dsl), BF16), dma((3 * n_out,)), dma((2 * n_out,))],
         compiler_params=pltpu.CompilerParams(collective_id=0, has_side_effects=True, vmem_limit_bytes=VMEM_LIMIT),
         cost_estimate=pl.CostEstimate(flops=0, bytes_accessed=8 * n_dev * tok * d, transcendentals=0),
         name="spread",
-    )(x_tok, dy_tok, table)
+    )(x_tok, dy_tok, table, w_gate, w_up, w_down)
 
 
 def collect_kernel(n_fs, n_ep, parts, part_ref, dr_ref, gx_ref, dr_home, acc, sib, got,
@@ -625,23 +659,17 @@
         position, weight = route_tables(expert_ids, route_w, experts, capacity)
         table = jnp.stack([position, weight], axis=1).reshape(n_ep, n_fs, n_loc, 2, tok)
         table = table.transpose(1, 0, 2, 3, 4).reshape(n_dev, n_loc * 2, tok)
-        x_all, dy_all, table = spread(x_tok, dy_tok, table, n_fs, n_ep)
+        x_all, dy_all, table, *packed = spread(x_tok, dy_tok, table, w_gate, w_up, w_down, n_fs, n_ep)
         table = table.reshape(n_dev, n_loc, 2, tok)
         me = lax.axis_index("fsdp").astype(jnp.int32)
-
-        def to_owners(k):
-            gate_up, down = [], []
-            for m in range(n_fs):
-                at = (me ^ m) * n_loc + k
-                gu = jnp.stack([lax.dynamic_index_in_dim(w, at, 0, keepdims=False) for w in (w_gate, w_up)])
-                dn = lax.dynamic_index_in_dim(w_down, at, 0, keepdims=False)
-                if m:
-                    gu, dn = [lax.ppermute(v, "fsdp", [(i, i ^ m) for i in range(n_fs)]) for v in (gu, dn)]
-                gate_up.append(gu)
-                down.append(dn)
-            return gate_up, down
-
-        weights = [to_owners(k) for k in range(n_loc)]
+        weights = []
+        for k in range(n_loc):
+            slices = []
+            for kind in range(2):
+                at = (kind * n_loc + k) * (n_fs - 1)
+                slices.append([lax.ppermute(packed[at + m - 1], "fsdp", [(i, i ^ m) for i in range(n_fs)])
+                               for m in range(1, n_fs)])
+            weights.append(slices)
 
         pos = table[:, :, 0, :].astype(jnp.int32)
         r = table[:, :, 1, :]
@@ -656,7 +684,8 @@
         dx_pools, dr_pools, pieces = [], [], []
         for k in range(n_loc):
             info = jnp.stack([rows[k], jnp.maximum(1, blocks(rows[k], TILE)), me])
-            dxk, drk, *slices = expert_call(k, info, x_pool, dy_pool, r_pool, *weights[k], region)
+            dxk, drk, *slices = expert_call(
+                k, n_loc, info, x_pool, dy_pool, r_pool, (w_gate, w_up, w_down), *weights[k], region)
             dx_pools.append(dxk)
             dr_pools.append(drk)
             pieces.append([slices[0]] + [lax.ppermute(slices[m], "fsdp", [(i, i ^ m) for i in range(n_fs)])

time: 898 us -> 859 us (0.957)
  waiting for transfers between devices: 106 us -> 88.4 us
  other arithmetic: 21.2 us -> 9.36 us
    pallas_call x1, Pallas kernels: 322 us -> 349 us  [collect(): pl.pallas_call(functools.partial(collect_kernel, n_fs, n_ep, parts), out_...]
    another operation x16 -> x0, other arithmetic: 12.8 us -> none  [to_owners(): jnp.stack([lax.dynamic_index_in_dim(w, at, 0, keepdims=False) for w in (w...]
    ppermute x24, waiting for transfers between devices: 17.6 us -> 4.98 us  [body(): lax.ppermute(packed[at + m - 1], 'fsdp', [(i, i ^ m) for i in range(n_fs)])]
  transfers between devices with their start and end apart: 36 -> 36, of which waited for: 8 -> 5; matrix products, arithmetic and copies ran while one was open for 4% -> 1% of each run, Pallas kernels for 77% -> 66%
where the time goes in v3:
time: 859 us; the launch traced here: 852 us
  Pallas kernels  699 us (81%)
  waiting for transfers between devices  88.4 us (10%)
  starting transfers between devices  42.6 us (5%)
  other arithmetic  9.36 us (1%)
    pallas_call x1, Pallas kernels, collect(): pl.pallas_call(functools.partial(collect_kernel, n_fs, n_ep, parts), out_...  349 us
    pallas_call x1, Pallas kernels, spread(): pl.pallas_call(functools.partial(spread_kernel, n_fs, n_ep, n_loc, parts)...  128 us
    pallas_call x4, Pallas kernels, expert_call(): pl.pallas_call(functools.partial(expert_kernel, n_fs), out_shape=[jax.Sha...  119 us
    ppermute x12, waiting for transfers between devices, body(): lax.ppermute(slices[m], 'fsdp', [(i, i ^ m) for i in range(n_fs)])  83.4 us
    pallas_call x2, Pallas kernels, gather_rows(): pl.pallas_call(functools.partial(gather_kernel, n_src, n_loc, region, wit...  48.4 us
    pallas_call x1, Pallas kernels, combine_rows(): pl.pallas_call(functools.partial(combine_kernel, n_src, n_loc), out_shape...  28.2 us
    ppermute x24, starting transfers between devices, body(): lax.ppermute(packed[at + m - 1], 'fsdp', [(i, i ^ m) for i in range(n_fs)])  27.7 us
    pallas_call x4, Pallas kernels, place(): pl.pallas_call(functools.partial(place_kernel, n_fs, n_loc, k, first), ou...  25.9 us
  transfers between devices with their start and end apart: 36, of which 5 were waited for; matrix products, arithmetic and copies ran while one was open for 1% of the time, Pallas kernels for 66%

profile of v3, /device:TPU:0, one launch (start us, length us, event | category | flops | bytes accessed | tf_op | source)
XLA Modules:
  0.0 851.8 jit_solution(10803221208156234407)
XLA Ops:
  0.7 1.1 fusion.1
  3.2 1.2 reshape.49.table_ref
  4.3 128.3 %spread.1 = (bf16[16384,512]{1,0:T(8,128)(2,1)}, bf16[16384,512]{1,0:T(8,128)(2,1)}, f32[16,8,1024]{2,1,0:T(8,128)}, bf16[2,128,1280]{2,1,0:T(8,128)(2,1)}, bf16...) custom-call(bf16[1024,512]{1,0:T(8,128)(2,1)} %x_ref.1, ...), custom_call_target="tpu_custom_call" | custom-call | bytes 67108864 | tf_op jit(solution)/shard_map/spread/pallas_call | solution.py:543
  133.2 1.5 collective-permute-start.4
  134.6 1.5 collective-permute-start.5
  136.7 1.5 collective-permute-start.10
  138.1 1.3 copy.28
  142.2 21.6 %gather_x.1.x_ref = bf16[26624,512]{1,0:T(8,128)(2,1)} custom-call(s32[64]{0:T(128)} %add.54.refs_0_.cnt, s32[64]{0:T(128)} %fusion.8.refs_1_.off, s32[16,4,1024]{2,1,0:T(4,128)} %fusion.2.refs_2_.pos_ref, bf16[16384,512]{1,0:T(8,128)(2,1)} %get-tuple-element.75.refs_3_), custom_call_target="tpu_custom_call" | custom-call | flops 12582912000 | bytes 33554432 | tf_op jit(solution)/shard_map/gather_x/pallas_call | solution.py:163
  164.6 1.5 collective-permute-start.15
  167.3 2.4 collective-permute-start.14
  169.7 26.9 %gather_r.1 = (bf16[26624,512]{1,0:T(8,128)(2,1)}, f32[26624,128]{1,0:T(8,128)}) custom-call(s32[64]{0:T(128)} %add.54.refs_0_.cnt, s32[64]{0:T(128)} %fusion.8.refs_1_.off, s32[16,4,1024]{2,1,0:T(4,128)} %fusion.2.refs_2_.pos_ref, f32[16,4,1024]{2,1,0:T(4,128)} %bitcast.30, bf16[16384,512]{1,0:T(8,128)(2,1)} %get-tuple-element.76.refs_4_), custom_call_target="tpu_custom_call" | custom-call | flops 12582912000 | bytes 33554432 | tf_op jit(solution)/shard_map/gather_r/pallas_call | solution.py:163
  199.8 1.3 add_add_fusion.3.info
  201.6 1.5 collective-permute-start.17
  203.1 1.3 add_add_fusion.2.info
  204.4 1.3 add_add_fusion.1.info
  205.6 1.3 add_add_fusion.info
  206.9 4.9 collective-permute-done.16.refs_7_
  211.9 1.0 collective-permute-start.11
  213.9 1.0 collective-permute-start.6
  214.9 1.0 collective-permute-start.7
  215.9 1.5 collective-permute-start.8
  217.4 29.7 %shard_map.112 = (bf16[6656,512]{1,0:T(8,128)(2,1)}, f32[6656,128]{1,0:T(8,128)}, f32[3,128,1280]{2,1,0:T(8,128)}, f32[3,128,1280]{2,1,0:T(8,128)}, f32[3,128,1280]{2,1,0:T(8,128)}, /*index=5*/f32[3,128,1280]{2,1,0:T(8,128)}) custom-call(s32[3]{0:T(128)} %add_add_fusion.2.info, bf16[26624,512]{1,0:T(8,128)(2,1)} %gather_x.1.x_ref, ...), custom_call_target="tpu_custom_call" | custom-call | flops 35389440000 | bytes 15728640 | tf_op jit(solution)/shard_map/pallas_call | solution.py:248
  247.1 1.5 collective-permute-start.22
  248.6 1.0 collective-permute-start.23
  250.7 1.5 collective-permute-start.1
  253.0 1.1 collective-permute-start.2
  254.0 29.9 %shard_map.111 = (bf16[6656,512]{1,0:T(8,128)(2,1)}, f32[6656,128]{1,0:T(8,128)}, f32[3,128,1280]{2,1,0:T(8,128)}, f32[3,128,1280]{2,1,0:T(8,128)}, f32[3,128,1280]{2,1,0:T(8,128)}, /*index=5*/f32[3,128,1280]{2,1,0:T(8,128)}) custom-call(s32[3]{0:T(128)} %add_add_fusion.1.info, bf16[26624,512]{1,0:T(8,128)(2,1)} %gather_x.1.x_ref, ...), custom_call_target="tpu_custom_call" | custom-call | flops 35389440000 | bytes 15728640 | tf_op jit(solution)/shard_map/pallas_call | solution.py:248
  284.0 1.2 collective-permute-start.18
  285.2 1.2 collective-permute-start.19
  286.4 1.2 collective-permute-start.20
  287.5 1.1 collective-permute-start.27
  289.6 29.7 %shard_map.110 = (bf16[6656,512]{1,0:T(8,128)(2,1)}, f32[6656,128]{1,0:T(8,128)}, f32[3,128,1280]{2,1,0:T(8,128)}, f32[3,128,1280]{2,1,0:T(8,128)}, f32[3,128,1280]{2,1,0:T(8,128)}, /*index=5*/f32[3,128,1280]{2,1,0:T(8,128)}) custom-call(s32[3]{0:T(128)} %add_add_fusion.info, bf16[26624,512]{1,0:T(8,128)(2,1)} %gather_x.1.x_ref, ...), custom_call_target="tpu_custom_call" | custom-call | flops 35389440000 | bytes 15728640 | tf_op jit(solution)/shard_map/pallas_call | solution.py:248
  320.2 1.7 collective-permute-start.32
  323.7 25.4 %collective-permute-done.30.refs_1_ = f32[3,128,1280]{2,1,0:T(8,128)} collective-permute-done((f32[3,128,1280]{2,1,0:T(8,128)}, f32[3,128,1280]{2,1,0:T(8,128)}, u32[]{:S(2)}, u32[]{:S(2)}) %collective-permute-start.30) | collective-permute-done | bytes 1966112 | tf_op jit(solution)/shard_map/ppermute | solution.py:691
  349.1 2.7 collective-permute-start.35
  351.8 29.6 %shard_map.113 = (bf16[6656,512]{1,0:T(8,128)(2,1)}, f32[6656,128]{1,0:T(8,128)}, f32[3,128,1280]{2,1,0:T(8,128)}, f32[3,128,1280]{2,1,0:T(8,128)}, f32[3,128,1280]{2,1,0:T(8,128)}, /*index=5*/f32[3,128,1280]{2,1,0:T(8,128)}) custom-call(s32[3]{0:T(128)} %add_add_fusion.3.info, bf16[26624,512]{1,0:T(8,128)(2,1)} %gather_x.1.x_ref, ...), custom_call_target="tpu_custom_call" | custom-call | flops 35389440000 | bytes 15728640 | tf_op jit(solution)/shard_map/pallas_call | solution.py:248
  381.4 1.3 collective-permute-start.28
  382.7 5.5 collective-permute-done.32.refs_3_
  388.2 3.4 collective-permute-start.29
  391.6 18.9 %collective-permute-done.33.refs_1_ = f32[3,128,1280]{2,1,0:T(8,128)S(1)} collective-permute-done((f32[3,128,1280]{2,1,0:T(8,128)}, f32[3,128,1280]{2,1,0:T(8,128)S(1)}, u32[]{:S(2)}, u32[]{:S(2)}) %collective-permute-start.33) | collective-permute-done | bytes 1966112 | tf_op jit(solution)/shard_map/ppermute | solution.py:691
  410.6 1.1 collective-permute-start.24
  411.7 33.4 %collective-permute-done.34.refs_2_ = f32[3,128,1280]{2,1,0:T(8,128)} collective-permute-done((f32[3,128,1280]{2,1,0:T(8,128)}, f32[3,128,1280]{2,1,0:T(8,128)}, u32[]{:S(2)}, u32[]{:S(2)}) %collective-permute-start.34) | collective-permute-done | bytes 1966112 | tf_op jit(solution)/shard_map/ppermute | solution.py:691
  445.2 28.2 %combine.1 = (f32[16384,512]{1,0:T(8,128)}, f32[16,4,1024]{2,1,0:T(4,128)}) custom-call(s32[64]{0:T(128)} %add.54.refs_0_.cnt, s32[64]{0:T(128)} %fusion.8.refs_1_.off, s32[16,4,1024]{2,1,0:T(4,128)} %fusion.2.refs_2_.pos_ref, bf16[6656,512]{1,0:T(8,128)(2,1)} %get-tuple-element.85.refs_0_, bf16[6656,512]{1,0:T(8,128)(2,1)} %get-tuple-element.92.refs_1_, ...), custom_call_target="tpu_custom_call" | custom-call | flops 12582912000 | bytes 33554432 | tf_op jit(solution)/shard_map/combine/pallas_call | solution.py:378
  473.4 349.0 %collect.1 = (bf16[1024,512]{1,0:T(8,128)(2,1)}, f32[16,4,1024]{2,1,0:T(4,128)}) custom-call(f32[16384,512]{1,0:T(8,128)} %get-tuple-element.111.part_ref, f32[16,4,1024]{2,1,0:T(4,128)} %get-tuple-element.112.dr_ref), custom_call_target="tpu_custom_call" | custom-call | bytes 67108864 | tf_op jit(solution)/shard_map/collect/pallas_call | solution.py:631
  824.4 6.4 shard_map.114
  830.9 6.5 shard_map.115
  837.4 6.5 shard_map.116
  843.9 6.5 shard_map.117
  (113 shorter events, 17.9 us)
Async XLA Ops:
  132.6 32.0 %collective-permute-start.3 = (bf16[1280,128]{1,0:T(8,128)(2,1)}, bf16[1280,128]{1,0:T(8,128)(2,1)S(1)}, u32[]{:S(2)}, u32[]{:S(2)}) collective-permute-start(bf16[1280,128]{1,0:T(8,128)(2,1)} %get-tuple-element.82), channel_id=1, source_target_pairs={{0,4},{4,0},{8,12},{12,8},{1,5},{5,1},{9,13},{13,9},{2,6},{6,2},{1... | collective-permute-start | bytes 983048 | tf_op jit(solution)/shard_map/ppermute | solution.py:670
  133.2 32.9 %collective-permute-start.4 = (bf16[1280,128]{1,0:T(8,128)(2,1)}, bf16[1280,128]{1,0:T(8,128)(2,1)S(1)}, u32[]{:S(2)}, u32[]{:S(2)}) collective-permute-start(bf16[1280,128]{1,0:T(8,128)(2,1)} %get-tuple-element.83), channel_id=1, source_target_pairs={{0,8},{4,12},{8,0},{12,4},{1,9},{5,13},{9,1},{13,5},{2,10},{6,14},... | collective-permute-start | bytes 983048 | tf_op jit(solution)/shard_map/ppermute | solution.py:670
  134.6 32.0 %collective-permute-start.5 = (bf16[1280,128]{1,0:T(8,128)(2,1)}, bf16[1280,128]{1,0:T(8,128)(2,1)S(1)}, u32[]{:S(2)}, u32[]{:S(2)}) collective-permute-start(bf16[1280,128]{1,0:T(8,128)(2,1)} %get-tuple-element.84), channel_id=1, source_target_pairs={{0,12},{4,8},{8,4},{12,0},{1,13},{5,9},{9,5},{13,1},{2,14},{6,10},... | collective-permute-start | bytes 983048 | tf_op jit(solution)/shard_map/ppermute | solution.py:670
  136.1 31.2 %collective-permute-start.9 = (bf16[1280,128]{1,0:T(8,128)(2,1)}, bf16[1280,128]{1,0:T(8,128)(2,1)S(1)}, u32[]{:S(2)}, u32[]{:S(2)}) collective-permute-start(bf16[1280,128]{1,0:T(8,128)(2,1)} %get-tuple-element.89), channel_id=1, source_target_pairs={{0,4},{4,0},{8,12},{12,8},{1,5},{5,1},{9,13},{13,9},{2,6},{6,2},{1... | collective-permute-start | bytes 983048 | tf_op jit(solution)/shard_map/ppermute | solution.py:670
  136.7 64.4 %collective-permute-start.10 = (bf16[1280,128]{1,0:T(8,128)(2,1)}, bf16[1280,128]{1,0:T(8,128)(2,1)}, u32[]{:S(2)}, u32[]{:S(2)}) collective-permute-start(bf16[1280,128]{1,0:T(8,128)(2,1)} %get-tuple-element.90), channel_id=1, source_target_pairs={{0,8},{4,12},{8,0},{12,4},{1,9},{5,13},{9,1},{13,5},{2,10},{6,14},... | collective-permute-start | bytes 983048 | tf_op jit(solution)/shard_map/ppermute | solution.py:670
  142.2 24.5 %copy-start.14 = (bf16[2,128,1280]{2,1,0:T(8,128)(2,1)S(1)}, bf16[2,128,1280]{2,1,0:T(8,128)(2,1)}, u32[]{:S(2)}) copy-start(bf16[2,128,1280]{2,1,0:T(8,128)(2,1)} %get-tuple-element.94) | copy-start | bytes 1966084
  142.2 25.1 %copy-start.13 = (bf16[2,128,1280]{2,1,0:T(8,128)(2,1)S(1)}, bf16[2,128,1280]{2,1,0:T(8,128)(2,1)}, u32[]{:S(2)}) copy-start(bf16[2,128,1280]{2,1,0:T(8,128)(2,1)} %get-tuple-element.95) | copy-start | bytes 1966084
  164.6 37.0 %collective-permute-start.15 = (bf16[1280,128]{1,0:T(8,128)(2,1)}, bf16[1280,128]{1,0:T(8,128)(2,1)}, u32[]{:S(2)}, u32[]{:S(2)}) collective-permute-start(bf16[1280,128]{1,0:T(8,128)(2,1)} %get-tuple-element.96), channel_id=1, source_target_pairs={{0,4},{4,0},{8,12},{12,8},{1,5},{5,1},{9,13},{13,9},{2,6},{6,2},{1... | collective-permute-start | bytes 983048 | tf_op jit(solution)/shard_map/ppermute | solution.py:670
  166.1 47.8 %collective-permute-start.12 = (bf16[2,128,1280]{2,1,0:T(8,128)(2,1)}, bf16[2,128,1280]{2,1,0:T(8,128)(2,1)}, u32[]{:S(2)}, u32[]{:S(2)}) collective-permute-start(bf16[2,128,1280]{2,1,0:T(8,128)(2,1)} %get-tuple-element.93), channel_id=1, source_target_pairs={{0,4},{4,0},{8,12},{12,8},{1,5},{5,1},{9,13},{13,9},{2,6},{6,2},{1... | collective-permute-start | bytes 1966088 | tf_op jit(solution)/shard_map/ppermute | solution.py:670
  166.7 48.3 %collective-permute-start.13 = (bf16[2,128,1280]{2,1,0:T(8,128)(2,1)S(1)}, bf16[2,128,1280]{2,1,0:T(8,128)(2,1)}, u32[]{:S(2)}, u32[]{:S(2)}) collective-permute-start(bf16[2,128,1280]{2,1,0:T(8,128)(2,1)S(1)} %copy-done.14), channel_id=1, source_target_pairs={{0,8},{4,12},{8,0},{12,4},{1,9},{5,13},{9,1},{13,5},{2,10},{6,14},... | collective-permute-start | bytes 1966088 | tf_op jit(solution)/shard_map/ppermute | solution.py:670
  167.3 48.7 %collective-permute-start.14 = (bf16[2,128,1280]{2,1,0:T(8,128)(2,1)S(1)}, bf16[2,128,1280]{2,1,0:T(8,128)(2,1)}, u32[]{:S(2)}, u32[]{:S(2)}) collective-permute-start(bf16[2,128,1280]{2,1,0:T(8,128)(2,1)S(1)} %copy-done.13), channel_id=1, source_target_pairs={{0,12},{4,8},{8,4},{12,0},{1,13},{5,9},{9,5},{13,1},{2,14},{6,10},... | collective-permute-start | bytes 1966088 | tf_op jit(solution)/shard_map/ppermute | solution.py:670
  169.7 44.2 %copy-start.12 = (bf16[2,128,1280]{2,1,0:T(8,128)(2,1)S(1)}, bf16[2,128,1280]{2,1,0:T(8,128)(2,1)}, u32[]{:S(2)}) copy-start(bf16[2,128,1280]{2,1,0:T(8,128)(2,1)} %get-tuple-element.86) | copy-start | bytes 1966084
  169.7 45.3 %copy-start.11 = (bf16[2,128,1280]{2,1,0:T(8,128)(2,1)S(1)}, bf16[2,128,1280]{2,1,0:T(8,128)(2,1)}, u32[]{:S(2)}) copy-start(bf16[2,128,1280]{2,1,0:T(8,128)(2,1)} %get-tuple-element.87) | copy-start | bytes 1966084
  169.7 46.2 %copy-start.10 = (bf16[2,128,1280]{2,1,0:T(8,128)(2,1)S(1)}, bf16[2,128,1280]{2,1,0:T(8,128)(2,1)}, u32[]{:S(2)}) copy-start(bf16[2,128,1280]{2,1,0:T(8,128)(2,1)} %get-tuple-element.88) | copy-start | bytes 1966084
  201.1 10.8 %collective-permute-start.16 = (bf16[1280,128]{1,0:T(8,128)(2,1)}, bf16[1280,128]{1,0:T(8,128)(2,1)S(1)}, u32[]{:S(2)}, u32[]{:S(2)}) collective-permute-start(bf16[1280,128]{1,0:T(8,128)(2,1)} %get-tuple-element.97), channel_id=1, source_target_pairs={{0,8},{4,12},{8,0},{12,4},{1,9},{5,13},{9,1},{13,5},{2,10},{6,14},... | collective-permute-start | bytes 983048 | tf_op jit(solution)/shard_map/ppermute | solution.py:670
  201.6 11.3 %collective-permute-start.17 = (bf16[1280,128]{1,0:T(8,128)(2,1)}, bf16[1280,128]{1,0:T(8,128)(2,1)S(1)}, u32[]{:S(2)}, u32[]{:S(2)}) collective-permute-start(bf16[1280,128]{1,0:T(8,128)(2,1)} %get-tuple-element.98), channel_id=1, source_target_pairs={{0,12},{4,8},{8,4},{12,0},{1,13},{5,9},{9,5},{13,1},{2,14},{6,10},... | collective-permute-start | bytes 983048 | tf_op jit(solution)/shard_map/ppermute | solution.py:670
  211.9 35.2 %collective-permute-start.11 = (bf16[1280,128]{1,0:T(8,128)(2,1)}, bf16[1280,128]{1,0:T(8,128)(2,1)}, u32[]{:S(2)}, u32[]{:S(2)}) collective-permute-start(bf16[1280,128]{1,0:T(8,128)(2,1)} %get-tuple-element.91), channel_id=1, source_target_pairs={{0,12},{4,8},{8,4},{12,0},{1,13},{5,9},{9,5},{13,1},{2,14},{6,10},... | collective-permute-start | bytes 983048 | tf_op jit(solution)/shard_map/ppermute | solution.py:670
  212.9 35.7 %collective-permute-start.21 = (bf16[1280,128]{1,0:T(8,128)(2,1)}, bf16[1280,128]{1,0:T(8,128)(2,1)S(1)}, u32[]{:S(2)}, u32[]{:S(2)}) collective-permute-start(bf16[1280,128]{1,0:T(8,128)(2,1)} %get-tuple-element.103), channel_id=1, source_target_pairs={{0,4},{4,0},{8,12},{12,8},{1,5},{5,1},{9,13},{13,9},{2,6},{6,2},{1... | collective-permute-start | bytes 983048 | tf_op jit(solution)/shard_map/ppermute | solution.py:670
  213.9 35.8 %collective-permute-start.6 = (bf16[2,128,1280]{2,1,0:T(8,128)(2,1)S(1)}, bf16[2,128,1280]{2,1,0:T(8,128)(2,1)}, u32[]{:S(2)}, u32[]{:S(2)}) collective-permute-start(bf16[2,128,1280]{2,1,0:T(8,128)(2,1)S(1)} %copy-done.12), channel_id=1, source_target_pairs={{0,4},{4,0},{8,12},{12,8},{1,5},{5,1},{9,13},{13,9},{2,6},{6,2},{1... | collective-permute-start | bytes 1966088 | tf_op jit(solution)/shard_map/ppermute | solution.py:670
  214.9 35.7 %collective-permute-start.7 = (bf16[2,128,1280]{2,1,0:T(8,128)(2,1)S(1)}, bf16[2,128,1280]{2,1,0:T(8,128)(2,1)S(1)}, u32[]{:S(2)}, u32[]{:S(2)}) collective-permute-start(bf16[2,128,1280]{2,1,0:T(8,128)(2,1)S(1)} %copy-done.11), channel_id=1, source_target_pairs={{0,8},{4,12},{8,0},{12,4},{1,9},{5,13},{9,1},{13,5},{2,10},{6,14},... | collective-permute-start | bytes 1966088 | tf_op jit(solution)/shard_map/ppermute | solution.py:670
  215.9 36.2 %collective-permute-start.8 = (bf16[2,128,1280]{2,1,0:T(8,128)(2,1)S(1)}, bf16[2,128,1280]{2,1,0:T(8,128)(2,1)S(1)}, u32[]{:S(2)}, u32[]{:S(2)}) collective-permute-start(bf16[2,128,1280]{2,1,0:T(8,128)(2,1)S(1)} %copy-done.10), channel_id=1, source_target_pairs={{0,12},{4,8},{8,4},{12,0},{1,13},{5,9},{9,5},{13,1},{2,14},{6,10},... | collective-permute-start | bytes 1966088 | tf_op jit(solution)/shard_map/ppermute | solution.py:670
  247.1 36.9 %collective-permute-start.22 = (bf16[1280,128]{1,0:T(8,128)(2,1)}, bf16[1280,128]{1,0:T(8,128)(2,1)}, u32[]{:S(2)}, u32[]{:S(2)}) collective-permute-start(bf16[1280,128]{1,0:T(8,128)(2,1)} %get-tuple-element.104), channel_id=1, source_target_pairs={{0,8},{4,12},{8,0},{12,4},{1,9},{5,13},{9,1},{13,5},{2,10},{6,14},... | collective-permute-start | bytes 983048 | tf_op jit(solution)/shard_map/ppermute | solution.py:670
  248.6 36.5 %collective-permute-start.23 = (bf16[1280,128]{1,0:T(8,128)(2,1)}, bf16[1280,128]{1,0:T(8,128)(2,1)}, u32[]{:S(2)}, u32[]{:S(2)}) collective-permute-start(bf16[1280,128]{1,0:T(8,128)(2,1)} %get-tuple-element.105), channel_id=1, source_target_pairs={{0,12},{4,8},{8,4},{12,0},{1,13},{5,9},{9,5},{13,1},{2,14},{6,10},... | collective-permute-start | bytes 983048 | tf_op jit(solution)/shard_map/ppermute | solution.py:670
  249.7 36.7 %collective-permute-start = (bf16[2,128,1280]{2,1,0:T(8,128)(2,1)}, bf16[2,128,1280]{2,1,0:T(8,128)(2,1)}, u32[]{:S(2)}, u32[]{:S(2)}) collective-permute-start(bf16[2,128,1280]{2,1,0:T(8,128)(2,1)} %get-tuple-element.79), channel_id=1, source_target_pairs={{0,4},{4,0},{8,12},{12,8},{1,5},{5,1},{9,13},{13,9},{2,6},{6,2},{1... | collective-permute-start | bytes 1966088 | tf_op jit(solution)/shard_map/ppermute | solution.py:670
  250.7 36.9 %collective-permute-start.1 = (bf16[2,128,1280]{2,1,0:T(8,128)(2,1)}, bf16[2,128,1280]{2,1,0:T(8,128)(2,1)}, u32[]{:S(2)}, u32[]{:S(2)}) collective-permute-start(bf16[2,128,1280]{2,1,0:T(8,128)(2,1)} %get-tuple-element.80), channel_id=1, source_target_pairs={{0,8},{4,12},{8,0},{12,4},{1,9},{5,13},{9,1},{13,5},{2,10},{6,14},... | collective-permute-start | bytes 1966088 | tf_op jit(solution)/shard_map/ppermute | solution.py:670
  253.0 31.0 %copy-start.9 = (bf16[2,128,1280]{2,1,0:T(8,128)(2,1)S(1)}, bf16[2,128,1280]{2,1,0:T(8,128)(2,1)}, u32[]{:S(2)}) copy-start(bf16[2,128,1280]{2,1,0:T(8,128)(2,1)} %get-tuple-element.100) | copy-start | bytes 1966084
  253.0 32.2 %copy-start.8 = (bf16[2,128,1280]{2,1,0:T(8,128)(2,1)S(1)}, bf16[2,128,1280]{2,1,0:T(8,128)(2,1)}, u32[]{:S(2)}) copy-start(bf16[2,128,1280]{2,1,0:T(8,128)(2,1)} %get-tuple-element.101) | copy-start | bytes 1966084
  253.0 33.4 %copy-start.7 = (bf16[2,128,1280]{2,1,0:T(8,128)(2,1)S(1)}, bf16[2,128,1280]{2,1,0:T(8,128)(2,1)}, u32[]{:S(2)}) copy-start(bf16[2,128,1280]{2,1,0:T(8,128)(2,1)} %get-tuple-element.102) | copy-start | bytes 1966084
  253.0 34.6 %copy-start.6 = (f32[3,128,1280]{2,1,0:T(8,128)S(1)}, f32[3,128,1280]{2,1,0:T(8,128)}, u32[]{:S(2)}) copy-start(f32[3,128,1280]{2,1,0:T(8,128)} %get-tuple-element.120) | copy-start | bytes 5898244
  253.0 35.7 %collective-permute-start.2 = (bf16[2,128,1280]{2,1,0:T(8,128)(2,1)}, bf16[2,128,1280]{2,1,0:T(8,128)(2,1)}, u32[]{:S(2)}, u32[]{:S(2)}) collective-permute-start(bf16[2,128,1280]{2,1,0:T(8,128)(2,1)} %get-tuple-element.81), channel_id=1, source_target_pairs={{0,12},{4,8},{8,4},{12,0},{1,13},{5,9},{9,5},{13,1},{2,14},{6,10},... | collective-permute-start | bytes 1966088 | tf_op jit(solution)/shard_map/ppermute | solution.py:670
  284.0 35.3 %collective-permute-start.18 = (bf16[2,128,1280]{2,1,0:T(8,128)(2,1)S(1)}, bf16[2,128,1280]{2,1,0:T(8,128)(2,1)}, u32[]{:S(2)}, u32[]{:S(2)}) collective-permute-start(bf16[2,128,1280]{2,1,0:T(8,128)(2,1)S(1)} %copy-done.9), channel_id=1, source_target_pairs={{0,4},{4,0},{8,12},{12,8},{1,5},{5,1},{9,13},{13,9},{2,6},{6,2},{1... | collective-permute-start | bytes 1966088 | tf_op jit(solution)/shard_map/ppermute | solution.py:670
  285.2 35.0 %collective-permute-start.19 = (bf16[2,128,1280]{2,1,0:T(8,128)(2,1)S(1)}, bf16[2,128,1280]{2,1,0:T(8,128)(2,1)}, u32[]{:S(2)}, u32[]{:S(2)}) collective-permute-start(bf16[2,128,1280]{2,1,0:T(8,128)(2,1)S(1)} %copy-done.8), channel_id=1, source_target_pairs={{0,8},{4,12},{8,0},{12,4},{1,9},{5,13},{9,1},{13,5},{2,10},{6,14},... | collective-permute-start | bytes 1966088 | tf_op jit(solution)/shard_map/ppermute | solution.py:670
  286.4 35.5 %collective-permute-start.20 = (bf16[2,128,1280]{2,1,0:T(8,128)(2,1)S(1)}, bf16[2,128,1280]{2,1,0:T(8,128)(2,1)}, u32[]{:S(2)}, u32[]{:S(2)}) collective-permute-start(bf16[2,128,1280]{2,1,0:T(8,128)(2,1)S(1)} %copy-done.7), channel_id=1, source_target_pairs={{0,12},{4,8},{8,4},{12,0},{1,13},{5,9},{9,5},{13,1},{2,14},{6,10},... | collective-permute-start | bytes 1966088 | tf_op jit(solution)/shard_map/ppermute | solution.py:670
  287.5 35.3 %collective-permute-start.27 = (f32[3,128,1280]{2,1,0:T(8,128)S(1)}, f32[3,128,1280]{2,1,0:T(8,128)}, u32[]{:S(2)}, u32[]{:S(2)}) collective-permute-start(f32[3,128,1280]{2,1,0:T(8,128)S(1)} %copy-done.6), channel_id=1, source_target_pairs={{0,4},{4,0},{8,12},{12,8},{1,5},{5,1},{9,13},{13,9},{2,6},{6,2},{1... | collective-permute-start | bytes 5898248 | tf_op jit(solution)/shard_map/ppermute | solution.py:691
  288.7 60.5 %collective-permute-start.30 = (f32[3,128,1280]{2,1,0:T(8,128)}, f32[3,128,1280]{2,1,0:T(8,128)}, u32[]{:S(2)}, u32[]{:S(2)}) collective-permute-start(f32[3,128,1280]{2,1,0:T(8,128)} %get-tuple-element.124), channel_id=1, source_target_pairs={{0,4},{4,0},{8,12},{12,8},{1,5},{5,1},{9,13},{13,9},{2,6},{6,2},{1... | collective-permute-start | bytes 5898248 | tf_op jit(solution)/shard_map/ppermute | solution.py:691
  319.3 62.1 %collective-permute-start.31 = (f32[3,128,1280]{2,1,0:T(8,128)}, f32[3,128,1280]{2,1,0:T(8,128)}, u32[]{:S(2)}, u32[]{:S(2)}) collective-permute-start(f32[3,128,1280]{2,1,0:T(8,128)} %get-tuple-element.125), channel_id=1, source_target_pairs={{0,8},{4,12},{8,0},{12,4},{1,9},{5,13},{9,1},{13,5},{2,10},{6,14},... | collective-permute-start | bytes 5898248 | tf_op jit(solution)/shard_map/ppermute | solution.py:691
  320.2 68.1 %collective-permute-start.32 = (f32[3,128,1280]{2,1,0:T(8,128)}, f32[3,128,1280]{2,1,0:T(8,128)}, u32[]{:S(2)}, u32[]{:S(2)}) collective-permute-start(f32[3,128,1280]{2,1,0:T(8,128)} %get-tuple-element.126), channel_id=1, source_target_pairs={{0,12},{4,8},{8,4},{12,0},{1,13},{5,9},{9,5},{13,1},{2,14},{6,10},... | collective-permute-start | bytes 5898248 | tf_op jit(solution)/shard_map/ppermute | solution.py:691
  321.9 88.7 %collective-permute-start.33 = (f32[3,128,1280]{2,1,0:T(8,128)}, f32[3,128,1280]{2,1,0:T(8,128)S(1)}, u32[]{:S(2)}, u32[]{:S(2)}) collective-permute-start(f32[3,128,1280]{2,1,0:T(8,128)} %get-tuple-element.128), channel_id=1, source_target_pairs={{0,4},{4,0},{8,12},{12,8},{1,5},{5,1},{9,13},{13,9},{2,6},{6,2},{1... | collective-permute-start | bytes 5898248 | tf_op jit(solution)/shard_map/ppermute | solution.py:691
  322.9 122.3 %collective-permute-start.34 = (f32[3,128,1280]{2,1,0:T(8,128)}, f32[3,128,1280]{2,1,0:T(8,128)}, u32[]{:S(2)}, u32[]{:S(2)}) collective-permute-start(f32[3,128,1280]{2,1,0:T(8,128)} %get-tuple-element.129), channel_id=1, source_target_pairs={{0,8},{4,12},{8,0},{12,4},{1,9},{5,13},{9,1},{13,5},{2,10},{6,14},... | collective-permute-start | bytes 5898248 | tf_op jit(solution)/shard_map/ppermute | solution.py:691
  349.1 39.1 %copy-start.5 = (f32[3,128,1280]{2,1,0:T(8,128)S(1)}, f32[3,128,1280]{2,1,0:T(8,128)}, u32[]{:S(2)}) copy-start(f32[3,128,1280]{2,1,0:T(8,128)} %get-tuple-element.122) | copy-start | bytes 5898244
  349.1 96.0 %collective-permute-start.35 = (f32[3,128,1280]{2,1,0:T(8,128)}, f32[3,128,1280]{2,1,0:T(8,128)}, u32[]{:S(2)}, u32[]{:S(2)}) collective-permute-start(f32[3,128,1280]{2,1,0:T(8,128)} %get-tuple-element.130), channel_id=1, source_target_pairs={{0,12},{4,8},{8,4},{12,0},{1,13},{5,9},{9,5},{13,1},{2,14},{6,10},... | collective-permute-start | bytes 5898248 | tf_op jit(solution)/shard_map/ppermute | solution.py:691
  381.4 455.9 %collective-permute-start.28 = (f32[3,128,1280]{2,1,0:T(8,128)}, f32[3,128,1280]{2,1,0:T(8,128)}, u32[]{:S(2)}, u32[]{:S(2)}) collective-permute-start(f32[3,128,1280]{2,1,0:T(8,128)} %get-tuple-element.121), channel_id=1, source_target_pairs={{0,8},{4,12},{8,0},{12,4},{1,9},{5,13},{9,1},{13,5},{2,10},{6,14},... | collective-permute-start | bytes 5898248 | tf_op jit(solution)/shard_map/ppermute | solution.py:691
  388.2 449.1 %collective-permute-start.29 = (f32[3,128,1280]{2,1,0:T(8,128)S(1)}, f32[3,128,1280]{2,1,0:T(8,128)}, u32[]{:S(2)}, u32[]{:S(2)}) collective-permute-start(f32[3,128,1280]{2,1,0:T(8,128)S(1)} %copy-done.5), channel_id=1, source_target_pairs={{0,12},{4,8},{8,4},{12,0},{1,13},{5,9},{9,5},{13,1},{2,14},{6,10},... | collective-permute-start | bytes 5898248 | tf_op jit(solution)/shard_map/ppermute | solution.py:691
  410.6 62.8 %copy-start = (f32[3,128,1280]{2,1,0:T(8,128)}, f32[3,128,1280]{2,1,0:T(8,128)S(1)}, u32[]{:S(2)}) copy-start(f32[3,128,1280]{2,1,0:T(8,128)S(1)} %collective-permute-done.33.refs_1_) | copy-start | bytes 5898244
  410.6 433.3 %collective-permute-start.24 = (f32[3,128,1280]{2,1,0:T(8,128)}, f32[3,128,1280]{2,1,0:T(8,128)}, u32[]{:S(2)}, u32[]{:S(2)}) collective-permute-start(f32[3,128,1280]{2,1,0:T(8,128)} %get-tuple-element.116), channel_id=1, source_target_pairs={{0,4},{4,0},{8,12},{12,8},{1,5},{5,1},{9,13},{13,9},{2,6},{6,2},{1... | collective-permute-start | bytes 5898248 | tf_op jit(solution)/shard_map/ppermute | solution.py:691
  445.1 398.7 %collective-permute-start.25 = (f32[3,128,1280]{2,1,0:T(8,128)}, f32[3,128,1280]{2,1,0:T(8,128)}, u32[]{:S(2)}, u32[]{:S(2)}) collective-permute-start(f32[3,128,1280]{2,1,0:T(8,128)} %get-tuple-element.117), channel_id=1, source_target_pairs={{0,8},{4,12},{8,0},{12,4},{1,9},{5,13},{9,1},{13,5},{2,10},{6,14},... | collective-permute-start | bytes 5898248 | tf_op jit(solution)/shard_map/ppermute | solution.py:691
  445.1 398.7 %collective-permute-start.26 = (f32[3,128,1280]{2,1,0:T(8,128)}, f32[3,128,1280]{2,1,0:T(8,128)}, u32[]{:S(2)}, u32[]{:S(2)}) collective-permute-start(f32[3,128,1280]{2,1,0:T(8,128)} %get-tuple-element.118), channel_id=1, source_target_pairs={{0,12},{4,8},{8,4},{12,0},{1,13},{5,9},{9,5},{13,1},{2,14},{6,10},... | collective-permute-start | bytes 5898248 | tf_op jit(solution)/shard_map/ppermute | solution.py:691
  473.4 350.1 %copy-start.3 = (s32[1024,8]{0,1:T(8,128)S(1)}, s32[1024,8]{0,1:T(8,128)}, u32[]{:S(2)}) copy-start(s32[1024,8]{0,1:T(8,128)} %param.9) | copy-start | bytes 98308
  (12 other events, 39.6 us)

commit v4 on v3

--- a/solution.py
+++ b/solution.py
@@ -149,12 +149,12 @@
 
 def gather_rows(src, cnt, off, pos, r, region):
     n_src, n_loc, tok = pos.shape
-    d = src.shape[1]
+    d = src.shape[1] // 2
     with_r = r is not None
     rows = n_loc * region
     scr = HEAD + up(n_loc * ((region - TILE) // n_src) + CHUNK - HEAD, MM)
     table = pl.BlockSpec((1, n_loc, tok), lambda s, *_: (s, 0, 0))
-    in_specs = [table] + ([table] if with_r else []) + [pl.BlockSpec((tok, d), lambda s, *_: (s, 0))]
+    in_specs = [table] + ([table] if with_r else []) + [pl.BlockSpec((tok, d), lambda s, *_: (s, 1 if with_r else 0))]
     out_shape = [jax.ShapeDtypeStruct((rows, d), BF16)]
     scratch = [pltpu.VMEM((scr, tok), BF16), pltpu.VMEM((scr, d), BF16), pltpu.VMEM((rows, d), BF16)]
     if with_r:
@@ -189,9 +189,9 @@
         dw2t[...] = jnp.zeros_like(dw2t)
         for m in range(n_fs):
             at = pl.ds(aligned((info[2] ^ m) * dsl, dsl), dsl)
-            w1_ref[at, :] = gu_refs[m - 1][0] if m else own[0][0]
-            w3_ref[at, :] = gu_refs[m - 1][1] if m else own[1][0]
-            w2[:, at] = down_refs[m - 1][...] if m else own[2][0]
+            w1_ref[at, :] = gu_refs[m - 1][0, 0] if m else own[0][0]
+            w3_ref[at, :] = gu_refs[m - 1][0, 1] if m else own[1][0]
+            w2[:, at] = down_refs[m - 1][0] if m else own[2][0]
 
     def tile(m):
         x, dy = x_ref[:m, :], dy_ref[:m, :]
@@ -236,13 +236,12 @@
                 outs[m][t] = acc[at, :]
 
 
-def expert_call(k, n_loc, info, x_pool, dy_pool, r_pool, own, gate_up, down, region):
-    n_fs, (f, dsl) = len(down) + 1, down[0].shape
+def expert_call(k, group_at, n_loc, info, x_pool, dy_pool, r_pool, own, gate_up, down, region):
+    n_fs, (_, f, dsl) = len(down) + 1, down[0].shape
     d = n_fs * dsl
     first = k * (region // TILE)
     row_map = lambda i, info: (first + jnp.minimum(i, info[1] - 1), 0)
     out_map = lambda i, info: (jnp.minimum(i, info[1] - 1), 0)
-    whole = lambda i, info: (0, 0)
     whole3 = lambda i, info: (0, 0, 0)
     mine = lambda i, info: (info[2] * n_loc + k, 0, 0)
     return pl.pallas_call(
@@ -253,7 +252,8 @@
             num_scalar_prefetch=1, grid=(region // TILE - 1,),
             in_specs=[pl.BlockSpec((TILE, d), row_map), pl.BlockSpec((TILE, d), row_map), pl.BlockSpec((TILE, 128), row_map),
                       *[pl.BlockSpec((1, dsl, f), mine)] * 2, pl.BlockSpec((1, f, dsl), mine),
-                      *[pl.BlockSpec((2, dsl, f), whole3)] * (n_fs - 1), *[pl.BlockSpec((f, dsl), whole)] * (n_fs - 1)],
+                      *[pl.BlockSpec((1, 2, dsl, f), lambda i, info: (group_at, 0, 0, 0))] * (n_fs - 1),
+                      *[pl.BlockSpec((1, f, dsl), lambda i, info: (group_at, 0, 0))] * (n_fs - 1)],
             out_specs=[pl.BlockSpec((TILE, d), out_map), pl.BlockSpec((TILE, 128), out_map)]
             + [pl.BlockSpec((3, dsl, f), whole3)] * n_fs,
             scratch_shapes=[pltpu.VMEM((d, f), BF16)] * 2 + [pltpu.VMEM((f, d), BF16)] + [pltpu.VMEM((TILE, f), BF16)] * 3 + [pltpu.VMEM((d, f), F32)] * 3),
@@ -396,6 +396,7 @@
 HOPS = ((0, 2), (1, 0), (2, 0))
 SIBLING = (0, 1)
 ORDERS = ((0, 1, 2), (1, 2, 0), (2, 0, 1))
+COLLECT_ORDERS = ((0, 1, 2), (0, 2, 1))
 
 
 def here():
@@ -438,41 +439,38 @@
     return copies
 
 
-def spread_kernel(n_fs, n_ep, n_loc, parts, x_ref, dy_ref, table_ref, wg_ref, wu_ref, wd_ref, x_all, dy_all, table_all, *refs):
-    n_out = n_loc * (n_fs - 1)
+def spread_kernel(n_fs, n_ep, n_loc, parts, x_ref, dy_ref, table_ref, wg_ref, wu_ref, wd_ref, full, table_all, *refs):
+    n_slices, n_out = n_loc * (n_fs - 1), 2 * (n_fs - 1)
     gu_out, down_out, refs = refs[:n_out], refs[n_out:2 * n_out], refs[2 * n_out:]
-    send, recv, c_send, c_recv, t_send, t_recv, own_sem, gu_buf, down_buf, in_sem, out_sem = refs
-    tok = x_ref.shape[0]
+    own, send, recv, c_send, c_recv, t_send, t_recv, own_sem, gu_buf, down_buf, in_sem, out_sem = refs
+    tok, d = x_ref.shape
     mine = block_of(0)
+    local = []
+    for n, src in enumerate((x_ref, dy_ref)):
+        local.append(pltpu.make_async_copy(src, own.at[:, pl.ds(n * d, d)], own_sem.at[n]))
+        local[-1].start()
     enter(n_fs, n_ep)
-    pending = []
-    local = []
-    for n, (src, dst) in enumerate(((x_ref, x_all), (dy_ref, dy_all))):
-        local.append(pltpu.make_async_copy(src, dst.at[pl.ds(aligned(mine * tok, tok), tok)], own_sem.at[n]))
-    local.append(pltpu.make_async_copy(table_ref.at[mine], table_all.at[mine], own_sem.at[2]))
     for copy in local:
-        copy.start()
-    pending += exchange(n_fs, n_ep, table_ref, table_all, t_send, t_recv)
-    arrays = ((x_ref, x_all), (dy_ref, dy_all))
+        copy.wait()
+    local = [pltpu.make_async_copy(own, full.at[pl.ds(aligned(mine * tok, tok), tok)], own_sem.at[0]),
+             pltpu.make_async_copy(table_ref.at[mine], table_all.at[mine], own_sem.at[2])]
     starts = [sum(parts[:q]) for q in range(3)]
     sem_at = {}
     inbound = {}
 
-    def send_on(a, q, phase, bits):
-        own, full = arrays[a]
+    def send_on(q, phase, bits):
         to = pl.ds(aligned(block_of(bits) * tok + starts[q], 16), parts[q])
         src = own.at[pl.ds(starts[q], parts[q])] if bits == 0 else full.at[to]
-        n = sem_at.setdefault((a, q, phase, bits), len(sem_at))
+        n = sem_at.setdefault((q, phase, bits), len(sem_at))
         copy = pltpu.make_async_remote_copy(
             src_ref=src, dst_ref=full.at[to], send_sem=send.at[n], recv_sem=recv.at[n],
             device_id=peer_of(HOPS[ORDERS[q][phase]]), device_id_type=MESH)
         copy.start()
-        inbound[(a, q, phase, bits)] = copy
+        inbound[(q, phase, bits)] = copy
 
     shared = []
 
-    def share(a, q, bits):
-        own, full = arrays[a]
+    def share(q, bits):
         to = pl.ds(aligned(block_of(bits) * tok + starts[q], 16), parts[q])
         src = own.at[pl.ds(starts[q], parts[q])] if bits == 0 else full.at[to]
         n = len(shared)
@@ -483,12 +481,13 @@
         shared.append(copy)
 
     for phase in range(3):
-        for a in range(2):
-            for q in range(3):
-                send_on(a, q, phase, 0)
-    for a in range(2):
         for q in range(3):
-            share(a, q, 0)
+            send_on(q, phase, 0)
+    for q in range(3):
+        share(q, 0)
+    for copy in local:
+        copy.start()
+    pending = exchange(n_fs, n_ep, table_ref, table_all, t_send, t_recv)
     f, _ = here()
     packs = []
     for k in range(n_loc):
@@ -500,25 +499,26 @@
                           pltpu.make_async_copy(wd_ref.at[at], down_buf.at[n], in_sem.at[3 * n + 2])])
             for copy in packs[-1]:
                 copy.start()
-    for n in range(n_out):
+    for n in range(n_slices):
         for copy in packs[n]:
             copy.wait()
-        for copy in (pltpu.make_async_copy(gu_buf.at[n], gu_out[n], out_sem.at[2 * n]),
-                     pltpu.make_async_copy(down_buf.at[n], down_out[n], out_sem.at[2 * n + 1])):
+        k, m = n // (n_fs - 1), n % (n_fs - 1)
+        to, at = (m, 0) if k == 0 else (n_fs - 1 + m, k - 1)
+        for copy in (pltpu.make_async_copy(gu_buf.at[n], gu_out[to].at[at], out_sem.at[2 * n]),
+                     pltpu.make_async_copy(down_buf.at[n], down_out[to].at[at], out_sem.at[2 * n + 1])):
             copy.start()
             local.append(copy)
     for phase in range(3):
-        for a in range(2):
-            for q in range(3):
-                held = [0]
-                for axis in ORDERS[q][:phase]:
-                    held += [b | 1 << axis for b in held]
-                for b in held:
-                    inbound[(a, q, phase, b)].wait_recv()
-                    got = b | 1 << ORDERS[q][phase]
-                    for later in range(phase + 1, 3):
-                        send_on(a, q, later, got)
-                    share(a, q, got)
+        for q in range(3):
+            held = [0]
+            for axis in ORDERS[q][:phase]:
+                held += [b | 1 << axis for b in held]
+            for b in held:
+                inbound[(q, phase, b)].wait_recv()
+                got = b | 1 << ORDERS[q][phase]
+                for later in range(phase + 1, 3):
+                    send_on(q, later, got)
+                share(q, got)
     for copy in inbound.values():
         copy.wait_send()
     for copy in shared:
@@ -534,19 +534,19 @@
     tok, d = x_tok.shape
     exp_local, dsl, f = w_gate.shape
     n_loc = exp_local // n_fs
-    n_out = n_loc * (n_fs - 1)
+    n_slices, groups = n_loc * (n_fs - 1), [1] * (n_fs - 1) + [n_loc - 1] * (n_fs - 1)
     third = tok // 3 // 16 * 16
     parts = (tok - 2 * third, third, third)
     vmem, hbm = pl.BlockSpec(memory_space=pltpu.VMEM), pl.BlockSpec(memory_space=pl.ANY)
-    full = jax.ShapeDtypeStruct((n_dev * tok, d), x_tok.dtype)
     dma = pltpu.SemaphoreType.DMA
     return pl.pallas_call(
         functools.partial(spread_kernel, n_fs, n_ep, n_loc, parts),
-        out_shape=[full, full, jax.ShapeDtypeStruct(table.shape, table.dtype)]
-        + [jax.ShapeDtypeStruct((2, dsl, f), BF16)] * n_out + [jax.ShapeDtypeStruct((f, dsl), BF16)] * n_out,
-        in_specs=[vmem] * 3 + [hbm] * 3, out_specs=[hbm] * (3 + 2 * n_out),
-        scratch_shapes=[dma((42,)), dma((42,)), dma((48,)), dma((48,)), dma((n_dev,)), dma((n_dev,)), dma((3,)),
-                        pltpu.VMEM((n_out, 2, dsl, f), BF16), pltpu.VMEM((n_out, f, dsl), BF16), dma((3 * n_out,)), dma((2 * n_out,))],
+        out_shape=[jax.ShapeDtypeStruct((n_dev * tok, 2 * d), x_tok.dtype), jax.ShapeDtypeStruct(table.shape, table.dtype)]
+        + [jax.ShapeDtypeStruct((g, 2, dsl, f), BF16) for g in groups] + [jax.ShapeDtypeStruct((g, f, dsl), BF16) for g in groups],
+        in_specs=[hbm] * 2 + [vmem] + [hbm] * 3, out_specs=[hbm] * (2 + 2 * len(groups)),
+        scratch_shapes=[pltpu.VMEM((tok, 2 * d), BF16), dma((21,)), dma((21,)), dma((24,)), dma((24,)), dma((n_dev,)), dma((n_dev,)),
+                        dma((3,)), pltpu.VMEM((n_slices, 2, dsl, f), BF16), pltpu.VMEM((n_slices, f, dsl), BF16),
+                        dma((3 * n_slices,)), dma((2 * n_slices,))],
         compiler_params=pltpu.CompilerParams(collective_id=0, has_side_effects=True, vmem_limit_bytes=VMEM_LIMIT),
         cost_estimate=pl.CostEstimate(flops=0, bytes_accessed=8 * n_dev * tok * d, transcendentals=0),
         name="spread",
@@ -561,7 +561,7 @@
     drs = exchange(n_fs, n_ep, dr_ref, dr_home, t_send, t_recv)
     local_dr = pltpu.make_async_copy(dr_ref.at[mine], dr_home.at[mine], own_sem.at[8])
     local_dr.start()
-    order = (7, 3, 5, 6, 1, 2, 4, 0)
+    order = (7, 3, 5, 1, 6, 2, 4, 0)
     loads, shares = {}, {}
     for bits in order:
         theirs = pl.ds(aligned(block_of(bits, 1) * tok, tok), tok)
@@ -572,23 +572,23 @@
         ours = pl.ds(aligned(block_of(bits) * tok, tok), tok)
         loads[bits] = pltpu.make_async_copy(part_ref.at[ours], acc.at[bits], own_sem.at[bits])
         loads[bits].start()
-    starts = [sum(parts[:q]) for q in range(3)]
-    slots = [(q, bits) for q in range(3) for bits in range(1, 8)]
+    starts = [sum(parts[:q]) for q in range(len(parts))]
+    slots = [(q, bits) for q in range(len(parts)) for bits in range(1, 8)]
     hops = {}
 
     def phase_of(q, bits):
-        return next(n for n in range(3) if bits >> ORDERS[q][n] & 1)
+        return next(n for n in range(3) if bits >> COLLECT_ORDERS[q][n] & 1)
 
     def send_off(q, bits):
         n = slots.index((q, bits))
         rows = pl.ds(starts[q], parts[q])
         hops[(q, bits)] = pltpu.make_async_remote_copy(
             src_ref=acc.at[bits, rows], dst_ref=got.at[bits - 1, rows], send_sem=send.at[n], recv_sem=recv.at[n],
-            device_id=peer_of(HOPS[ORDERS[q][phase_of(q, bits)]]), device_id_type=MESH)
+            device_id=peer_of(HOPS[COLLECT_ORDERS[q][phase_of(q, bits)]]), device_id_type=MESH)
         hops[(q, bits)].start()
 
     def add_arrival(q, bits, phase):
-        frm = bits | 1 << ORDERS[q][phase]
+        frm = bits | 1 << COLLECT_ORDERS[q][phase]
         hops[(q, frm)].wait_recv()
         rows = slice(starts[q], starts[q] + parts[q])
         acc[bits, rows, :] = acc[bits, rows, :] + got[frm - 1, rows, :]
@@ -597,17 +597,17 @@
         loads[bits].wait()
         shares[bits].wait_recv()
         acc[bits] = acc[bits] + sib[bits]
-        for q in range(3):
+        for q in range(len(parts)):
             if bits and phase_of(q, bits) == 0:
                 send_off(q, bits)
     for phase in (1, 2):
-        for q in range(3):
+        for q in range(len(parts)):
             for bits in range(1, 8):
                 if phase_of(q, bits) == phase:
                     for earlier in range(phase):
                         add_arrival(q, bits, earlier)
                     send_off(q, bits)
-    for q in range(3):
+    for q in range(len(parts)):
         for phase in range(3):
             add_arrival(q, 0, phase)
         rows = slice(starts[q], starts[q] + parts[q])
@@ -624,8 +624,8 @@
 def collect(dx_part, dr_part, n_fs, n_ep):
     n_dev = n_fs * n_ep
     tok, d = dx_part.shape[0] // n_dev, dx_part.shape[1]
-    quarter = tok // 4 // 8 * 8
-    parts = (tok - 2 * quarter, quarter, quarter)
+    half = tok // 2 // 8 * 8
+    parts = (tok - half, half)
     vmem, hbm = pl.BlockSpec(memory_space=pltpu.VMEM), pl.BlockSpec(memory_space=pl.ANY)
     dma = pltpu.SemaphoreType.DMA
     return pl.pallas_call(
@@ -633,7 +633,7 @@
         out_shape=[jax.ShapeDtypeStruct((tok, d), BF16), jax.ShapeDtypeStruct(dr_part.shape, F32)],
         in_specs=[hbm, vmem], out_specs=[vmem, vmem],
         scratch_shapes=[pltpu.VMEM((8, tok, d), F32), pltpu.VMEM((8, tok, d), F32), pltpu.VMEM((7, tok, d), F32),
-                        dma((8,)), dma((8,)), dma((21,)), dma((21,)), dma((n_dev,)), dma((n_dev,)), dma((9,))],
+                        dma((8,)), dma((8,)), dma((14,)), dma((14,)), dma((n_dev,)), dma((n_dev,)), dma((9,))],
         compiler_params=pltpu.CompilerParams(collective_id=1, has_side_effects=True, vmem_limit_bytes=VMEM_LIMIT),
         cost_estimate=pl.CostEstimate(flops=0, bytes_accessed=8 * n_dev * tok * d, transcendentals=0),
         name="collect",
@@ -659,17 +659,14 @@
         position, weight = route_tables(expert_ids, route_w, experts, capacity)
         table = jnp.stack([position, weight], axis=1).reshape(n_ep, n_fs, n_loc, 2, tok)
         table = table.transpose(1, 0, 2, 3, 4).reshape(n_dev, n_loc * 2, tok)
-        x_all, dy_all, table, *packed = spread(x_tok, dy_tok, table, w_gate, w_up, w_down, n_fs, n_ep)
+        xdy_all, table, *packed = spread(x_tok, dy_tok, table, w_gate, w_up, w_down, n_fs, n_ep)
         table = table.reshape(n_dev, n_loc, 2, tok)
         me = lax.axis_index("fsdp").astype(jnp.int32)
         weights = []
-        for k in range(n_loc):
-            slices = []
-            for kind in range(2):
-                at = (kind * n_loc + k) * (n_fs - 1)
-                slices.append([lax.ppermute(packed[at + m - 1], "fsdp", [(i, i ^ m) for i in range(n_fs)])
-                               for m in range(1, n_fs)])
-            weights.append(slices)
+        for group in range(2):
+            weights.append([[lax.ppermute(packed[(2 * kind + group) * (n_fs - 1) + m - 1], "fsdp",
+                                          [(i, i ^ m) for i in range(n_fs)]) for m in range(1, n_fs)]
+                            for kind in range(2)])
 
         pos = table[:, :, 0, :].astype(jnp.int32)
         r = table[:, :, 1, :]
@@ -678,14 +675,15 @@
         off = jnp.cumsum(padded, axis=0) - padded
         rows = jnp.sum(padded, axis=0)
         cnt_flat, off_flat = cnt.reshape(-1), off.reshape(-1)
-        x_pool = gather_rows(x_all, cnt_flat, off_flat, pos, None, region)
-        dy_pool, r_pool = gather_rows(dy_all, cnt_flat, off_flat, pos, r, region)
+        x_pool = gather_rows(xdy_all, cnt_flat, off_flat, pos, None, region)
+        dy_pool, r_pool = gather_rows(xdy_all, cnt_flat, off_flat, pos, r, region)
 
         dx_pools, dr_pools, pieces = [], [], []
         for k in range(n_loc):
             info = jnp.stack([rows[k], jnp.maximum(1, blocks(rows[k], TILE)), me])
             dxk, drk, *slices = expert_call(
-                k, n_loc, info, x_pool, dy_pool, r_pool, (w_gate, w_up, w_down), *weights[k], region)
+                k, max(k - 1, 0), n_loc, info, x_pool, dy_pool, r_pool, (w_gate, w_up, w_down),
+                *weights[min(k, 1)], region)
             dx_pools.append(dxk)
             dr_pools.append(drk)
             pieces.append([slices[0]] + [lax.ppermute(slices[m], "fsdp", [(i, i ^ m) for i in range(n_fs)])

time: 859 us -> 918 us (1.069)
  waiting for transfers between devices: 88.4 us -> 130 us
  Pallas kernels: 699 us -> 714 us
    ppermute x24 -> x12, waiting for transfers between devices: 4.98 us -> 68.8 us  [body(): lax.ppermute(packed[(2 * kind + group) * (n_fs - 1) + m - 1], 'fsdp', [(i...]
    ppermute x12, waiting for transfers between devices: 83.4 us -> 61 us  [body(): lax.ppermute(slices[m], 'fsdp', [(i, i ^ m) for i in range(n_fs)])]
    ppermute x12, starting transfers between devices: 14.9 us -> 30.8 us  [body(): lax.ppermute(slices[m], 'fsdp', [(i, i ^ m) for i in range(n_fs)])]
    ppermute x24 -> x12, starting transfers between devices: 27.7 us -> 13.1 us  [body(): lax.ppermute(packed[(2 * kind + group) * (n_fs - 1) + m - 1], 'fsdp', [(i...]
    pallas_call x1, Pallas kernels: 349 us -> 362 us  [collect(): pl.pallas_call(functools.partial(collect_kernel, n_fs, n_ep, parts), out_...]
  transfers between devices with their start and end apart: 36 -> 24, of which waited for: 5 -> 6; matrix products, arithmetic and copies ran while one was open for 1% -> 1% of each run, Pallas kernels for 66% -> 63%
where the time goes in v4:
time: 918 us; the launch traced here: 911 us
  Pallas kernels  714 us (78%)
  waiting for transfers between devices  130 us (14%)
  starting transfers between devices  43.9 us (5%)
  local copies, waits for them, and re-layouts  10.2 us (1%)
    pallas_call x1, Pallas kernels, collect(): pl.pallas_call(functools.partial(collect_kernel, n_fs, n_ep, parts), out_...  362 us
    pallas_call x1, Pallas kernels, spread(): pl.pallas_call(functools.partial(spread_kernel, n_fs, n_ep, n_loc, parts)...  131 us
    pallas_call x4, Pallas kernels, expert_call(): pl.pallas_call(functools.partial(expert_kernel, n_fs), out_shape=[jax.Sha...  119 us
    ppermute x12, waiting for transfers between devices, body(): lax.ppermute(packed[(2 * kind + group) * (n_fs - 1) + m - 1], 'fsdp', [(i...  68.8 us
    ppermute x12, waiting for transfers between devices, body(): lax.ppermute(slices[m], 'fsdp', [(i, i ^ m) for i in range(n_fs)])  61 us
    pallas_call x2, Pallas kernels, gather_rows(): pl.pallas_call(functools.partial(gather_kernel, n_src, n_loc, region, wit...  48.2 us
    ppermute x12, starting transfers between devices, body(): lax.ppermute(slices[m], 'fsdp', [(i, i ^ m) for i in range(n_fs)])  30.8 us
    pallas_call x1, Pallas kernels, combine_rows(): pl.pallas_call(functools.partial(combine_kernel, n_src, n_loc), out_shape...  28.2 us
  transfers between devices with their start and end apart: 24, of which 6 were waited for; matrix products, arithmetic and copies ran while one was open for 1% of the time, Pallas kernels for 63%

profile of v4, /device:TPU:0, one launch (start us, length us, event | category | flops | bytes accessed | tf_op | source)
XLA Modules:
  0.0 911.2 jit_solution(9028169187551804027)
XLA Ops:
  0.7 1.1 fusion.1
  3.2 1.2 reshape.49.table_ref
  4.3 131.3 %spread.1 = (bf16[16384,1024]{1,0:T(8,128)(2,1)}, f32[16,8,1024]{2,1,0:T(8,128)}, bf16[1,2,128,1280]{3,2,1,0:T(8,128)(2,1)}, bf16[1,2,128,1280]{3,2,1,0:T(8,128)...) custom-call(bf16[1024,512]{1,0:T(8,128)(2,1)} %x_ref.1, ...), custom_call_target="tpu_custom_call" | custom-call | bytes 67108864 | tf_op jit(solution)/shard_map/spread/pallas_call | solution.py:542
  135.6 0.6 collective-permute-start.3
  136.2 1.5 collective-permute-start.4
  137.7 1.5 collective-permute-start
  139.7 1.5 collective-permute-start.2
  141.1 1.3 copy.28
  142.9 0.9 fusion.2.refs_2_.pos_ref
  143.8 0.6 add.54.refs_0_.cnt
  145.1 21.4 %gather_x.1.x_ref = bf16[26624,512]{1,0:T(8,128)(2,1)} custom-call(s32[64]{0:T(128)} %add.54.refs_0_.cnt, s32[64]{0:T(128)} %fusion.8.refs_1_.off, s32[16,4,1024]{2,1,0:T(4,128)} %fusion.2.refs_2_.pos_ref, bf16[16384,1024]{1,0:T(8,128)(2,1)} %get-tuple-element.62.refs_3_.refs_4_), custom_call_target="tpu_custom_call" | custom-call | flops 12582912000 | bytes 33554432 | tf_op jit(solution)/shard_map/gather_x/pallas_call | solution.py:163
  166.6 0.9 copy.41
  167.4 0.7 copy-done.10
  168.2 1.5 collective-permute-start.9
  169.6 26.8 %gather_r.1 = (bf16[26624,512]{1,0:T(8,128)(2,1)}, f32[26624,128]{1,0:T(8,128)}) custom-call(s32[64]{0:T(128)} %add.54.refs_0_.cnt, s32[64]{0:T(128)} %fusion.8.refs_1_.off, s32[16,4,1024]{2,1,0:T(4,128)} %fusion.2.refs_2_.pos_ref, f32[16,4,1024]{2,1,0:T(4,128)} %bitcast.30, bf16[16384,1024]{1,0:T(8,128)(2,1)} %get-tuple-element.62.refs_3_.refs_4_), custom_call_target="tpu_custom_call" | custom-call | flops 12582912000 | bytes 33554432 | tf_op jit(solution)/shard_map/gather_r/pallas_call | solution.py:163
  200.3 1.3 add_add_fusion.3.info
  201.6 1.3 add_add_fusion.info
  202.9 1.9 add_add_fusion.1
  204.9 2.9 collective-permute-done.5.refs_8_
  208.3 1.5 collective-permute-start.11
  209.8 0.8 copy-done.9
  210.6 1.5 collective-permute-start.6
  212.6 1.5 collective-permute-start.8
  214.1 29.7 %shard_map.110 = (bf16[6656,512]{1,0:T(8,128)(2,1)}, f32[6656,128]{1,0:T(8,128)}, f32[3,128,1280]{2,1,0:T(8,128)}, f32[3,128,1280]{2,1,0:T(8,128)}, f32[3,128,1280]{2,1,0:T(8,128)}, /*index=5*/f32[3,128,1280]{2,1,0:T(8,128)}) custom-call(s32[3]{0:T(128)} %add_add_fusion.info, bf16[26624,512]{1,0:T(8,128)(2,1)} %gather_x.1.x_ref, ...), custom_call_target="tpu_custom_call" | custom-call | flops 35389440000 | bytes 15728640 | tf_op jit(solution)/shard_map/pallas_call | solution.py:247
  243.8 1.5 collective-permute-start.21
  245.9 9.0 collective-permute-done.6.refs_3_
  254.9 2.1 collective-permute-start.23
  257.0 56.9 %collective-permute-done.7.refs_4_ = bf16[3,2,128,1280]{3,2,1,0:T(8,128)(2,1)} collective-permute-done((bf16[3,2,128,1280]{3,2,1,0:T(8,128)(2,1)}, bf16[3,2,128,1280]{3,2,1,0:T(8,128)(2,1)}, u32[]{:S(2)}, u32[]{:S(2)}) %collective-permute-start.7) | collective-permute-done | bytes 1966112 | tf_op jit(solution)/shard_map/ppermute | solution.py:667
  313.9 29.9 %shard_map.112 = (bf16[6656,512]{1,0:T(8,128)(2,1)}, f32[6656,128]{1,0:T(8,128)}, f32[3,128,1280]{2,1,0:T(8,128)}, f32[3,128,1280]{2,1,0:T(8,128)}, f32[3,128,1280]{2,1,0:T(8,128)}, /*index=5*/f32[3,128,1280]{2,1,0:T(8,128)}) custom-call(s32[3]{0:T(128)} %get-tuple-element.128.info, bf16[26624,512]{1,0:T(8,128)(2,1)} %gather_x.1.x_ref, ...), custom_call_target="tpu_custom_call" | custom-call | flops 35389440000 | bytes 15728640 | tf_op jit(solution)/shard_map/pallas_call | solution.py:247
  343.9 29.6 %shard_map.111 = (bf16[6656,512]{1,0:T(8,128)(2,1)}, f32[6656,128]{1,0:T(8,128)}, f32[3,128,1280]{2,1,0:T(8,128)}, f32[3,128,1280]{2,1,0:T(8,128)}, f32[3,128,1280]{2,1,0:T(8,128)}, /*index=5*/f32[3,128,1280]{2,1,0:T(8,128)}) custom-call(s32[3]{0:T(128)} %get-tuple-element.127.info, bf16[26624,512]{1,0:T(8,128)(2,1)} %gather_x.1.x_ref, ...), custom_call_target="tpu_custom_call" | custom-call | flops 35389440000 | bytes 15728640 | tf_op jit(solution)/shard_map/pallas_call | solution.py:247
  373.5 2.0 collective-permute-start.18
  375.5 22.6 %collective-permute-done.22.refs_2_ = f32[3,128,1280]{2,1,0:T(8,128)} collective-permute-done((f32[3,128,1280]{2,1,0:T(8,128)}, f32[3,128,1280]{2,1,0:T(8,128)}, u32[]{:S(2)}, u32[]{:S(2)}) %collective-permute-start.22) | collective-permute-done | bytes 1966112 | tf_op jit(solution)/shard_map/ppermute | solution.py:689
  398.1 29.7 %shard_map.113 = (bf16[6656,512]{1,0:T(8,128)(2,1)}, f32[6656,128]{1,0:T(8,128)}, f32[3,128,1280]{2,1,0:T(8,128)}, f32[3,128,1280]{2,1,0:T(8,128)}, f32[3,128,1280]{2,1,0:T(8,128)}, /*index=5*/f32[3,128,1280]{2,1,0:T(8,128)}) custom-call(s32[3]{0:T(128)} %add_add_fusion.3.info, bf16[26624,512]{1,0:T(8,128)(2,1)} %gather_x.1.x_ref, ...), custom_call_target="tpu_custom_call" | custom-call | flops 35389440000 | bytes 15728640 | tf_op jit(solution)/shard_map/pallas_call | solution.py:247
  427.9 3.0 collective-permute-start.17
  430.8 16.5 %collective-permute-done.18.refs_1_ = f32[3,128,1280]{2,1,0:T(8,128)} collective-permute-done((f32[3,128,1280]{2,1,0:T(8,128)}, f32[3,128,1280]{2,1,0:T(8,128)}, u32[]{:S(2)}, u32[]{:S(2)}) %collective-permute-start.18) | collective-permute-done | bytes 1966112 | tf_op jit(solution)/shard_map/ppermute | solution.py:689
  447.3 1.7 collective-permute-start.12
  449.0 19.8 %collective-permute-start.13 = (f32[3,128,1280]{2,1,0:T(8,128)}, f32[3,128,1280]{2,1,0:T(8,128)}, u32[]{:S(2)}, u32[]{:S(2)}) collective-permute-start(f32[3,128,1280]{2,1,0:T(8,128)} %get-tuple-element.91), channel_id=1, source_target_pairs={{0,8},{4,12},{8,0},{12,4},{1,9},{5,13},{9,1},{13,5},{2,10},{6,14},... | collective-permute-start | bytes 5898248 | tf_op jit(solution)/shard_map/ppermute | solution.py:689
  468.8 21.9 %collective-permute-done.20.refs_3_ = f32[3,128,1280]{2,1,0:T(8,128)} collective-permute-done((f32[3,128,1280]{2,1,0:T(8,128)}, f32[3,128,1280]{2,1,0:T(8,128)}, u32[]{:S(2)}, u32[]{:S(2)}) %collective-permute-start.20) | collective-permute-done | bytes 1966112 | tf_op jit(solution)/shard_map/ppermute | solution.py:689
  490.7 28.2 %combine.1 = (f32[16384,512]{1,0:T(8,128)}, f32[16,4,1024]{2,1,0:T(4,128)}) custom-call(s32[64]{0:T(128)} %add.54.refs_0_.cnt, s32[64]{0:T(128)} %fusion.8.refs_1_.off, s32[16,4,1024]{2,1,0:T(4,128)} %fusion.2.refs_2_.pos_ref, bf16[6656,512]{1,0:T(8,128)(2,1)} %get-tuple-element.71.refs_0_, bf16[6656,512]{1,0:T(8,128)(2,1)} %get-tuple-element.78.refs_1_, ...), custom_call_target="tpu_custom_call" | custom-call | flops 12582912000 | bytes 33554432 | tf_op jit(solution)/shard_map/combine/pallas_call | solution.py:378
  518.9 361.6 %collect.1 = (bf16[1024,512]{1,0:T(8,128)(2,1)}, f32[16,4,1024]{2,1,0:T(4,128)}) custom-call(f32[16384,512]{1,0:T(8,128)} %get-tuple-element.85.part_ref, f32[16,4,1024]{2,1,0:T(4,128)} %get-tuple-element.86.dr_ref), custom_call_target="tpu_custom_call" | custom-call | bytes 67108864 | tf_op jit(solution)/shard_map/collect/pallas_call | solution.py:631
  880.5 1.0 copy.42
  881.6 0.9 select_reduce_fusion
  882.5 6.4 shard_map.114
  889.0 6.5 shard_map.115
  895.5 6.5 shard_map.116
  902.0 1.2 copy-done.1
  903.2 6.5 shard_map.117
  909.8 1.0 copy.53
  (68 shorter events, 6.3 us)
Async XLA Ops:
  0.6 1.6 copy-start.3
  0.6 1.6 copy-start.5
  135.6 31.8 %collective-permute-start.3 = (bf16[1,1280,128]{2,1,0:T(8,128)(2,1)}, bf16[1,1280,128]{2,1,0:T(8,128)(2,1)S(1)}, u32[]{:S(2)}, u32[]{:S(2)}) collective-permute-start(bf16[1,1280,128]{2,1,0:T(8,128)(2,1)} %get-tuple-element.68), channel_id=1, source_target_pairs={{0,4},{4,0},{8,12},{12,8},{1,5},{5,1},{9,13},{13,9},{2,6},{6,2},{1... | collective-permute-start | bytes 983048 | tf_op jit(solution)/shard_map/ppermute | solution.py:667
  136.2 63.5 %collective-permute-start.4 = (bf16[1,1280,128]{2,1,0:T(8,128)(2,1)}, bf16[1,1280,128]{2,1,0:T(8,128)(2,1)S(1)}, u32[]{:S(2)}, u32[]{:S(2)}) collective-permute-start(bf16[1,1280,128]{2,1,0:T(8,128)(2,1)} %get-tuple-element.69), channel_id=1, source_target_pairs={{0,8},{4,12},{8,0},{12,4},{1,9},{5,13},{9,1},{13,5},{2,10},{6,14},... | collective-permute-start | bytes 983048 | tf_op jit(solution)/shard_map/ppermute | solution.py:667
  137.7 70.6 %collective-permute-start = (bf16[1,2,128,1280]{3,2,1,0:T(8,128)(2,1)}, bf16[1,2,128,1280]{3,2,1,0:T(8,128)(2,1)S(1)}, u32[]{:S(2)}, u32[]{:S(2)}) collective-permute-start(bf16[1,2,128,1280]{3,2,1,0:T(8,128)(2,1)} %get-tuple-element.65), channel_id=1, source_target_pairs={{0,4},{4,0},{8,12},{12,8},{1,5},{5,1},{9,13},{13,9},{2,6},{6,2},{1... | collective-permute-start | bytes 1966088 | tf_op jit(solution)/shard_map/ppermute | solution.py:667
  139.1 70.6 %collective-permute-start.1 = (bf16[1,2,128,1280]{3,2,1,0:T(8,128)(2,1)}, bf16[1,2,128,1280]{3,2,1,0:T(8,128)(2,1)S(1)}, u32[]{:S(2)}, u32[]{:S(2)}) collective-permute-start(bf16[1,2,128,1280]{3,2,1,0:T(8,128)(2,1)} %get-tuple-element.66), channel_id=1, source_target_pairs={{0,8},{4,12},{8,0},{12,4},{1,9},{5,13},{9,1},{13,5},{2,10},{6,14},... | collective-permute-start | bytes 1966088 | tf_op jit(solution)/shard_map/ppermute | solution.py:667
  139.7 72.4 %collective-permute-start.2 = (bf16[1,2,128,1280]{3,2,1,0:T(8,128)(2,1)}, bf16[1,2,128,1280]{3,2,1,0:T(8,128)(2,1)}, u32[]{:S(2)}, u32[]{:S(2)}) collective-permute-start(bf16[1,2,128,1280]{3,2,1,0:T(8,128)(2,1)} %get-tuple-element.67), channel_id=1, source_target_pairs={{0,12},{4,8},{8,4},{12,0},{1,13},{5,9},{9,5},{13,1},{2,14},{6,10},... | collective-permute-start | bytes 1966088 | tf_op jit(solution)/shard_map/ppermute | solution.py:667
  167.4 0.7 copy-start.10
  168.2 44.5 %collective-permute-start.9 = (bf16[3,1280,128]{2,1,0:T(8,128)(2,1)}, bf16[3,1280,128]{2,1,0:T(8,128)(2,1)S(1)}, u32[]{:S(2)}, u32[]{:S(2)}) collective-permute-start(bf16[3,1280,128]{2,1,0:T(8,128)(2,1)} %get-tuple-element.75), channel_id=1, source_target_pairs={{0,4},{4,0},{8,12},{12,8},{1,5},{5,1},{9,13},{13,9},{2,6},{6,2},{1... | collective-permute-start | bytes 2949128 | tf_op jit(solution)/shard_map/ppermute | solution.py:667
  169.6 30.1 %copy-start.12 = (bf16[1,1280,128]{2,1,0:T(8,128)(2,1)S(1)}, bf16[1,1280,128]{2,1,0:T(8,128)(2,1)}, u32[]{:S(2)}) copy-start(bf16[1,1280,128]{2,1,0:T(8,128)(2,1)} %get-tuple-element.70) | copy-start | bytes 983044
  199.7 10.1 %copy-start.11 = (bf16[1,1280,128]{2,1,0:T(8,128)(2,1)}, bf16[1,1280,128]{2,1,0:T(8,128)(2,1)S(1)}, u32[]{:S(2)}) copy-start(bf16[1,1280,128]{2,1,0:T(8,128)(2,1)S(1)} %collective-permute-done.4.refs_7_) | copy-start | bytes 983044
  199.7 8.0 collective-permute-start.5
  207.7 6.4 copy-start.13
  207.7 36.1 %collective-permute-start.10 = (bf16[3,1280,128]{2,1,0:T(8,128)(2,1)}, bf16[3,1280,128]{2,1,0:T(8,128)(2,1)}, u32[]{:S(2)}, u32[]{:S(2)}) collective-permute-start(bf16[3,1280,128]{2,1,0:T(8,128)(2,1)} %get-tuple-element.76), channel_id=1, source_target_pairs={{0,8},{4,12},{8,0},{12,4},{1,9},{5,13},{9,1},{13,5},{2,10},{6,14},... | collective-permute-start | bytes 2949128 | tf_op jit(solution)/shard_map/ppermute | solution.py:667
  208.3 1.5 copy-start.8
  208.3 37.1 %collective-permute-start.11 = (bf16[3,1280,128]{2,1,0:T(8,128)(2,1)}, bf16[3,1280,128]{2,1,0:T(8,128)(2,1)}, u32[]{:S(2)}, u32[]{:S(2)}) collective-permute-start(bf16[3,1280,128]{2,1,0:T(8,128)(2,1)} %get-tuple-element.77), channel_id=1, source_target_pairs={{0,12},{4,8},{8,4},{12,0},{1,13},{5,9},{9,5},{13,1},{2,14},{6,10},... | collective-permute-start | bytes 2949128 | tf_op jit(solution)/shard_map/ppermute | solution.py:667
  209.8 0.8 copy-start.9
  210.6 44.3 %collective-permute-start.6 = (bf16[3,2,128,1280]{3,2,1,0:T(8,128)(2,1)}, bf16[3,2,128,1280]{3,2,1,0:T(8,128)(2,1)S(1)}, u32[]{:S(2)}, u32[]{:S(2)}) collective-permute-start(bf16[3,2,128,1280]{3,2,1,0:T(8,128)(2,1)} %get-tuple-element.72), channel_id=1, source_target_pairs={{0,4},{4,0},{8,12},{12,8},{1,5},{5,1},{9,13},{13,9},{2,6},{6,2},{1... | collective-permute-start | bytes 5898248 | tf_op jit(solution)/shard_map/ppermute | solution.py:667
  212.1 101.8 %collective-permute-start.7 = (bf16[3,2,128,1280]{3,2,1,0:T(8,128)(2,1)}, bf16[3,2,128,1280]{3,2,1,0:T(8,128)(2,1)}, u32[]{:S(2)}, u32[]{:S(2)}) collective-permute-start(bf16[3,2,128,1280]{3,2,1,0:T(8,128)(2,1)} %get-tuple-element.73), channel_id=1, source_target_pairs={{0,8},{4,12},{8,0},{12,4},{1,9},{5,13},{9,1},{13,5},{2,10},{6,14},... | collective-permute-start | bytes 5898248 | tf_op jit(solution)/shard_map/ppermute | solution.py:667
  212.6 31.2 %copy-start.7 = (bf16[3,1280,128]{2,1,0:T(8,128)(2,1)}, bf16[3,1280,128]{2,1,0:T(8,128)(2,1)S(1)}, u32[]{:S(2)}) copy-start(bf16[3,1280,128]{2,1,0:T(8,128)(2,1)S(1)} %collective-permute-done.9.refs_6_) | copy-start | bytes 2949124
  212.6 101.3 %collective-permute-start.8 = (bf16[3,2,128,1280]{3,2,1,0:T(8,128)(2,1)}, bf16[3,2,128,1280]{3,2,1,0:T(8,128)(2,1)}, u32[]{:S(2)}, u32[]{:S(2)}) collective-permute-start(bf16[3,2,128,1280]{3,2,1,0:T(8,128)(2,1)} %get-tuple-element.74), channel_id=1, source_target_pairs={{0,12},{4,8},{8,4},{12,0},{1,13},{5,9},{9,5},{13,1},{2,14},{6,10},... | collective-permute-start | bytes 5898248 | tf_op jit(solution)/shard_map/ppermute | solution.py:667
  243.8 131.7 %collective-permute-start.21 = (f32[3,128,1280]{2,1,0:T(8,128)}, f32[3,128,1280]{2,1,0:T(8,128)S(1)}, u32[]{:S(2)}, u32[]{:S(2)}) collective-permute-start(f32[3,128,1280]{2,1,0:T(8,128)} %get-tuple-element.102), channel_id=1, source_target_pairs={{0,4},{4,0},{8,12},{12,8},{1,5},{5,1},{9,13},{13,9},{2,6},{6,2},{1... | collective-permute-start | bytes 5898248 | tf_op jit(solution)/shard_map/ppermute | solution.py:689
  245.4 152.8 %collective-permute-start.22 = (f32[3,128,1280]{2,1,0:T(8,128)}, f32[3,128,1280]{2,1,0:T(8,128)}, u32[]{:S(2)}, u32[]{:S(2)}) collective-permute-start(f32[3,128,1280]{2,1,0:T(8,128)} %get-tuple-element.103), channel_id=1, source_target_pairs={{0,8},{4,12},{8,0},{12,4},{1,9},{5,13},{9,1},{13,5},{2,10},{6,14},... | collective-permute-start | bytes 5898248 | tf_op jit(solution)/shard_map/ppermute | solution.py:689
  254.9 59.0 %copy-start.6 = (bf16[3,2,128,1280]{3,2,1,0:T(8,128)(2,1)}, bf16[3,2,128,1280]{3,2,1,0:T(8,128)(2,1)S(1)}, u32[]{:S(2)}) copy-start(bf16[3,2,128,1280]{3,2,1,0:T(8,128)(2,1)S(1)} %collective-permute-done.6.refs_3_) | copy-start | bytes 5898244
  254.9 172.9 %collective-permute-start.23 = (f32[3,128,1280]{2,1,0:T(8,128)}, f32[3,128,1280]{2,1,0:T(8,128)}, u32[]{:S(2)}, u32[]{:S(2)}) collective-permute-start(f32[3,128,1280]{2,1,0:T(8,128)} %get-tuple-element.104), channel_id=1, source_target_pairs={{0,12},{4,8},{8,4},{12,0},{1,13},{5,9},{9,5},{13,1},{2,14},{6,10},... | collective-permute-start | bytes 5898248 | tf_op jit(solution)/shard_map/ppermute | solution.py:689
  343.8 84.1 %collective-permute-start.15 = (f32[3,128,1280]{2,1,0:T(8,128)}, f32[3,128,1280]{2,1,0:T(8,128)}, u32[]{:S(2)}, u32[]{:S(2)}) collective-permute-start(f32[3,128,1280]{2,1,0:T(8,128)} %get-tuple-element.94), channel_id=1, source_target_pairs={{0,4},{4,0},{8,12},{12,8},{1,5},{5,1},{9,13},{13,9},{2,6},{6,2},{1... | collective-permute-start | bytes 5898248 | tf_op jit(solution)/shard_map/ppermute | solution.py:689
  373.5 73.8 %collective-permute-start.18 = (f32[3,128,1280]{2,1,0:T(8,128)}, f32[3,128,1280]{2,1,0:T(8,128)}, u32[]{:S(2)}, u32[]{:S(2)}) collective-permute-start(f32[3,128,1280]{2,1,0:T(8,128)} %get-tuple-element.98), channel_id=1, source_target_pairs={{0,4},{4,0},{8,12},{12,8},{1,5},{5,1},{9,13},{13,9},{2,6},{6,2},{1... | collective-permute-start | bytes 5898248 | tf_op jit(solution)/shard_map/ppermute | solution.py:689
  375.5 52.3 %copy-start = (f32[3,128,1280]{2,1,0:T(8,128)}, f32[3,128,1280]{2,1,0:T(8,128)S(1)}, u32[]{:S(2)}) copy-start(f32[3,128,1280]{2,1,0:T(8,128)S(1)} %collective-permute-done.21.refs_1_) | copy-start | bytes 5898244
  375.5 73.5 %collective-permute-start.19 = (f32[3,128,1280]{2,1,0:T(8,128)}, f32[3,128,1280]{2,1,0:T(8,128)}, u32[]{:S(2)}, u32[]{:S(2)}) collective-permute-start(f32[3,128,1280]{2,1,0:T(8,128)} %get-tuple-element.99), channel_id=1, source_target_pairs={{0,8},{4,12},{8,0},{12,4},{1,9},{5,13},{9,1},{13,5},{2,10},{6,14},... | collective-permute-start | bytes 5898248 | tf_op jit(solution)/shard_map/ppermute | solution.py:689
  398.1 92.5 %collective-permute-start.20 = (f32[3,128,1280]{2,1,0:T(8,128)}, f32[3,128,1280]{2,1,0:T(8,128)}, u32[]{:S(2)}, u32[]{:S(2)}) collective-permute-start(f32[3,128,1280]{2,1,0:T(8,128)} %get-tuple-element.100), channel_id=1, source_target_pairs={{0,12},{4,8},{8,4},{12,0},{1,13},{5,9},{9,5},{13,1},{2,14},{6,10},... | collective-permute-start | bytes 5898248 | tf_op jit(solution)/shard_map/ppermute | solution.py:689
  427.8 467.6 %collective-permute-start.16 = (f32[3,128,1280]{2,1,0:T(8,128)}, f32[3,128,1280]{2,1,0:T(8,128)}, u32[]{:S(2)}, u32[]{:S(2)}) collective-permute-start(f32[3,128,1280]{2,1,0:T(8,128)} %get-tuple-element.95), channel_id=1, source_target_pairs={{0,8},{4,12},{8,0},{12,4},{1,9},{5,13},{9,1},{13,5},{2,10},{6,14},... | collective-permute-start | bytes 5898248 | tf_op jit(solution)/shard_map/ppermute | solution.py:689
  427.9 467.6 %collective-permute-start.17 = (f32[3,128,1280]{2,1,0:T(8,128)}, f32[3,128,1280]{2,1,0:T(8,128)}, u32[]{:S(2)}, u32[]{:S(2)}) collective-permute-start(f32[3,128,1280]{2,1,0:T(8,128)} %get-tuple-element.96), channel_id=1, source_target_pairs={{0,12},{4,8},{8,4},{12,0},{1,13},{5,9},{9,5},{13,1},{2,14},{6,10},... | collective-permute-start | bytes 5898248 | tf_op jit(solution)/shard_map/ppermute | solution.py:689
  447.3 454.6 %collective-permute-start.12 = (f32[3,128,1280]{2,1,0:T(8,128)}, f32[3,128,1280]{2,1,0:T(8,128)S(1)}, u32[]{:S(2)}, u32[]{:S(2)}) collective-permute-start(f32[3,128,1280]{2,1,0:T(8,128)} %get-tuple-element.90), channel_id=1, source_target_pairs={{0,4},{4,0},{8,12},{12,8},{1,5},{5,1},{9,13},{13,9},{2,6},{6,2},{1... | collective-permute-start | bytes 5898248 | tf_op jit(solution)/shard_map/ppermute | solution.py:689
  449.0 452.9 %collective-permute-start.13 = (f32[3,128,1280]{2,1,0:T(8,128)}, f32[3,128,1280]{2,1,0:T(8,128)}, u32[]{:S(2)}, u32[]{:S(2)}) collective-permute-start(f32[3,128,1280]{2,1,0:T(8,128)} %get-tuple-element.91), channel_id=1, source_target_pairs={{0,8},{4,12},{8,0},{12,4},{1,9},{5,13},{9,1},{13,5},{2,10},{6,14},... | collective-permute-start | bytes 5898248 | tf_op jit(solution)/shard_map/ppermute | solution.py:689
  490.7 411.3 %collective-permute-start.14 = (f32[3,128,1280]{2,1,0:T(8,128)}, f32[3,128,1280]{2,1,0:T(8,128)}, u32[]{:S(2)}, u32[]{:S(2)}) collective-permute-start(f32[3,128,1280]{2,1,0:T(8,128)} %get-tuple-element.92), channel_id=1, source_target_pairs={{0,12},{4,8},{8,4},{12,0},{1,13},{5,9},{9,5},{13,1},{2,14},{6,10},... | collective-permute-start | bytes 5898248 | tf_op jit(solution)/shard_map/ppermute | solution.py:689
  518.9 362.7 %copy-start.4 = (s32[1024,8]{0,1:T(8,128)S(1)}, s32[1024,8]{0,1:T(8,128)}, u32[]{:S(2)}) copy-start(s32[1024,8]{0,1:T(8,128)} %param.9) | copy-start | bytes 98308
  901.9 1.3 copy-start.1
  903.2 6.5 copy-start.2

commit v5 on v4

--- a/solution.py
+++ b/solution.py
@@ -11,8 +11,7 @@
 CAP_FACTOR = 3
 CHUNK = 128
 TILE = 512
-MM = 256
-HEAD = 384
+TIERS = (384, 640, 1024)
 VMEM_LIMIT = 60 * 1024 * 1024
 F32 = jnp.float32
 BF16 = jnp.bfloat16
@@ -54,16 +53,21 @@
     return position, weight
 
 
-def one_hot_block(pos_row, c):
-    row = lax.broadcasted_iota(jnp.int32, (CHUNK, pos_row.shape[1]), 0) + c * CHUNK
-    return row == pos_row
+def one_hot_block(pos_row, first, size):
+    return lax.broadcasted_iota(jnp.int32, (size, pos_row.shape[1]), 0) + first == pos_row
+
+
+def tiers(rows, limit, work):
+    work(0, TIERS[0])
+    for first, last in zip(TIERS, (*TIERS[1:], limit)):
+        pl.when(rows > first)(functools.partial(work, first, last - first))
 
 
 def aligned(v, m=16):
     return pl.multiple_of(v, m)
 
 
-def gather_kernel(n_src, n_loc, region, with_r, *refs):
+def gather_kernel(n_src, n_loc, region, slots, with_r, *refs):
     if with_r:
         (cnt, off, pos_ref, r_ref, src_ref, out, r_out, hot, stage, pool, rstage, rpool, sem) = refs
     else:
@@ -76,43 +80,37 @@
         starts.append(base)
         pos_row = pos_ref[0, k:k + 1, :]
 
-        def build(c, carry=0, base=base, pos_row=pos_row, k=k):
-            m = one_hot_block(pos_row, c)
-            at = pl.ds(aligned(base + c * CHUNK), CHUNK)
+        def build(first, size, base=base, pos_row=pos_row, k=k):
+            m = one_hot_block(pos_row, first, size)
+            at = pl.ds(aligned(base + first), size)
             hot[at, :] = jnp.where(m, 1.0, 0.0).astype(BF16)
             if with_r:
                 r = jnp.sum(jnp.where(m, r_ref[0, k:k + 1, :], 0.0), axis=1, keepdims=True)
-                rstage[at, :] = jnp.broadcast_to(r, (CHUNK, 128))
-            return carry
-
-        build(0)
-        lax.fori_loop(1, blocks(n, CHUNK), build, 0)
+                rstage[at, :] = jnp.broadcast_to(r, (size, 128))
+
+        build(0, CHUNK)
+        pl.when(n > CHUNK)(functools.partial(build, CHUNK, slots - CHUNK))
         base = base + blocks(n, 16) * 16
 
-    head = pl.ds(0, HEAD)
-    stage[head, :] = dot(hot[head, :], src_ref[...]).astype(BF16)
-
-    def mm(c, carry):
-        at = pl.ds(aligned(HEAD + c * MM), MM)
+    def mm(first, size):
+        at = pl.ds(first, size)
         stage[at, :] = dot(hot[at, :], src_ref[...]).astype(BF16)
-        return carry
-
-    lax.fori_loop(0, blocks(jnp.maximum(base - HEAD, 0), MM), mm, 0)
+
+    tiers(base, hot.shape[0], mm)
 
     for k in range(n_loc):
         n = cnt[s * n_loc + k]
         to = off[s * n_loc + k] + k * region
 
-        def move(c, carry=0, start=starts[k], to=to):
-            dst = pl.ds(aligned(to + c * CHUNK), CHUNK)
-            frm = pl.ds(aligned(start + c * CHUNK), CHUNK)
+        def move(first, size, start=starts[k], to=to):
+            dst = pl.ds(aligned(to + first), size)
+            frm = pl.ds(aligned(start + first), size)
             pool[dst, :] = stage[frm, :]
             if with_r:
                 rpool[dst, :] = rstage[frm, :]
-            return carry
-
-        move(0)
-        lax.fori_loop(1, blocks(n, CHUNK), move, 0)
+
+        move(0, CHUNK)
+        pl.when(n > CHUNK)(functools.partial(move, CHUNK, slots - CHUNK))
 
     @pl.when(s == n_src - 1)
     def _():
@@ -152,7 +150,7 @@
     d = src.shape[1] // 2
     with_r = r is not None
     rows = n_loc * region
-    scr = HEAD + up(n_loc * ((region - TILE) // n_src) + CHUNK - HEAD, MM)
+    scr = up(n_loc * ((region - TILE) // n_src) + CHUNK, CHUNK)
     table = pl.BlockSpec((1, n_loc, tok), lambda s, *_: (s, 0, 0))
     in_specs = [table] + ([table] if with_r else []) + [pl.BlockSpec((tok, d), lambda s, *_: (s, 1 if with_r else 0))]
     out_shape = [jax.ShapeDtypeStruct((rows, d), BF16)]
@@ -161,7 +159,7 @@
         out_shape.append(jax.ShapeDtypeStruct((rows, 128), F32))
         scratch += [pltpu.VMEM((scr, 128), F32), pltpu.VMEM((rows, 128), F32)]
     out = pl.pallas_call(
-        functools.partial(gather_kernel, n_src, n_loc, region, with_r),
+        functools.partial(gather_kernel, n_src, n_loc, region, up((region - TILE) // n_src, CHUNK), with_r),
         out_shape=out_shape,
         grid_spec=pltpu.PrefetchScalarGridSpec(
             num_scalar_prefetch=2, grid=(n_src,), in_specs=in_specs,
@@ -175,9 +173,9 @@
 
 
 def expert_kernel(n_fs, info, x_ref, dy_ref, r_ref, *refs):
-    own, gu_refs, down_refs, refs = refs[:3], refs[3:n_fs + 2], refs[n_fs + 2:2 * n_fs + 1], refs[2 * n_fs + 1:]
+    own, peers, refs = refs[:3], refs[3:n_fs + 2], refs[n_fs + 2:]
     (dx_ref, dr_ref), outs, refs = refs[:2], refs[2:n_fs + 2], refs[n_fs + 2:]
-    w1_ref, w3_ref, w2, a_buf, dh1_buf, dh3_buf, dw1, dw3, dw2t = refs
+    w1_ref, w3_ref, w2t, a_buf, dh1_buf, dh3_buf, dw1, dw3, dw2t = refs
     i = pl.program_id(0)
     d, f = w1_ref.shape
     dsl = d // n_fs
@@ -189,9 +187,8 @@
         dw2t[...] = jnp.zeros_like(dw2t)
         for m in range(n_fs):
             at = pl.ds(aligned((info[2] ^ m) * dsl, dsl), dsl)
-            w1_ref[at, :] = gu_refs[m - 1][0, 0] if m else own[0][0]
-            w3_ref[at, :] = gu_refs[m - 1][0, 1] if m else own[1][0]
-            w2[:, at] = down_refs[m - 1][0] if m else own[2][0]
+            for t, whole in enumerate((w1_ref, w3_ref, w2t)):
+                whole[at, :] = peers[m - 1][0, t] if m else own[t][0]
 
     def tile(m):
         x, dy = x_ref[:m, :], dy_ref[:m, :]
@@ -202,13 +199,13 @@
             cs = slice(c, c + step)
             h1 = dot(x, w1_ref[:, cs])
             h3 = dot(x, w3_ref[:, cs])
-            da = dot_nt(g, w2[cs, :])
+            da = dot(g, w2t[:, cs])
             s = jax.nn.sigmoid(h1)
             hs = h1 * s
             a_buf[:m, cs] = (hs * h3).astype(BF16)
             dh1_buf[:m, cs] = (da * h3 * s * (1.0 + h1 * (1.0 - s))).astype(BF16)
             dh3_buf[:m, cs] = (da * hs).astype(BF16)
-        y = dot(a_buf[:m, :], w2[...])
+        y = dot_nt(a_buf[:m, :], w2t[...])
         dr = jnp.sum(dy_wide * y, axis=1, keepdims=True)
         dr_ref[:m, :] = jnp.broadcast_to(dr, (m, 128))
         dx_ref[:m, :] = (dot_nt(dh1_buf[:m, :], w1_ref[...]) + dot_nt(dh3_buf[:m, :], w3_ref[...])).astype(BF16)
@@ -236,8 +233,8 @@
                 outs[m][t] = acc[at, :]
 
 
-def expert_call(k, group_at, n_loc, info, x_pool, dy_pool, r_pool, own, gate_up, down, region):
-    n_fs, (_, f, dsl) = len(down) + 1, down[0].shape
+def expert_call(k, group_at, n_loc, info, x_pool, dy_pool, r_pool, own, peers, region):
+    n_fs, (_, _, dsl, f) = len(peers) + 1, peers[0].shape
     d = n_fs * dsl
     first = k * (region // TILE)
     row_map = lambda i, info: (first + jnp.minimum(i, info[1] - 1), 0)
@@ -251,15 +248,14 @@
         grid_spec=pltpu.PrefetchScalarGridSpec(
             num_scalar_prefetch=1, grid=(region // TILE - 1,),
             in_specs=[pl.BlockSpec((TILE, d), row_map), pl.BlockSpec((TILE, d), row_map), pl.BlockSpec((TILE, 128), row_map),
-                      *[pl.BlockSpec((1, dsl, f), mine)] * 2, pl.BlockSpec((1, f, dsl), mine),
-                      *[pl.BlockSpec((1, 2, dsl, f), lambda i, info: (group_at, 0, 0, 0))] * (n_fs - 1),
-                      *[pl.BlockSpec((1, f, dsl), lambda i, info: (group_at, 0, 0))] * (n_fs - 1)],
+                      *[pl.BlockSpec((1, dsl, f), mine)] * 2, pl.BlockSpec((1, dsl, f), lambda i, info: (k, 0, 0)),
+                      *[pl.BlockSpec((1, 3, dsl, f), lambda i, info: (group_at, 0, 0, 0))] * (n_fs - 1)],
             out_specs=[pl.BlockSpec((TILE, d), out_map), pl.BlockSpec((TILE, 128), out_map)]
             + [pl.BlockSpec((3, dsl, f), whole3)] * n_fs,
-            scratch_shapes=[pltpu.VMEM((d, f), BF16)] * 2 + [pltpu.VMEM((f, d), BF16)] + [pltpu.VMEM((TILE, f), BF16)] * 3 + [pltpu.VMEM((d, f), F32)] * 3),
+            scratch_shapes=[pltpu.VMEM((d, f), BF16)] * 3 + [pltpu.VMEM((TILE, f), BF16)] * 3 + [pltpu.VMEM((d, f), F32)] * 3),
         compiler_params=pltpu.CompilerParams(vmem_limit_bytes=VMEM_LIMIT, dimension_semantics=("arbitrary",)),
         cost_estimate=pl.CostEstimate(flops=18 * 3000 * d * f, bytes_accessed=24 * d * f, transcendentals=3000 * f),
-    )(info, x_pool, dy_pool, r_pool, *own, *gate_up, *down)
+    )(info, x_pool, dy_pool, r_pool, *own, *peers)
 
 
 def place_kernel(n_fs, n_loc, k, first, me, *refs):
@@ -299,7 +295,7 @@
     )(me, *pieces, *([] if first else grads))
 
 
-def combine_kernel(n_src, n_loc, cnt, off, pos_ref, *refs):
+def combine_kernel(n_src, n_loc, slots, cnt, off, pos_ref, *refs):
     dx_in, dr_in = refs[:n_loc], refs[n_loc:2 * n_loc]
     out, dr_out, hot, stage, pool, rpool, sem = refs[2 * n_loc:]
     s = pl.program_id(0)
@@ -325,9 +321,9 @@
                 return carry
 
             lax.fori_loop(0, tiles[k], start, 0)
-            at = pl.ds(aligned(tiles[k] * TILE), CHUNK)
-            pool[k, at, :] = jnp.zeros((CHUNK, d), BF16)
-            rpool[k, at, :] = jnp.zeros((CHUNK, 128), F32)
+            at = pl.ds(aligned(tiles[k] * TILE), TILE)
+            pool[k, at, :] = jnp.zeros((TILE, d), BF16)
+            rpool[k, at, :] = jnp.zeros((TILE, 128), F32)
         for k in range(n_loc):
             def wait(i, carry, k=k):
                 for copy in copies(k, i):
@@ -343,40 +339,43 @@
         frm = off[s * n_loc + k]
         pos_row = pos_ref[0, k:k + 1, :]
 
-        def build(c, carry=0, base=base, frm=frm, pos_row=pos_row, k=k):
-            m = one_hot_block(pos_row, c)
-            at = pl.ds(aligned(base + c * CHUNK), CHUNK)
-            src = pl.ds(aligned(frm + c * CHUNK), CHUNK)
+        def build(first, size, base=base, frm=frm, pos_row=pos_row, k=k):
+            m = one_hot_block(pos_row, first, size)
+            at = pl.ds(aligned(base + first), size)
+            src = pl.ds(aligned(frm + first), size)
             hot[at, :] = jnp.where(m, 1.0, 0.0).astype(BF16)
             stage[at, :] = pool[k, src, :]
             r = jnp.concatenate([rpool[k, src, :]] * (tok // 128), axis=1)
             dr_out[0, k:k + 1, :] += jnp.sum(jnp.where(m, r, 0.0), axis=0, keepdims=True)
-            return carry
-
-        build(0)
-        lax.fori_loop(1, blocks(n, CHUNK), build, 0)
+
+        build(0, CHUNK)
+        pl.when(n > CHUNK)(functools.partial(build, CHUNK, slots - CHUNK))
         base = base + blocks(n, 16) * 16
-    tail = pl.ds(aligned(base), HEAD)
-    hot[tail, :] = jnp.zeros((HEAD, tok), BF16)
-    stage[tail, :] = jnp.zeros((HEAD, d), BF16)
-    head = pl.ds(0, HEAD)
-    out[...] = dot_tn(hot[head, :], stage[head, :])
-
-    def mm(c, carry):
-        at = pl.ds(aligned(HEAD + c * MM), MM)
-        out[...] += dot_tn(hot[at, :], stage[at, :])
-        return carry
-
-    lax.fori_loop(0, blocks(jnp.maximum(base - HEAD, 0), MM), mm, 0)
+
+    def clear(size):
+        tail = pl.ds(aligned(base), size)
+        hot[tail, :] = jnp.zeros((size, tok), BF16)
+        stage[tail, :] = jnp.zeros((size, d), BF16)
+
+    clear(TIERS[0])
+    pl.when(base > TIERS[1])(functools.partial(clear, hot.shape[0] - n_loc * slots))
+
+    def mm(first, size):
+        at = pl.ds(first, size)
+        part = dot_tn(hot[at, :], stage[at, :])
+        out[...] = part if first == 0 else out[...] + part
+
+    tiers(base, n_loc * slots, mm)
 
 
 def combine_rows(cnt, off, pos, dx_pools, dr_pools, region):
     n_src, n_loc, tok = pos.shape
     d = dx_pools[0].shape[1]
-    scr = n_loc * ((region - TILE) // n_src) + HEAD
+    slots = up((region - TILE) // n_src, CHUNK)
+    scr = n_loc * slots + TILE
     hbm = pl.BlockSpec(memory_space=pl.ANY)
     return pl.pallas_call(
-        functools.partial(combine_kernel, n_src, n_loc),
+        functools.partial(combine_kernel, n_src, n_loc, slots),
         out_shape=[jax.ShapeDtypeStruct((n_src * tok, d), F32), jax.ShapeDtypeStruct((n_src, n_loc, tok), F32)],
         grid_spec=pltpu.PrefetchScalarGridSpec(
             num_scalar_prefetch=2, grid=(n_src,),
@@ -396,7 +395,6 @@
 HOPS = ((0, 2), (1, 0), (2, 0))
 SIBLING = (0, 1)
 ORDERS = ((0, 1, 2), (1, 2, 0), (2, 0, 1))
-COLLECT_ORDERS = ((0, 1, 2), (0, 2, 1))
 
 
 def here():
@@ -440,9 +438,9 @@
 
 
 def spread_kernel(n_fs, n_ep, n_loc, parts, x_ref, dy_ref, table_ref, wg_ref, wu_ref, wd_ref, full, table_all, *refs):
-    n_slices, n_out = n_loc * (n_fs - 1), 2 * (n_fs - 1)
-    gu_out, down_out, refs = refs[:n_out], refs[n_out:2 * n_out], refs[2 * n_out:]
-    own, send, recv, c_send, c_recv, t_send, t_recv, own_sem, gu_buf, down_buf, in_sem, out_sem = refs
+    n_out = 2 * (n_fs - 1)
+    own_down, w_out, refs = refs[0], refs[1:n_out + 1], refs[n_out + 1:]
+    own, send, recv, c_send, c_recv, t_send, t_recv, own_sem, w_buf, down_buf, in_sem, out_sem = refs
     tok, d = x_ref.shape
     mine = block_of(0)
     local = []
@@ -491,23 +489,27 @@
     f, _ = here()
     packs = []
     for k in range(n_loc):
-        for m in range(1, n_fs):
-            n = k * (n_fs - 1) + m - 1
+        for m in range(n_fs):
+            n = k * n_fs + m
             at = (f ^ m) * n_loc + k
-            packs.append([pltpu.make_async_copy(wg_ref.at[at], gu_buf.at[n, 0], in_sem.at[3 * n]),
-                          pltpu.make_async_copy(wu_ref.at[at], gu_buf.at[n, 1], in_sem.at[3 * n + 1]),
-                          pltpu.make_async_copy(wd_ref.at[at], down_buf.at[n], in_sem.at[3 * n + 2])])
+            packs.append([pltpu.make_async_copy(wd_ref.at[at], down_buf.at[n], in_sem.at[3 * n])])
+            if m:
+                packs[-1] += [pltpu.make_async_copy(w.at[at], w_buf.at[n, t], in_sem.at[3 * n + 1 + t])
+                              for t, w in enumerate((wg_ref, wu_ref))]
             for copy in packs[-1]:
                 copy.start()
-    for n in range(n_slices):
+    for n in range(n_loc * n_fs):
         for copy in packs[n]:
             copy.wait()
-        k, m = n // (n_fs - 1), n % (n_fs - 1)
-        to, at = (m, 0) if k == 0 else (n_fs - 1 + m, k - 1)
-        for copy in (pltpu.make_async_copy(gu_buf.at[n], gu_out[to].at[at], out_sem.at[2 * n]),
-                     pltpu.make_async_copy(down_buf.at[n], down_out[to].at[at], out_sem.at[2 * n + 1])):
-            copy.start()
-            local.append(copy)
+        w_buf[n, 2] = down_buf[n].T
+        k, m = n // n_fs, n % n_fs
+        if m == 0:
+            copy = pltpu.make_async_copy(w_buf.at[n, 2], own_down.at[k], out_sem.at[n])
+        else:
+            to, at = (m - 1, 0) if k == 0 else (n_fs + m - 2, k - 1)
+            copy = pltpu.make_async_copy(w_buf.at[n], w_out[to].at[at], out_sem.at[n])
+        copy.start()
+        local.append(copy)
     for phase in range(3):
         for q in range(3):
             held = [0]
@@ -534,7 +536,7 @@
     tok, d = x_tok.shape
     exp_local, dsl, f = w_gate.shape
     n_loc = exp_local // n_fs
-    n_slices, groups = n_loc * (n_fs - 1), [1] * (n_fs - 1) + [n_loc - 1] * (n_fs - 1)
+    n_slices, groups = n_loc * n_fs, [1] * (n_fs - 1) + [n_loc - 1] * (n_fs - 1)
     third = tok // 3 // 16 * 16
     parts = (tok - 2 * third, third, third)
     vmem, hbm = pl.BlockSpec(memory_space=pltpu.VMEM), pl.BlockSpec(memory_space=pl.ANY)
@@ -542,11 +544,11 @@
     return pl.pallas_call(
         functools.partial(spread_kernel, n_fs, n_ep, n_loc, parts),
         out_shape=[jax.ShapeDtypeStruct((n_dev * tok, 2 * d), x_tok.dtype), jax.ShapeDtypeStruct(table.shape, table.dtype)]
-        + [jax.ShapeDtypeStruct((g, 2, dsl, f), BF16) for g in groups] + [jax.ShapeDtypeStruct((g, f, dsl), BF16) for g in groups],
-        in_specs=[hbm] * 2 + [vmem] + [hbm] * 3, out_specs=[hbm] * (2 + 2 * len(groups)),
+        + [jax.ShapeDtypeStruct((n_loc, dsl, f), BF16)] + [jax.ShapeDtypeStruct((g, 3, dsl, f), BF16) for g in groups],
+        in_specs=[hbm] * 2 + [vmem] + [hbm] * 3, out_specs=[hbm] * (3 + len(groups)),
         scratch_shapes=[pltpu.VMEM((tok, 2 * d), BF16), dma((21,)), dma((21,)), dma((24,)), dma((24,)), dma((n_dev,)), dma((n_dev,)),
-                        dma((3,)), pltpu.VMEM((n_slices, 2, dsl, f), BF16), pltpu.VMEM((n_slices, f, dsl), BF16),
-                        dma((3 * n_slices,)), dma((2 * n_slices,))],
+                        dma((3,)), pltpu.VMEM((n_slices, 3, dsl, f), BF16), pltpu.VMEM((n_slices, f, dsl), BF16),
+                        dma((3 * n_slices,)), dma((n_slices,))],
         compiler_params=pltpu.CompilerParams(collective_id=0, has_side_effects=True, vmem_limit_bytes=VMEM_LIMIT),
         cost_estimate=pl.CostEstimate(flops=0, bytes_accessed=8 * n_dev * tok * d, transcendentals=0),
         name="spread",
@@ -561,7 +563,7 @@
     drs = exchange(n_fs, n_ep, dr_ref, dr_home, t_send, t_recv)
     local_dr = pltpu.make_async_copy(dr_ref.at[mine], dr_home.at[mine], own_sem.at[8])
     local_dr.start()
-    order = (7, 3, 5, 1, 6, 2, 4, 0)
+    order = (7, 3, 5, 6, 1, 2, 4, 0)
     loads, shares = {}, {}
     for bits in order:
         theirs = pl.ds(aligned(block_of(bits, 1) * tok, tok), tok)
@@ -577,18 +579,18 @@
     hops = {}
 
     def phase_of(q, bits):
-        return next(n for n in range(3) if bits >> COLLECT_ORDERS[q][n] & 1)
+        return next(n for n in range(3) if bits >> ORDERS[q][n] & 1)
 
     def send_off(q, bits):
         n = slots.index((q, bits))
         rows = pl.ds(starts[q], parts[q])
         hops[(q, bits)] = pltpu.make_async_remote_copy(
             src_ref=acc.at[bits, rows], dst_ref=got.at[bits - 1, rows], send_sem=send.at[n], recv_sem=recv.at[n],
-            device_id=peer_of(HOPS[COLLECT_ORDERS[q][phase_of(q, bits)]]), device_id_type=MESH)
+            device_id=peer_of(HOPS[ORDERS[q][phase_of(q, bits)]]), device_id_type=MESH)
         hops[(q, bits)].start()
 
     def add_arrival(q, bits, phase):
-        frm = bits | 1 << COLLECT_ORDERS[q][phase]
+        frm = bits | 1 << ORDERS[q][phase]
         hops[(q, frm)].wait_recv()
         rows = slice(starts[q], starts[q] + parts[q])
         acc[bits, rows, :] = acc[bits, rows, :] + got[frm - 1, rows, :]
@@ -624,8 +626,8 @@
 def collect(dx_part, dr_part, n_fs, n_ep):
     n_dev = n_fs * n_ep
     tok, d = dx_part.shape[0] // n_dev, dx_part.shape[1]
-    half = tok // 2 // 8 * 8
-    parts = (tok - half, half)
+    quarter = tok // 4 // 8 * 8
+    parts = (tok - 2 * quarter, quarter, quarter)
     vmem, hbm = pl.BlockSpec(memory_space=pltpu.VMEM), pl.BlockSpec(memory_space=pl.ANY)
     dma = pltpu.SemaphoreType.DMA
     return pl.pallas_call(
@@ -633,7 +635,7 @@
         out_shape=[jax.ShapeDtypeStruct((tok, d), BF16), jax.ShapeDtypeStruct(dr_part.shape, F32)],
         in_specs=[hbm, vmem], out_specs=[vmem, vmem],
         scratch_shapes=[pltpu.VMEM((8, tok, d), F32), pltpu.VMEM((8, tok, d), F32), pltpu.VMEM((7, tok, d), F32),
-                        dma((8,)), dma((8,)), dma((14,)), dma((14,)), dma((n_dev,)), dma((n_dev,)), dma((9,))],
+                        dma((8,)), dma((8,)), dma((21,)), dma((21,)), dma((n_dev,)), dma((n_dev,)), dma((9,))],
         compiler_params=pltpu.CompilerParams(collective_id=1, has_side_effects=True, vmem_limit_bytes=VMEM_LIMIT),
         cost_estimate=pl.CostEstimate(flops=0, bytes_accessed=8 * n_dev * tok * d, transcendentals=0),
         name="collect",
@@ -659,14 +661,13 @@
         position, weight = route_tables(expert_ids, route_w, experts, capacity)
         table = jnp.stack([position, weight], axis=1).reshape(n_ep, n_fs, n_loc, 2, tok)
         table = table.transpose(1, 0, 2, 3, 4).reshape(n_dev, n_loc * 2, tok)
-        xdy_all, table, *packed = spread(x_tok, dy_tok, table, w_gate, w_up, w_down, n_fs, n_ep)
+        xdy_all, table, own_down, *packed = spread(x_tok, dy_tok, table, w_gate, w_up, w_down, n_fs, n_ep)
         table = table.reshape(n_dev, n_loc, 2, tok)
         me = lax.axis_index("fsdp").astype(jnp.int32)
         weights = []
         for group in range(2):
-            weights.append([[lax.ppermute(packed[(2 * kind + group) * (n_fs - 1) + m - 1], "fsdp",
-                                          [(i, i ^ m) for i in range(n_fs)]) for m in range(1, n_fs)]
-                            for kind in range(2)])
+            weights.append([lax.ppermute(packed[group * (n_fs - 1) + m - 1], "fsdp", [(i, i ^ m) for i in range(n_fs)])
+                            for m in range(1, n_fs)])
 
         pos = table[:, :, 0, :].astype(jnp.int32)
         r = table[:, :, 1, :]
@@ -682,8 +683,8 @@
         for k in range(n_loc):
             info = jnp.stack([rows[k], jnp.maximum(1, blocks(rows[k], TILE)), me])
             dxk, drk, *slices = expert_call(
-                k, max(k - 1, 0), n_loc, info, x_pool, dy_pool, r_pool, (w_gate, w_up, w_down),
-                *weights[min(k, 1)], region)
+                k, max(k - 1, 0), n_loc, info, x_pool, dy_pool, r_pool, (w_gate, w_up, own_down),
+                weights[min(k, 1)], region)
             dx_pools.append(dxk)
             dr_pools.append(drk)
             pieces.append([slices[0]] + [lax.ppermute(slices[m], "fsdp", [(i, i ^ m) for i in range(n_fs)])

time: 918 us -> 804 us (0.88)
  Pallas kernels: 714 us -> 568 us
  waiting for transfers between devices: 130 us -> 148 us
  starting transfers between devices: 43.9 us -> 56.1 us
    pallas_call x1, Pallas kernels: 362 us -> 216 us  [collect(): pl.pallas_call(functools.partial(collect_kernel, n_fs, n_ep, parts), out_...]
    ppermute x12, starting transfers between devices: 30.8 us -> 49.1 us  [body(): lax.ppermute(slices[m], 'fsdp', [(i, i ^ m) for i in range(n_fs)])]
    ppermute x12, waiting for transfers between devices: 61 us -> 76.7 us  [body(): lax.ppermute(slices[m], 'fsdp', [(i, i ^ m) for i in range(n_fs)])]
    ppermute x12 -> x6, waiting for transfers between devices: 68.8 us -> 71 us  [body(): lax.ppermute(packed[group * (n_fs - 1) + m - 1], 'fsdp', [(i, i ^ m) for...]
  transfers between devices with their start and end apart: 24 -> 18, of which waited for: 6 -> 5; matrix products, arithmetic and copies ran while one was open for 1% -> 2% of each run, Pallas kernels for 63% -> 54%
where the time goes in v5:
time: 804 us; the launch traced here: 795 us
  Pallas kernels  568 us (71%)
  waiting for transfers between devices  148 us (18%)
  starting transfers between devices  56.1 us (7%)
  local copies, waits for them, and re-layouts  9.91 us (1%)
  other arithmetic  8.9 us (1%)
    pallas_call x1, Pallas kernels, collect(): pl.pallas_call(functools.partial(collect_kernel, n_fs, n_ep, parts), out_...  216 us
    pallas_call x1, Pallas kernels, spread(): pl.pallas_call(functools.partial(spread_kernel, n_fs, n_ep, n_loc, parts)...  131 us
    pallas_call x4, Pallas kernels, expert_call(): pl.pallas_call(functools.partial(expert_kernel, n_fs), out_shape=[jax.Sha...  118 us
    ppermute x12, waiting for transfers between devices, body(): lax.ppermute(slices[m], 'fsdp', [(i, i ^ m) for i in range(n_fs)])  76.7 us
    ppermute x6, waiting for transfers between devices, body(): lax.ppermute(packed[group * (n_fs - 1) + m - 1], 'fsdp', [(i, i ^ m) for...  71 us
    ppermute x12, starting transfers between devices, body(): lax.ppermute(slices[m], 'fsdp', [(i, i ^ m) for i in range(n_fs)])  49.1 us
    pallas_call x2, Pallas kernels, gather_rows(): pl.pallas_call(functools.partial(gather_kernel, n_src, n_loc, region, up(...  48.4 us
    pallas_call x1, Pallas kernels, combine_rows(): pl.pallas_call(functools.partial(combine_kernel, n_src, n_loc, slots), ou...  28.8 us
  transfers between devices with their start and end apart: 18, of which 5 were waited for; matrix products, arithmetic and copies ran while one was open for 2% of the time, Pallas kernels for 54%

profile of v5, /device:TPU:0, one launch (start us, length us, event | category | flops | bytes accessed | tf_op | source)
XLA Modules:
  0.0 795.0 jit_solution(15475961777543951455)
XLA Ops:
  0.7 1.1 fusion.1
  3.2 1.2 reshape.49.table_ref
  4.3 131.3 %spread.1 = (bf16[16384,1024]{1,0:T(8,128)(2,1)}, f32[16,8,1024]{2,1,0:T(8,128)}, bf16[4,128,1280]{2,1,0:T(8,128)(2,1)}, bf16[1,3,128,1280]{3,2,1,0:T(8,128)(2,1...) custom-call(bf16[1024,512]{1,0:T(8,128)(2,1)} %x_ref.1, ...), custom_call_target="tpu_custom_call" | custom-call | bytes 67108864 | tf_op jit(solution)/shard_map/spread/pallas_call | solution.py:544
  135.6 0.6 collective-permute-start
  136.2 1.5 collective-permute-start.1
  137.7 1.5 collective-permute-start.2
  139.7 1.5 collective-permute-start.4
  141.2 1.3 copy.28
  142.9 0.9 fusion.2.refs_2_.pos_ref
  143.8 0.6 fusion.11
  147.1 0.9 copy.41
  148.0 0.6 add.54.refs_0_.cnt
  148.7 1.3 add_add_fusion.3.info
  150.0 1.3 add_add_fusion.info
  151.5 0.6 fusion.8.refs_1_.off
  152.1 1.9 add_add_fusion.1
  154.0 21.3 %gather_x.1.x_ref = bf16[26624,512]{1,0:T(8,128)(2,1)} custom-call(s32[64]{0:T(128)} %add.54.refs_0_.cnt, s32[64]{0:T(128)} %fusion.8.refs_1_.off, s32[16,4,1024]{2,1,0:T(4,128)} %fusion.2.refs_2_.pos_ref, bf16[16384,1024]{1,0:T(8,128)(2,1)} %get-tuple-element.57.refs_3_.refs_4_), custom_call_target="tpu_custom_call" | custom-call | flops 12582912000 | bytes 33554432 | tf_op jit(solution)/shard_map/gather_x/pallas_call | solution.py:161
  175.3 27.1 %gather_r.1 = (bf16[26624,512]{1,0:T(8,128)(2,1)}, f32[26624,128]{1,0:T(8,128)}) custom-call(s32[64]{0:T(128)} %add.54.refs_0_.cnt, s32[64]{0:T(128)} %fusion.8.refs_1_.off, s32[16,4,1024]{2,1,0:T(4,128)} %fusion.2.refs_2_.pos_ref, f32[16,4,1024]{2,1,0:T(4,128)} %bitcast.30, bf16[16384,1024]{1,0:T(8,128)(2,1)} %get-tuple-element.57.refs_3_.refs_4_), custom_call_target="tpu_custom_call" | custom-call | flops 12582912000 | bytes 33554432 | tf_op jit(solution)/shard_map/gather_r/pallas_call | solution.py:161
  202.5 1.5 collective-permute-start.5
  204.0 0.9 copy-done.7
  205.2 29.3 %shard_map.110 = (bf16[6656,512]{1,0:T(8,128)(2,1)}, f32[6656,128]{1,0:T(8,128)}, f32[3,128,1280]{2,1,0:T(8,128)}, f32[3,128,1280]{2,1,0:T(8,128)}, f32[3,128,1280]{2,1,0:T(8,128)}, /*index=5*/f32[3,128,1280]{2,1,0:T(8,128)}) custom-call(s32[3]{0:T(128)} %add_add_fusion.info, bf16[26624,512]{1,0:T(8,128)(2,1)} %gather_x.1.x_ref, ...), custom_call_target="tpu_custom_call" | custom-call | flops 35389440000 | bytes 15728640 | tf_op jit(solution)/shard_map/pallas_call | solution.py:244
  234.6 0.6 collective-permute-start.15
  235.2 1.5 collective-permute-start.16
  236.6 8.3 %collective-permute-done.3.refs_3_ = bf16[3,3,128,1280]{3,2,1,0:T(8,128)(2,1)} collective-permute-done((bf16[3,3,128,1280]{3,2,1,0:T(8,128)(2,1)}, bf16[3,3,128,1280]{3,2,1,0:T(8,128)(2,1)}, u32[]{:S(2)}, u32[]{:S(2)}) %collective-permute-start.3) | collective-permute-done | bytes 2949152 | tf_op jit(solution)/shard_map/ppermute | solution.py:669
  244.9 1.5 collective-permute-start.17
  246.4 62.7 %collective-permute-done.5.refs_5_ = bf16[3,3,128,1280]{3,2,1,0:T(8,128)(2,1)} collective-permute-done((bf16[3,3,128,1280]{3,2,1,0:T(8,128)(2,1)}, bf16[3,3,128,1280]{3,2,1,0:T(8,128)(2,1)}, u32[]{:S(2)}, u32[]{:S(2)}) %collective-permute-start.5) | collective-permute-done | bytes 2949152 | tf_op jit(solution)/shard_map/ppermute | solution.py:669
  309.1 29.6 %shard_map.112 = (bf16[6656,512]{1,0:T(8,128)(2,1)}, f32[6656,128]{1,0:T(8,128)}, f32[3,128,1280]{2,1,0:T(8,128)}, f32[3,128,1280]{2,1,0:T(8,128)}, f32[3,128,1280]{2,1,0:T(8,128)}, /*index=5*/f32[3,128,1280]{2,1,0:T(8,128)}) custom-call(s32[3]{0:T(128)} %get-tuple-element.118.info, bf16[26624,512]{1,0:T(8,128)(2,1)} %gather_x.1.x_ref, ...), custom_call_target="tpu_custom_call" | custom-call | flops 35389440000 | bytes 15728640 | tf_op jit(solution)/shard_map/pallas_call | solution.py:244
  338.6 0.6 collective-permute-start.9
  339.2 29.3 %shard_map.111 = (bf16[6656,512]{1,0:T(8,128)(2,1)}, f32[6656,128]{1,0:T(8,128)}, f32[3,128,1280]{2,1,0:T(8,128)}, f32[3,128,1280]{2,1,0:T(8,128)}, f32[3,128,1280]{2,1,0:T(8,128)}, /*index=5*/f32[3,128,1280]{2,1,0:T(8,128)}) custom-call(s32[3]{0:T(128)} %get-tuple-element.117.info, bf16[26624,512]{1,0:T(8,128)(2,1)} %gather_x.1.x_ref, ...), custom_call_target="tpu_custom_call" | custom-call | flops 35389440000 | bytes 15728640 | tf_op jit(solution)/shard_map/pallas_call | solution.py:244
  368.6 1.5 collective-permute-start.12
  370.6 23.8 %collective-permute-start.14 = (f32[3,128,1280]{2,1,0:T(8,128)}, f32[3,128,1280]{2,1,0:T(8,128)}, u32[]{:S(2)}, u32[]{:S(2)}) collective-permute-start(f32[3,128,1280]{2,1,0:T(8,128)} %get-tuple-element.90), channel_id=1, source_target_pairs={{0,12},{4,8},{8,4},{12,0},{1,13},{5,9},{9,5},{13,1},{2,14},{6,10},... | collective-permute-start | bytes 5898248 | tf_op jit(solution)/shard_map/ppermute | solution.py:690
  394.4 29.6 %shard_map.113 = (bf16[6656,512]{1,0:T(8,128)(2,1)}, f32[6656,128]{1,0:T(8,128)}, f32[3,128,1280]{2,1,0:T(8,128)}, f32[3,128,1280]{2,1,0:T(8,128)}, f32[3,128,1280]{2,1,0:T(8,128)}, /*index=5*/f32[3,128,1280]{2,1,0:T(8,128)}) custom-call(s32[3]{0:T(128)} %add_add_fusion.3.info, bf16[26624,512]{1,0:T(8,128)(2,1)} %gather_x.1.x_ref, ...), custom_call_target="tpu_custom_call" | custom-call | flops 35389440000 | bytes 15728640 | tf_op jit(solution)/shard_map/pallas_call | solution.py:244
  424.2 2.7 collective-permute-done.9.refs_1_
  426.9 9.2 %collective-permute-start.11 = (f32[3,128,1280]{2,1,0:T(8,128)}, f32[3,128,1280]{2,1,0:T(8,128)}, u32[]{:S(2)}, u32[]{:S(2)}) collective-permute-start(f32[3,128,1280]{2,1,0:T(8,128)} %get-tuple-element.86), channel_id=1, source_target_pairs={{0,12},{4,8},{8,4},{12,0},{1,13},{5,9},{9,5},{13,1},{2,14},{6,10},... | collective-permute-start | bytes 5898248 | tf_op jit(solution)/shard_map/ppermute | solution.py:690
  436.1 32.9 %collective-permute-done.12.refs_1_ = f32[3,128,1280]{2,1,0:T(8,128)} collective-permute-done((f32[3,128,1280]{2,1,0:T(8,128)}, f32[3,128,1280]{2,1,0:T(8,128)}, u32[]{:S(2)}, u32[]{:S(2)}) %collective-permute-start.12) | collective-permute-done | bytes 1966112 | tf_op jit(solution)/shard_map/ppermute | solution.py:690
  469.0 0.8 collective-permute-start.6
  469.8 8.9 %collective-permute-start.7 = (f32[3,128,1280]{2,1,0:T(8,128)}, f32[3,128,1280]{2,1,0:T(8,128)}, u32[]{:S(2)}, u32[]{:S(2)}) collective-permute-start(f32[3,128,1280]{2,1,0:T(8,128)} %get-tuple-element.81), channel_id=1, source_target_pairs={{0,8},{4,12},{8,0},{12,4},{1,9},{5,13},{9,1},{13,5},{2,10},{6,14},... | collective-permute-start | bytes 5898248 | tf_op jit(solution)/shard_map/ppermute | solution.py:690
  478.8 41.1 %collective-permute-done.14.refs_3_ = f32[3,128,1280]{2,1,0:T(8,128)} collective-permute-done((f32[3,128,1280]{2,1,0:T(8,128)}, f32[3,128,1280]{2,1,0:T(8,128)}, u32[]{:S(2)}, u32[]{:S(2)}) %collective-permute-start.14) | collective-permute-done | bytes 1966112 | tf_op jit(solution)/shard_map/ppermute | solution.py:690
  519.9 28.8 %combine.1 = (f32[16384,512]{1,0:T(8,128)}, f32[16,4,1024]{2,1,0:T(4,128)}) custom-call(s32[64]{0:T(128)} %add.54.refs_0_.cnt, s32[64]{0:T(128)} %fusion.8.refs_1_.off, s32[16,4,1024]{2,1,0:T(4,128)} %fusion.2.refs_2_.pos_ref, bf16[6656,512]{1,0:T(8,128)(2,1)} %get-tuple-element.64.refs_0_, bf16[6656,512]{1,0:T(8,128)(2,1)} %get-tuple-element.68.refs_1_, ...), custom_call_target="tpu_custom_call" | custom-call | flops 12582912000 | bytes 33554432 | tf_op jit(solution)/shard_map/combine/pallas_call | solution.py:377
  548.7 215.6 %collect.1 = (bf16[1024,512]{1,0:T(8,128)(2,1)}, f32[16,4,1024]{2,1,0:T(4,128)}) custom-call(f32[16384,512]{1,0:T(8,128)} %get-tuple-element.75.part_ref, f32[16,4,1024]{2,1,0:T(4,128)} %get-tuple-element.76.dr_ref), custom_call_target="tpu_custom_call" | custom-call | bytes 67108864 | tf_op jit(solution)/shard_map/collect/pallas_call | solution.py:633
  764.3 1.0 copy.42
  765.4 6.5 shard_map.114
  771.9 0.9 select_reduce_fusion
  772.8 6.4 shard_map.115
  779.3 6.5 shard_map.116
  785.8 1.3 copy-done.1
  787.0 6.5 shard_map.117
  793.6 1.0 copy.53
  (46 shorter events, 3.7 us)
Async XLA Ops:
  0.6 1.6 copy-start.3
  0.6 1.6 copy-start.5
  135.6 66.8 %collective-permute-start = (bf16[1,3,128,1280]{3,2,1,0:T(8,128)(2,1)}, bf16[1,3,128,1280]{3,2,1,0:T(8,128)(2,1)S(1)}, u32[]{:S(2)}, u32[]{:S(2)}) collective-permute-start(bf16[1,3,128,1280]{3,2,1,0:T(8,128)(2,1)} %get-tuple-element.61), channel_id=1, source_target_pairs={{0,4},{4,0},{8,12},{12,8},{1,5},{5,1},{9,13},{13,9},{2,6},{6,2},{1... | collective-permute-start | bytes 2949128 | tf_op jit(solution)/shard_map/ppermute | solution.py:669
  136.2 67.7 %collective-permute-start.1 = (bf16[1,3,128,1280]{3,2,1,0:T(8,128)(2,1)}, bf16[1,3,128,1280]{3,2,1,0:T(8,128)(2,1)S(1)}, u32[]{:S(2)}, u32[]{:S(2)}) collective-permute-start(bf16[1,3,128,1280]{3,2,1,0:T(8,128)(2,1)} %get-tuple-element.62), channel_id=1, source_target_pairs={{0,8},{4,12},{8,0},{12,4},{1,9},{5,13},{9,1},{13,5},{2,10},{6,14},... | collective-permute-start | bytes 2949128 | tf_op jit(solution)/shard_map/ppermute | solution.py:669
  137.7 66.3 %collective-permute-start.2 = (bf16[1,3,128,1280]{3,2,1,0:T(8,128)(2,1)}, bf16[1,3,128,1280]{3,2,1,0:T(8,128)(2,1)S(1)}, u32[]{:S(2)}, u32[]{:S(2)}) collective-permute-start(bf16[1,3,128,1280]{3,2,1,0:T(8,128)(2,1)} %get-tuple-element.63), channel_id=1, source_target_pairs={{0,12},{4,8},{8,4},{12,0},{1,13},{5,9},{9,5},{13,1},{2,14},{6,10},... | collective-permute-start | bytes 2949128 | tf_op jit(solution)/shard_map/ppermute | solution.py:669
  139.1 105.8 %collective-permute-start.3 = (bf16[3,3,128,1280]{3,2,1,0:T(8,128)(2,1)}, bf16[3,3,128,1280]{3,2,1,0:T(8,128)(2,1)}, u32[]{:S(2)}, u32[]{:S(2)}) collective-permute-start(bf16[3,3,128,1280]{3,2,1,0:T(8,128)(2,1)} %get-tuple-element.65), channel_id=1, source_target_pairs={{0,4},{4,0},{8,12},{12,8},{1,5},{5,1},{9,13},{13,9},{2,6},{6,2},{1... | collective-permute-start | bytes 8847368 | tf_op jit(solution)/shard_map/ppermute | solution.py:669
  139.7 106.7 %collective-permute-start.4 = (bf16[3,3,128,1280]{3,2,1,0:T(8,128)(2,1)}, bf16[3,3,128,1280]{3,2,1,0:T(8,128)(2,1)}, u32[]{:S(2)}, u32[]{:S(2)}) collective-permute-start(bf16[3,3,128,1280]{3,2,1,0:T(8,128)(2,1)} %get-tuple-element.66), channel_id=1, source_target_pairs={{0,8},{4,12},{8,0},{12,4},{1,9},{5,13},{9,1},{13,5},{2,10},{6,14},... | collective-permute-start | bytes 8847368 | tf_op jit(solution)/shard_map/ppermute | solution.py:669
  202.4 1.5 copy-start.6
  202.5 106.6 %collective-permute-start.5 = (bf16[3,3,128,1280]{3,2,1,0:T(8,128)(2,1)}, bf16[3,3,128,1280]{3,2,1,0:T(8,128)(2,1)}, u32[]{:S(2)}, u32[]{:S(2)}) collective-permute-start(bf16[3,3,128,1280]{3,2,1,0:T(8,128)(2,1)} %get-tuple-element.67), channel_id=1, source_target_pairs={{0,12},{4,8},{8,4},{12,0},{1,13},{5,9},{9,5},{13,1},{2,14},{6,10},... | collective-permute-start | bytes 8847368 | tf_op jit(solution)/shard_map/ppermute | solution.py:669
  203.9 0.9 copy-start.7
  204.0 1.3 copy-start.8
  234.6 135.5 %collective-permute-start.15 = (f32[3,128,1280]{2,1,0:T(8,128)}, f32[3,128,1280]{2,1,0:T(8,128)S(1)}, u32[]{:S(2)}, u32[]{:S(2)}) collective-permute-start(f32[3,128,1280]{2,1,0:T(8,128)} %get-tuple-element.92), channel_id=1, source_target_pairs={{0,4},{4,0},{8,12},{12,8},{1,5},{5,1},{9,13},{13,9},{2,6},{6,2},{1... | collective-permute-start | bytes 5898248 | tf_op jit(solution)/shard_map/ppermute | solution.py:690
  235.2 135.4 %collective-permute-start.16 = (f32[3,128,1280]{2,1,0:T(8,128)}, f32[3,128,1280]{2,1,0:T(8,128)}, u32[]{:S(2)}, u32[]{:S(2)}) collective-permute-start(f32[3,128,1280]{2,1,0:T(8,128)} %get-tuple-element.93), channel_id=1, source_target_pairs={{0,8},{4,12},{8,0},{12,4},{1,9},{5,13},{9,1},{13,5},{2,10},{6,14},... | collective-permute-start | bytes 5898248 | tf_op jit(solution)/shard_map/ppermute | solution.py:690
  244.9 179.1 %collective-permute-start.17 = (f32[3,128,1280]{2,1,0:T(8,128)}, f32[3,128,1280]{2,1,0:T(8,128)}, u32[]{:S(2)}, u32[]{:S(2)}) collective-permute-start(f32[3,128,1280]{2,1,0:T(8,128)} %get-tuple-element.94), channel_id=1, source_target_pairs={{0,12},{4,8},{8,4},{12,0},{1,13},{5,9},{9,5},{13,1},{2,14},{6,10},... | collective-permute-start | bytes 5898248 | tf_op jit(solution)/shard_map/ppermute | solution.py:690
  338.6 88.2 %collective-permute-start.9 = (f32[3,128,1280]{2,1,0:T(8,128)}, f32[3,128,1280]{2,1,0:T(8,128)}, u32[]{:S(2)}, u32[]{:S(2)}) collective-permute-start(f32[3,128,1280]{2,1,0:T(8,128)} %get-tuple-element.84), channel_id=1, source_target_pairs={{0,4},{4,0},{8,12},{12,8},{1,5},{5,1},{9,13},{13,9},{2,6},{6,2},{1... | collective-permute-start | bytes 5898248 | tf_op jit(solution)/shard_map/ppermute | solution.py:690
  368.6 100.4 %collective-permute-start.12 = (f32[3,128,1280]{2,1,0:T(8,128)}, f32[3,128,1280]{2,1,0:T(8,128)}, u32[]{:S(2)}, u32[]{:S(2)}) collective-permute-start(f32[3,128,1280]{2,1,0:T(8,128)} %get-tuple-element.88), channel_id=1, source_target_pairs={{0,4},{4,0},{8,12},{12,8},{1,5},{5,1},{9,13},{13,9},{2,6},{6,2},{1... | collective-permute-start | bytes 5898248 | tf_op jit(solution)/shard_map/ppermute | solution.py:690
  370.1 53.9 %copy-start = (f32[3,128,1280]{2,1,0:T(8,128)}, f32[3,128,1280]{2,1,0:T(8,128)S(1)}, u32[]{:S(2)}) copy-start(f32[3,128,1280]{2,1,0:T(8,128)S(1)} %collective-permute-done.15.refs_1_) | copy-start | bytes 5898244
  370.1 99.8 %collective-permute-start.13 = (f32[3,128,1280]{2,1,0:T(8,128)}, f32[3,128,1280]{2,1,0:T(8,128)}, u32[]{:S(2)}, u32[]{:S(2)}) collective-permute-start(f32[3,128,1280]{2,1,0:T(8,128)} %get-tuple-element.89), channel_id=1, source_target_pairs={{0,8},{4,12},{8,0},{12,4},{1,9},{5,13},{9,1},{13,5},{2,10},{6,14},... | collective-permute-start | bytes 5898248 | tf_op jit(solution)/shard_map/ppermute | solution.py:690
  370.6 149.3 %collective-permute-start.14 = (f32[3,128,1280]{2,1,0:T(8,128)}, f32[3,128,1280]{2,1,0:T(8,128)}, u32[]{:S(2)}, u32[]{:S(2)}) collective-permute-start(f32[3,128,1280]{2,1,0:T(8,128)} %get-tuple-element.90), channel_id=1, source_target_pairs={{0,12},{4,8},{8,4},{12,0},{1,13},{5,9},{9,5},{13,1},{2,14},{6,10},... | collective-permute-start | bytes 5898248 | tf_op jit(solution)/shard_map/ppermute | solution.py:690
  424.0 355.2 %collective-permute-start.10 = (f32[3,128,1280]{2,1,0:T(8,128)}, f32[3,128,1280]{2,1,0:T(8,128)}, u32[]{:S(2)}, u32[]{:S(2)}) collective-permute-start(f32[3,128,1280]{2,1,0:T(8,128)} %get-tuple-element.85), channel_id=1, source_target_pairs={{0,8},{4,12},{8,0},{12,4},{1,9},{5,13},{9,1},{13,5},{2,10},{6,14},... | collective-permute-start | bytes 5898248 | tf_op jit(solution)/shard_map/ppermute | solution.py:690
  426.9 352.4 %collective-permute-start.11 = (f32[3,128,1280]{2,1,0:T(8,128)}, f32[3,128,1280]{2,1,0:T(8,128)}, u32[]{:S(2)}, u32[]{:S(2)}) collective-permute-start(f32[3,128,1280]{2,1,0:T(8,128)} %get-tuple-element.86), channel_id=1, source_target_pairs={{0,12},{4,8},{8,4},{12,0},{1,13},{5,9},{9,5},{13,1},{2,14},{6,10},... | collective-permute-start | bytes 5898248 | tf_op jit(solution)/shard_map/ppermute | solution.py:690
  469.0 316.8 %collective-permute-start.6 = (f32[3,128,1280]{2,1,0:T(8,128)}, f32[3,128,1280]{2,1,0:T(8,128)S(1)}, u32[]{:S(2)}, u32[]{:S(2)}) collective-permute-start(f32[3,128,1280]{2,1,0:T(8,128)} %get-tuple-element.80), channel_id=1, source_target_pairs={{0,4},{4,0},{8,12},{12,8},{1,5},{5,1},{9,13},{13,9},{2,6},{6,2},{1... | collective-permute-start | bytes 5898248 | tf_op jit(solution)/shard_map/ppermute | solution.py:690
  469.8 315.9 %collective-permute-start.7 = (f32[3,128,1280]{2,1,0:T(8,128)}, f32[3,128,1280]{2,1,0:T(8,128)}, u32[]{:S(2)}, u32[]{:S(2)}) collective-permute-start(f32[3,128,1280]{2,1,0:T(8,128)} %get-tuple-element.81), channel_id=1, source_target_pairs={{0,8},{4,12},{8,0},{12,4},{1,9},{5,13},{9,1},{13,5},{2,10},{6,14},... | collective-permute-start | bytes 5898248 | tf_op jit(solution)/shard_map/ppermute | solution.py:690
  519.9 265.9 %collective-permute-start.8 = (f32[3,128,1280]{2,1,0:T(8,128)}, f32[3,128,1280]{2,1,0:T(8,128)}, u32[]{:S(2)}, u32[]{:S(2)}) collective-permute-start(f32[3,128,1280]{2,1,0:T(8,128)} %get-tuple-element.82), channel_id=1, source_target_pairs={{0,12},{4,8},{8,4},{12,0},{1,13},{5,9},{9,5},{13,1},{2,14},{6,10},... | collective-permute-start | bytes 5898248 | tf_op jit(solution)/shard_map/ppermute | solution.py:690
  765.4 6.5 copy-start.4
  785.7 1.3 copy-start.1
  787.0 6.5 copy-start.2

commit v6 on v5

--- a/solution.py
+++ b/solution.py
@@ -258,40 +258,44 @@
     )(info, x_pool, dy_pool, r_pool, *own, *peers)
 
 
-def place_kernel(n_fs, n_loc, k, first, me, *refs):
-    pieces = refs[:n_fs]
-    n_in = n_fs if first else n_fs + 3
-    outs, (turned, sem) = refs[n_in:n_in + 3], refs[n_in + 3:]
-    copies = []
-    for m in range(n_fs):
-        to = (me[0] ^ m) * n_loc + k
-        copies.append(pltpu.make_async_copy(pieces[m].at[0], outs[0].at[to], sem))
-        copies.append(pltpu.make_async_copy(pieces[m].at[1], outs[1].at[to], sem))
-    for copy in copies:
+def place_kernel(n_fs, n_loc, ks, first, me, *refs):
+    n_pieces = n_fs * len(ks)
+    pieces, refs = refs[:n_pieces], refs[n_pieces + (0 if first else 3):]
+    outs, (held, turned, in_sem, out_sem) = refs[:3], refs[3:]
+    reads = [pltpu.make_async_copy(piece, held.at[n], in_sem.at[n]) for n, piece in enumerate(pieces)]
+    for copy in reads:
         copy.start()
-    for m in range(n_fs):
-        turned[m] = pieces[m][2].T
-        copies.append(pltpu.make_async_copy(turned.at[m], outs[2].at[(me[0] ^ m) * n_loc + k], sem))
-        copies[-1].start()
-    for copy in copies:
+    writes = []
+    for n, copy in enumerate(reads):
         copy.wait()
-
-
-def place(k, n_loc, me, pieces, grads):
-    n_fs = len(pieces)
+        to = (me[0] ^ n % n_fs) * n_loc + ks[n // n_fs]
+        for t in range(2):
+            writes.append(pltpu.make_async_copy(held.at[n, t], outs[t].at[to], out_sem))
+            writes[-1].start()
+        turned[n] = held[n, 2].T
+        writes.append(pltpu.make_async_copy(turned.at[n], outs[2].at[to], out_sem))
+        writes[-1].start()
+    for copy in writes:
+        copy.wait()
+
+
+def place(ks, n_loc, me, pieces, grads):
+    n_fs = len(pieces) // len(ks)
     _, dsl, f = pieces[0].shape
-    vmem, hbm = pl.BlockSpec(memory_space=pltpu.VMEM), pl.BlockSpec(memory_space=pl.ANY)
+    hbm = pl.BlockSpec(memory_space=pl.ANY)
     first = grads is None
+    n = len(pieces)
     shapes = [(n_fs * n_loc, dsl, f)] * 2 + [(n_fs * n_loc, f, dsl)]
     return pl.pallas_call(
-        functools.partial(place_kernel, n_fs, n_loc, k, first),
+        functools.partial(place_kernel, n_fs, n_loc, ks, first),
         out_shape=[jax.ShapeDtypeStruct(v, F32) for v in shapes],
-        in_specs=[pl.BlockSpec(memory_space=pltpu.SMEM)] + [vmem] * n_fs + ([] if first else [hbm] * 3),
+        in_specs=[pl.BlockSpec(memory_space=pltpu.SMEM)] + [hbm] * (n if first else n + 3),
         out_specs=[hbm] * 3,
-        scratch_shapes=[pltpu.VMEM((n_fs, f, dsl), F32), pltpu.SemaphoreType.DMA],
-        input_output_aliases={} if first else {n_fs + 1 + t: t for t in range(3)},
+        scratch_shapes=[pltpu.VMEM((n, 3, dsl, f), F32), pltpu.VMEM((n, f, dsl), F32),
+                        pltpu.SemaphoreType.DMA((n,)), pltpu.SemaphoreType.DMA],
+        input_output_aliases={} if first else {n + 1 + t: t for t in range(3)},
         compiler_params=pltpu.CompilerParams(vmem_limit_bytes=VMEM_LIMIT),
-        cost_estimate=pl.CostEstimate(flops=0, bytes_accessed=6 * 4 * n_fs * dsl * f, transcendentals=0),
+        cost_estimate=pl.CostEstimate(flops=0, bytes_accessed=6 * 4 * n * dsl * f, transcendentals=0),
     )(me, *pieces, *([] if first else grads))
 
 
@@ -394,7 +398,13 @@
 MESH = pl.DeviceIdType.MESH
 HOPS = ((0, 2), (1, 0), (2, 0))
 SIBLING = (0, 1)
-ORDERS = ((0, 1, 2), (1, 2, 0), (2, 0, 1))
+SPREAD_ORDERS = ((1, 2, 0), (2, 1, 0), (0, 1, 2), (0, 2, 1))
+COLLECT_ORDERS = ((0, 1, 2), (0, 2, 1), (1, 2, 0), (2, 1, 0))
+
+
+def parts_of(tok):
+    long = tok * 5 // 16 // 16 * 16
+    return long, long, tok // 2 - long, tok // 2 - long
 
 
 def here():
@@ -440,7 +450,7 @@
 def spread_kernel(n_fs, n_ep, n_loc, parts, x_ref, dy_ref, table_ref, wg_ref, wu_ref, wd_ref, full, table_all, *refs):
     n_out = 2 * (n_fs - 1)
     own_down, w_out, refs = refs[0], refs[1:n_out + 1], refs[n_out + 1:]
-    own, send, recv, c_send, c_recv, t_send, t_recv, own_sem, w_buf, down_buf, in_sem, out_sem = refs
+    own, send, recv, c_send, c_recv, t_send, t_recv, own_sem, w_buf, down_buf, in_sem, out_sem, w_send, w_recv = refs
     tok, d = x_ref.shape
     mine = block_of(0)
     local = []
@@ -452,7 +462,7 @@
         copy.wait()
     local = [pltpu.make_async_copy(own, full.at[pl.ds(aligned(mine * tok, tok), tok)], own_sem.at[0]),
              pltpu.make_async_copy(table_ref.at[mine], table_all.at[mine], own_sem.at[2])]
-    starts = [sum(parts[:q]) for q in range(3)]
+    starts = [sum(parts[:q]) for q in range(len(parts))]
     sem_at = {}
     inbound = {}
 
@@ -462,7 +472,7 @@
         n = sem_at.setdefault((q, phase, bits), len(sem_at))
         copy = pltpu.make_async_remote_copy(
             src_ref=src, dst_ref=full.at[to], send_sem=send.at[n], recv_sem=recv.at[n],
-            device_id=peer_of(HOPS[ORDERS[q][phase]]), device_id_type=MESH)
+            device_id=peer_of(HOPS[SPREAD_ORDERS[q][phase]]), device_id_type=MESH)
         copy.start()
         inbound[(q, phase, bits)] = copy
 
@@ -479,9 +489,9 @@
         shared.append(copy)
 
     for phase in range(3):
-        for q in range(3):
+        for q in range(len(parts)):
             send_on(q, phase, 0)
-    for q in range(3):
+    for q in range(len(parts)):
         share(q, 0)
     for copy in local:
         copy.start()
@@ -505,22 +515,29 @@
         k, m = n // n_fs, n % n_fs
         if m == 0:
             copy = pltpu.make_async_copy(w_buf.at[n, 2], own_down.at[k], out_sem.at[n])
+        elif k == 0:
+            continue
         else:
-            to, at = (m - 1, 0) if k == 0 else (n_fs + m - 2, k - 1)
-            copy = pltpu.make_async_copy(w_buf.at[n], w_out[to].at[at], out_sem.at[n])
+            copy = pltpu.make_async_copy(w_buf.at[n], w_out[n_fs + m - 2].at[k - 1], out_sem.at[n])
         copy.start()
         local.append(copy)
     for phase in range(3):
-        for q in range(3):
+        for q in range(len(parts)):
             held = [0]
-            for axis in ORDERS[q][:phase]:
+            for axis in SPREAD_ORDERS[q][:phase]:
                 held += [b | 1 << axis for b in held]
             for b in held:
                 inbound[(q, phase, b)].wait_recv()
-                got = b | 1 << ORDERS[q][phase]
+                got = b | 1 << SPREAD_ORDERS[q][phase]
                 for later in range(phase + 1, 3):
                     send_on(q, later, got)
                 share(q, got)
+        if phase == 1:
+            for m in range(1, n_fs):
+                pending.append(pltpu.make_async_remote_copy(
+                    src_ref=w_buf.at[m], dst_ref=w_out[m - 1].at[0], send_sem=w_send.at[m - 1], recv_sem=w_recv.at[m - 1],
+                    device_id=peer_of((m, 0)), device_id_type=MESH))
+                pending[-1].start()
     for copy in inbound.values():
         copy.wait_send()
     for copy in shared:
@@ -537,8 +554,7 @@
     exp_local, dsl, f = w_gate.shape
     n_loc = exp_local // n_fs
     n_slices, groups = n_loc * n_fs, [1] * (n_fs - 1) + [n_loc - 1] * (n_fs - 1)
-    third = tok // 3 // 16 * 16
-    parts = (tok - 2 * third, third, third)
+    parts = parts_of(tok)
     vmem, hbm = pl.BlockSpec(memory_space=pltpu.VMEM), pl.BlockSpec(memory_space=pl.ANY)
     dma = pltpu.SemaphoreType.DMA
     return pl.pallas_call(
@@ -546,9 +562,9 @@
         out_shape=[jax.ShapeDtypeStruct((n_dev * tok, 2 * d), x_tok.dtype), jax.ShapeDtypeStruct(table.shape, table.dtype)]
         + [jax.ShapeDtypeStruct((n_loc, dsl, f), BF16)] + [jax.ShapeDtypeStruct((g, 3, dsl, f), BF16) for g in groups],
         in_specs=[hbm] * 2 + [vmem] + [hbm] * 3, out_specs=[hbm] * (3 + len(groups)),
-        scratch_shapes=[pltpu.VMEM((tok, 2 * d), BF16), dma((21,)), dma((21,)), dma((24,)), dma((24,)), dma((n_dev,)), dma((n_dev,)),
+        scratch_shapes=[pltpu.VMEM((tok, 2 * d), BF16), dma((28,)), dma((28,)), dma((32,)), dma((32,)), dma((n_dev,)), dma((n_dev,)),
                         dma((3,)), pltpu.VMEM((n_slices, 3, dsl, f), BF16), pltpu.VMEM((n_slices, f, dsl), BF16),
-                        dma((3 * n_slices,)), dma((n_slices,))],
+                        dma((3 * n_slices,)), dma((n_slices,)), dma((n_fs - 1,)), dma((n_fs - 1,))],
         compiler_params=pltpu.CompilerParams(collective_id=0, has_side_effects=True, vmem_limit_bytes=VMEM_LIMIT),
         cost_estimate=pl.CostEstimate(flops=0, bytes_accessed=8 * n_dev * tok * d, transcendentals=0),
         name="spread",
@@ -579,18 +595,18 @@
     hops = {}
 
     def phase_of(q, bits):
-        return next(n for n in range(3) if bits >> ORDERS[q][n] & 1)
+        return next(n for n in range(3) if bits >> COLLECT_ORDERS[q][n] & 1)
 
     def send_off(q, bits):
         n = slots.index((q, bits))
         rows = pl.ds(starts[q], parts[q])
         hops[(q, bits)] = pltpu.make_async_remote_copy(
             src_ref=acc.at[bits, rows], dst_ref=got.at[bits - 1, rows], send_sem=send.at[n], recv_sem=recv.at[n],
-            device_id=peer_of(HOPS[ORDERS[q][phase_of(q, bits)]]), device_id_type=MESH)
+            device_id=peer_of(HOPS[COLLECT_ORDERS[q][phase_of(q, bits)]]), device_id_type=MESH)
         hops[(q, bits)].start()
 
     def add_arrival(q, bits, phase):
-        frm = bits | 1 << ORDERS[q][phase]
+        frm = bits | 1 << COLLECT_ORDERS[q][phase]
         hops[(q, frm)].wait_recv()
         rows = slice(starts[q], starts[q] + parts[q])
         acc[bits, rows, :] = acc[bits, rows, :] + got[frm - 1, rows, :]
@@ -626,8 +642,7 @@
 def collect(dx_part, dr_part, n_fs, n_ep):
     n_dev = n_fs * n_ep
     tok, d = dx_part.shape[0] // n_dev, dx_part.shape[1]
-    quarter = tok // 4 // 8 * 8
-    parts = (tok - 2 * quarter, quarter, quarter)
+    parts = parts_of(tok)
     vmem, hbm = pl.BlockSpec(memory_space=pltpu.VMEM), pl.BlockSpec(memory_space=pl.ANY)
     dma = pltpu.SemaphoreType.DMA
     return pl.pallas_call(
@@ -635,7 +650,7 @@
         out_shape=[jax.ShapeDtypeStruct((tok, d), BF16), jax.ShapeDtypeStruct(dr_part.shape, F32)],
         in_specs=[hbm, vmem], out_specs=[vmem, vmem],
         scratch_shapes=[pltpu.VMEM((8, tok, d), F32), pltpu.VMEM((8, tok, d), F32), pltpu.VMEM((7, tok, d), F32),
-                        dma((8,)), dma((8,)), dma((21,)), dma((21,)), dma((n_dev,)), dma((n_dev,)), dma((9,))],
+                        dma((8,)), dma((8,)), dma((28,)), dma((28,)), dma((n_dev,)), dma((n_dev,)), dma((9,))],
         compiler_params=pltpu.CompilerParams(collective_id=1, has_side_effects=True, vmem_limit_bytes=VMEM_LIMIT),
         cost_estimate=pl.CostEstimate(flops=0, bytes_accessed=8 * n_dev * tok * d, transcendentals=0),
         name="collect",
@@ -664,10 +679,9 @@
         xdy_all, table, own_down, *packed = spread(x_tok, dy_tok, table, w_gate, w_up, w_down, n_fs, n_ep)
         table = table.reshape(n_dev, n_loc, 2, tok)
         me = lax.axis_index("fsdp").astype(jnp.int32)
-        weights = []
-        for group in range(2):
-            weights.append([lax.ppermute(packed[group * (n_fs - 1) + m - 1], "fsdp", [(i, i ^ m) for i in range(n_fs)])
-                            for m in range(1, n_fs)])
+        first_w, later_w = packed[:n_fs - 1], packed[n_fs - 1:]
+        later_w = [lax.ppermute(later_w[m - 1], "fsdp", [(i, i ^ m) for i in range(n_fs)]) for m in range(1, n_fs)]
+        weights = [first_w, later_w]
 
         pos = table[:, :, 0, :].astype(jnp.int32)
         r = table[:, :, 1, :]
@@ -695,8 +709,8 @@
         hit = expert_ids.T[:, None, :] == jnp.arange(experts, dtype=jnp.int32)[None, :, None]
         route_grad = jnp.sum(jnp.where(hit, dr_home[None], 0.0), axis=1).T
         grads = None
-        for k in range(n_loc):
-            grads = place(k, n_loc, me.reshape(1), pieces[k], grads)
+        for ks in (tuple(range(n_loc // 2)), tuple(range(n_loc // 2, n_loc))):
+            grads = place(ks, n_loc, me.reshape(1), [piece for k in ks for piece in pieces[k]], grads)
         return grad_x, route_grad, *grads
 
     return jax.shard_map(

time: 804 us -> 860 us (1.070)
  Pallas kernels: 568 us -> 665 us
  starting transfers between devices: 56.1 us -> 18.9 us
    pallas_call x1, Pallas kernels: 216 us -> 297 us  [collect(): pl.pallas_call(functools.partial(collect_kernel, n_fs, n_ep, parts), out_...]
    ppermute x6 -> x3, waiting for transfers between devices: 71 us -> 33.4 us  [body(): lax.ppermute(later_w[m - 1], 'fsdp', [(i, i ^ m) for i in range(n_fs)])]
    ppermute x12, waiting for transfers between devices: 76.7 us -> 112 us  [body(): lax.ppermute(slices[m], 'fsdp', [(i, i ^ m) for i in range(n_fs)])]
    ppermute x12, starting transfers between devices: 49.1 us -> 15.4 us  [body(): lax.ppermute(slices[m], 'fsdp', [(i, i ^ m) for i in range(n_fs)])]
    pallas_call x1, Pallas kernels: 131 us -> 151 us  [spread(): pl.pallas_call(functools.partial(spread_kernel, n_fs, n_ep, n_loc, parts)...]
    pallas_call x4 -> x2, Pallas kernels: 25.9 us -> 22.4 us  [place(): pl.pallas_call(functools.partial(place_kernel, n_fs, n_loc, ks, first), o...]
  transfers between devices with their start and end apart: 18 -> 15, of which waited for: 5 -> 6; matrix products, arithmetic and copies ran while one was open for 2% -> 1% of each run, Pallas kernels for 54% -> 59%
where the time goes in v6:
time: 860 us; the launch traced here: 851 us
  Pallas kernels  665 us (77%)
  waiting for transfers between devices  145 us (17%)
  starting transfers between devices  18.9 us (2%)
  local copies, waits for them, and re-layouts  8.69 us (1%)
  other arithmetic  8.68 us (1%)
    pallas_call x1, Pallas kernels, collect(): pl.pallas_call(functools.partial(collect_kernel, n_fs, n_ep, parts), out_...  297 us
    pallas_call x1, Pallas kernels, spread(): pl.pallas_call(functools.partial(spread_kernel, n_fs, n_ep, n_loc, parts)...  151 us
    pallas_call x4, Pallas kernels, expert_call(): pl.pallas_call(functools.partial(expert_kernel, n_fs), out_shape=[jax.Sha...  118 us
    ppermute x12, waiting for transfers between devices, body(): lax.ppermute(slices[m], 'fsdp', [(i, i ^ m) for i in range(n_fs)])  112 us
    pallas_call x2, Pallas kernels, gather_rows(): pl.pallas_call(functools.partial(gather_kernel, n_src, n_loc, region, up(...  48.2 us
    ppermute x3, waiting for transfers between devices, body(): lax.ppermute(later_w[m - 1], 'fsdp', [(i, i ^ m) for i in range(n_fs)])  33.4 us
    pallas_call x1, Pallas kernels, combine_rows(): pl.pallas_call(functools.partial(combine_kernel, n_src, n_loc, slots), ou...  28.8 us
    pallas_call x2, Pallas kernels, place(): pl.pallas_call(functools.partial(place_kernel, n_fs, n_loc, ks, first), o...  22.4 us
  transfers between devices with their start and end apart: 15, of which 6 were waited for; matrix products, arithmetic and copies ran while one was open for 1% of the time, Pallas kernels for 59%

profile of v6, /device:TPU:0, one launch (start us, length us, event | category | flops | bytes accessed | tf_op | source)
XLA Modules:
  0.0 850.6 jit_solution(9928313320228078342)
XLA Ops:
  0.7 1.1 fusion.1
  2.7 0.4 copy.21
  3.2 1.2 reshape.47.table_ref
  4.3 151.3 %spread.1 = (bf16[16384,1024]{1,0:T(8,128)(2,1)}, f32[16,8,1024]{2,1,0:T(8,128)}, bf16[4,128,1280]{2,1,0:T(8,128)(2,1)}, bf16[1,3,128,1280]{3,2,1,0:T(8,128)(2,1...) custom-call(bf16[1024,512]{1,0:T(8,128)(2,1)} %x_ref.1, ...), custom_call_target="tpu_custom_call" | custom-call | bytes 67108864 | tf_op jit(solution)/shard_map/spread/pallas_call | solution.py:560
  155.7 0.6 collective-permute-start
  156.3 1.3 collective-permute-start.1
  157.6 1.6 collective-permute-start.2
  159.2 1.3 copy.22
  161.0 0.9 fusion.2.refs_2_.pos_ref
  161.8 0.9 copy.35
  162.7 0.6 add.54.refs_0_.cnt
  163.4 0.7 fusion.11
  164.9 0.6 fusion.8.refs_1_.off
  165.5 21.3 %gather_x.1.x_ref = bf16[26624,512]{1,0:T(8,128)(2,1)} custom-call(s32[64]{0:T(128)} %add.54.refs_0_.cnt, s32[64]{0:T(128)} %fusion.8.refs_1_.off, s32[16,4,1024]{2,1,0:T(4,128)} %fusion.2.refs_2_.pos_ref, bf16[16384,1024]{1,0:T(8,128)(2,1)} %get-tuple-element.51.refs_3_.refs_4_), custom_call_target="tpu_custom_call" | custom-call | flops 12582912000 | bytes 33554432 | tf_op jit(solution)/shard_map/gather_x/pallas_call | solution.py:161
  186.8 26.9 %gather_r.1 = (bf16[26624,512]{1,0:T(8,128)(2,1)}, f32[26624,128]{1,0:T(8,128)}) custom-call(s32[64]{0:T(128)} %add.54.refs_0_.cnt, s32[64]{0:T(128)} %fusion.8.refs_1_.off, s32[16,4,1024]{2,1,0:T(4,128)} %fusion.2.refs_2_.pos_ref, f32[16,4,1024]{2,1,0:T(4,128)} %bitcast.30, bf16[16384,1024]{1,0:T(8,128)(2,1)} %get-tuple-element.51.refs_3_.refs_4_), custom_call_target="tpu_custom_call" | custom-call | flops 12582912000 | bytes 33554432 | tf_op jit(solution)/shard_map/gather_r/pallas_call | solution.py:161
  213.7 1.2 add_add_fusion.info
  214.9 29.3 %shard_map.110 = (bf16[6656,512]{1,0:T(8,128)(2,1)}, f32[6656,128]{1,0:T(8,128)}, f32[3,128,1280]{2,1,0:T(8,128)}, f32[3,128,1280]{2,1,0:T(8,128)}, f32[3,128,1280]{2,1,0:T(8,128)}, /*index=5*/f32[3,128,1280]{2,1,0:T(8,128)}) custom-call(s32[3]{0:T(128)} %add_add_fusion.info, bf16[26624,512]{1,0:T(8,128)(2,1)} %gather_x.1.x_ref, ...), custom_call_target="tpu_custom_call" | custom-call | flops 35389440000 | bytes 15728640 | tf_op jit(solution)/shard_map/pallas_call | solution.py:244
  244.2 0.6 collective-permute-start.9
  244.9 1.3 collective-permute-start.10
  248.1 1.3 add_add_fusion.3.info
  249.4 1.8 add_add_fusion.1
  251.3 1.6 collective-permute-start.11
  252.9 32.5 %collective-permute-done.1.refs_4_ = bf16[3,3,128,1280]{3,2,1,0:T(8,128)(2,1)} collective-permute-done((bf16[3,3,128,1280]{3,2,1,0:T(8,128)(2,1)}, bf16[3,3,128,1280]{3,2,1,0:T(8,128)(2,1)}, u32[]{:S(2)}, u32[]{:S(2)}) %collective-permute-start.1) | collective-permute-done | bytes 2949152 | tf_op jit(solution)/shard_map/ppermute | solution.py:683
  285.4 0.9 collective-permute-done.2.refs_5_
  286.3 29.5 %shard_map.113 = (bf16[6656,512]{1,0:T(8,128)(2,1)}, f32[6656,128]{1,0:T(8,128)}, f32[3,128,1280]{2,1,0:T(8,128)}, f32[3,128,1280]{2,1,0:T(8,128)}, f32[3,128,1280]{2,1,0:T(8,128)}, /*index=5*/f32[3,128,1280]{2,1,0:T(8,128)}) custom-call(s32[3]{0:T(128)} %add_add_fusion.3.info, bf16[26624,512]{1,0:T(8,128)(2,1)} %gather_x.1.x_ref, ...), custom_call_target="tpu_custom_call" | custom-call | flops 35389440000 | bytes 15728640 | tf_op jit(solution)/shard_map/pallas_call | solution.py:244
  315.8 1.3 collective-permute-start.6
  317.1 29.4 %shard_map.111 = (bf16[6656,512]{1,0:T(8,128)(2,1)}, f32[6656,128]{1,0:T(8,128)}, f32[3,128,1280]{2,1,0:T(8,128)}, f32[3,128,1280]{2,1,0:T(8,128)}, f32[3,128,1280]{2,1,0:T(8,128)}, /*index=5*/f32[3,128,1280]{2,1,0:T(8,128)}) custom-call(s32[3]{0:T(128)} %get-tuple-element.105.info, bf16[26624,512]{1,0:T(8,128)(2,1)} %gather_x.1.x_ref, ...), custom_call_target="tpu_custom_call" | custom-call | flops 35389440000 | bytes 15728640 | tf_op jit(solution)/shard_map/pallas_call | solution.py:244
  346.5 0.8 collective-permute-start.12
  347.3 1.2 collective-permute-start.13
  348.5 20.8 %collective-permute-done.10.refs_2_ = f32[3,128,1280]{2,1,0:T(8,128)} collective-permute-done((f32[3,128,1280]{2,1,0:T(8,128)}, f32[3,128,1280]{2,1,0:T(8,128)}, u32[]{:S(2)}, u32[]{:S(2)}) %collective-permute-start.10) | collective-permute-done | bytes 1966112 | tf_op jit(solution)/shard_map/ppermute | solution.py:704
  369.2 1.7 collective-permute-start.14
  370.9 29.4 %shard_map.112 = (bf16[6656,512]{1,0:T(8,128)(2,1)}, f32[6656,128]{1,0:T(8,128)}, f32[3,128,1280]{2,1,0:T(8,128)}, f32[3,128,1280]{2,1,0:T(8,128)}, f32[3,128,1280]{2,1,0:T(8,128)}, /*index=5*/f32[3,128,1280]{2,1,0:T(8,128)}) custom-call(s32[3]{0:T(128)} %get-tuple-element.106.info, bf16[26624,512]{1,0:T(8,128)(2,1)} %gather_x.1.x_ref, ...), custom_call_target="tpu_custom_call" | custom-call | flops 35389440000 | bytes 15728640 | tf_op jit(solution)/shard_map/pallas_call | solution.py:244
  400.3 1.7 collective-permute-start.7
  402.0 10.5 %collective-permute-done.6.refs_5_ = f32[3,128,1280]{2,1,0:T(8,128)} collective-permute-done((f32[3,128,1280]{2,1,0:T(8,128)}, f32[3,128,1280]{2,1,0:T(8,128)}, u32[]{:S(2)}, u32[]{:S(2)}) %collective-permute-start.6) | collective-permute-done | bytes 1966112 | tf_op jit(solution)/shard_map/ppermute | solution.py:704
  412.5 1.3 collective-permute-start.8
  413.8 40.8 %collective-permute-done.12.refs_5_ = f32[3,128,1280]{2,1,0:T(8,128)} collective-permute-done((f32[3,128,1280]{2,1,0:T(8,128)}, f32[3,128,1280]{2,1,0:T(8,128)}, u32[]{:S(2)}, u32[]{:S(2)}) %collective-permute-start.12) | collective-permute-done | bytes 1966112 | tf_op jit(solution)/shard_map/ppermute | solution.py:704
  454.6 0.6 collective-permute-start.3
  455.2 1.3 collective-permute-start.4
  456.5 39.7 %collective-permute-done.14.refs_7_ = f32[3,128,1280]{2,1,0:T(8,128)} collective-permute-done((f32[3,128,1280]{2,1,0:T(8,128)}, f32[3,128,1280]{2,1,0:T(8,128)}, u32[]{:S(2)}, u32[]{:S(2)}) %collective-permute-start.14) | collective-permute-done | bytes 1966112 | tf_op jit(solution)/shard_map/ppermute | solution.py:704
  496.2 2.0 collective-permute-start.5
  498.2 28.8 %combine.1 = (f32[16384,512]{1,0:T(8,128)}, f32[16,4,1024]{2,1,0:T(4,128)}) custom-call(s32[64]{0:T(128)} %add.54.refs_0_.cnt, s32[64]{0:T(128)} %fusion.8.refs_1_.off, s32[16,4,1024]{2,1,0:T(4,128)} %fusion.2.refs_2_.pos_ref, bf16[6656,512]{1,0:T(8,128)(2,1)} %get-tuple-element.58.refs_0_, bf16[6656,512]{1,0:T(8,128)(2,1)} %get-tuple-element.62.refs_1_, ...), custom_call_target="tpu_custom_call" | custom-call | flops 12582912000 | bytes 33554432 | tf_op jit(solution)/shard_map/combine/pallas_call | solution.py:381
  527.0 296.5 %collect.1 = (bf16[1024,512]{1,0:T(8,128)(2,1)}, f32[16,4,1024]{2,1,0:T(4,128)}) custom-call(f32[16384,512]{1,0:T(8,128)} %get-tuple-element.69.part_ref, f32[16,4,1024]{2,1,0:T(4,128)} %get-tuple-element.70.dr_ref), custom_call_target="tpu_custom_call" | custom-call | bytes 67108864 | tf_op jit(solution)/shard_map/collect/pallas_call | solution.py:648
  823.6 1.0 copy.36
  824.6 0.9 select_reduce_fusion
  825.5 11.1 %shard_map.114 = (f32[16,128,1280]{2,1,0:T(8,128)}, f32[16,128,1280]{2,1,0:T(8,128)}, f32[16,1280,128]{2,1,0:T(8,128)}) custom-call(s32[1]{0:T(128)} %bitcast.7.me, f32[3,128,1280]{2,1,0:T(8,128)} %get-tuple-element.81.refs_0_, f32[3,128,1280]{2,1,0:T(8,128)} %copy-done, f32[3,128,1280]{2,1,0:T(8,128)} %collective-permute-done.10.refs_2_, ...), custom_call_target="tpu_custom_call" | custom-call | bytes 31457280 | tf_op jit(solution)/shard_map/pallas_call | solution.py:289
  836.7 1.2 copy-done.1
  837.9 11.3 %shard_map.115 = (f32[16,128,1280]{2,1,0:T(8,128)}, f32[16,128,1280]{2,1,0:T(8,128)}, f32[16,1280,128]{2,1,0:T(8,128)}) custom-call(s32[1]{0:T(128)} %bitcast.7.me, f32[3,128,1280]{2,1,0:T(8,128)} %get-tuple-element.73.refs_0_, f32[3,128,1280]{2,1,0:T(8,128)} %collective-permute-done.3.refs_1_, ...), custom_call_target="tpu_custom_call", output_to_operand_aliasing={{0}: (9, {}), {1}: (10, {}), {2}: (11, {})} | custom-call | bytes 31457280 | tf_op jit(solution)/shard_map/pallas_call | solution.py:289
  849.2 1.0 copy.41
  (32 shorter events, 1.7 us)
Async XLA Ops:
  0.6 1.6 copy-start.3
  0.6 1.6 copy-start.5
  155.7 95.6 %collective-permute-start = (bf16[3,3,128,1280]{3,2,1,0:T(8,128)(2,1)}, bf16[3,3,128,1280]{3,2,1,0:T(8,128)(2,1)}, u32[]{:S(2)}, u32[]{:S(2)}) collective-permute-start(bf16[3,3,128,1280]{3,2,1,0:T(8,128)(2,1)} %get-tuple-element.59), channel_id=1, source_target_pairs={{0,4},{4,0},{8,12},{12,8},{1,5},{5,1},{9,13},{13,9},{2,6},{6,2},{1... | collective-permute-start | bytes 8847368 | tf_op jit(solution)/shard_map/ppermute | solution.py:683
  156.3 129.1 %collective-permute-start.1 = (bf16[3,3,128,1280]{3,2,1,0:T(8,128)(2,1)}, bf16[3,3,128,1280]{3,2,1,0:T(8,128)(2,1)}, u32[]{:S(2)}, u32[]{:S(2)}) collective-permute-start(bf16[3,3,128,1280]{3,2,1,0:T(8,128)(2,1)} %get-tuple-element.60), channel_id=1, source_target_pairs={{0,8},{4,12},{8,0},{12,4},{1,9},{5,13},{9,1},{13,5},{2,10},{6,14},... | collective-permute-start | bytes 8847368 | tf_op jit(solution)/shard_map/ppermute | solution.py:683
  157.6 128.7 %collective-permute-start.2 = (bf16[3,3,128,1280]{3,2,1,0:T(8,128)(2,1)}, bf16[3,3,128,1280]{3,2,1,0:T(8,128)(2,1)}, u32[]{:S(2)}, u32[]{:S(2)}) collective-permute-start(bf16[3,3,128,1280]{3,2,1,0:T(8,128)(2,1)} %get-tuple-element.61), channel_id=1, source_target_pairs={{0,12},{4,8},{8,4},{12,0},{1,13},{5,9},{9,5},{13,1},{2,14},{6,10},... | collective-permute-start | bytes 8847368 | tf_op jit(solution)/shard_map/ppermute | solution.py:683
  244.2 103.0 %collective-permute-start.9 = (f32[3,128,1280]{2,1,0:T(8,128)}, f32[3,128,1280]{2,1,0:T(8,128)S(1)}, u32[]{:S(2)}, u32[]{:S(2)}) collective-permute-start(f32[3,128,1280]{2,1,0:T(8,128)} %get-tuple-element.82), channel_id=1, source_target_pairs={{0,4},{4,0},{8,12},{12,8},{1,5},{5,1},{9,13},{13,9},{2,6},{6,2},{1... | collective-permute-start | bytes 5898248 | tf_op jit(solution)/shard_map/ppermute | solution.py:704
  244.9 124.4 %collective-permute-start.10 = (f32[3,128,1280]{2,1,0:T(8,128)}, f32[3,128,1280]{2,1,0:T(8,128)}, u32[]{:S(2)}, u32[]{:S(2)}) collective-permute-start(f32[3,128,1280]{2,1,0:T(8,128)} %get-tuple-element.83), channel_id=1, source_target_pairs={{0,8},{4,12},{8,0},{12,4},{1,9},{5,13},{9,1},{13,5},{2,10},{6,14},... | collective-permute-start | bytes 5898248 | tf_op jit(solution)/shard_map/ppermute | solution.py:704
  251.3 149.0 %collective-permute-start.11 = (f32[3,128,1280]{2,1,0:T(8,128)}, f32[3,128,1280]{2,1,0:T(8,128)}, u32[]{:S(2)}, u32[]{:S(2)}) collective-permute-start(f32[3,128,1280]{2,1,0:T(8,128)} %get-tuple-element.84), channel_id=1, source_target_pairs={{0,12},{4,8},{8,4},{12,0},{1,13},{5,9},{9,5},{13,1},{2,14},{6,10},... | collective-permute-start | bytes 5898248 | tf_op jit(solution)/shard_map/ppermute | solution.py:704
  315.8 96.6 %collective-permute-start.6 = (f32[3,128,1280]{2,1,0:T(8,128)}, f32[3,128,1280]{2,1,0:T(8,128)}, u32[]{:S(2)}, u32[]{:S(2)}) collective-permute-start(f32[3,128,1280]{2,1,0:T(8,128)} %get-tuple-element.78), channel_id=1, source_target_pairs={{0,4},{4,0},{8,12},{12,8},{1,5},{5,1},{9,13},{13,9},{2,6},{6,2},{1... | collective-permute-start | bytes 5898248 | tf_op jit(solution)/shard_map/ppermute | solution.py:704
  346.5 108.1 %collective-permute-start.12 = (f32[3,128,1280]{2,1,0:T(8,128)}, f32[3,128,1280]{2,1,0:T(8,128)}, u32[]{:S(2)}, u32[]{:S(2)}) collective-permute-start(f32[3,128,1280]{2,1,0:T(8,128)} %get-tuple-element.86), channel_id=1, source_target_pairs={{0,4},{4,0},{8,12},{12,8},{1,5},{5,1},{9,13},{13,9},{2,6},{6,2},{1... | collective-permute-start | bytes 5898248 | tf_op jit(solution)/shard_map/ppermute | solution.py:704
  347.3 53.0 %copy-start = (f32[3,128,1280]{2,1,0:T(8,128)}, f32[3,128,1280]{2,1,0:T(8,128)S(1)}, u32[]{:S(2)}) copy-start(f32[3,128,1280]{2,1,0:T(8,128)S(1)} %collective-permute-done.9.refs_1_) | copy-start | bytes 5898244
  347.3 107.9 %collective-permute-start.13 = (f32[3,128,1280]{2,1,0:T(8,128)}, f32[3,128,1280]{2,1,0:T(8,128)}, u32[]{:S(2)}, u32[]{:S(2)}) collective-permute-start(f32[3,128,1280]{2,1,0:T(8,128)} %get-tuple-element.87), channel_id=1, source_target_pairs={{0,8},{4,12},{8,0},{12,4},{1,9},{5,13},{9,1},{13,5},{2,10},{6,14},... | collective-permute-start | bytes 5898248 | tf_op jit(solution)/shard_map/ppermute | solution.py:704
  369.2 127.0 %collective-permute-start.14 = (f32[3,128,1280]{2,1,0:T(8,128)}, f32[3,128,1280]{2,1,0:T(8,128)}, u32[]{:S(2)}, u32[]{:S(2)}) collective-permute-start(f32[3,128,1280]{2,1,0:T(8,128)} %get-tuple-element.88), channel_id=1, source_target_pairs={{0,12},{4,8},{8,4},{12,0},{1,13},{5,9},{9,5},{13,1},{2,14},{6,10},... | collective-permute-start | bytes 5898248 | tf_op jit(solution)/shard_map/ppermute | solution.py:704
  400.3 436.3 %collective-permute-start.7 = (f32[3,128,1280]{2,1,0:T(8,128)}, f32[3,128,1280]{2,1,0:T(8,128)S(1)}, u32[]{:S(2)}, u32[]{:S(2)}) collective-permute-start(f32[3,128,1280]{2,1,0:T(8,128)} %get-tuple-element.79), channel_id=1, source_target_pairs={{0,8},{4,12},{8,0},{12,4},{1,9},{5,13},{9,1},{13,5},{2,10},{6,14},... | collective-permute-start | bytes 5898248 | tf_op jit(solution)/shard_map/ppermute | solution.py:704
  412.5 424.2 %collective-permute-start.8 = (f32[3,128,1280]{2,1,0:T(8,128)}, f32[3,128,1280]{2,1,0:T(8,128)}, u32[]{:S(2)}, u32[]{:S(2)}) collective-permute-start(f32[3,128,1280]{2,1,0:T(8,128)} %get-tuple-element.80), channel_id=1, source_target_pairs={{0,12},{4,8},{8,4},{12,0},{1,13},{5,9},{9,5},{13,1},{2,14},{6,10},... | collective-permute-start | bytes 5898248 | tf_op jit(solution)/shard_map/ppermute | solution.py:704
  454.6 382.1 %collective-permute-start.3 = (f32[3,128,1280]{2,1,0:T(8,128)}, f32[3,128,1280]{2,1,0:T(8,128)}, u32[]{:S(2)}, u32[]{:S(2)}) collective-permute-start(f32[3,128,1280]{2,1,0:T(8,128)} %get-tuple-element.74), channel_id=1, source_target_pairs={{0,4},{4,0},{8,12},{12,8},{1,5},{5,1},{9,13},{13,9},{2,6},{6,2},{1... | collective-permute-start | bytes 5898248 | tf_op jit(solution)/shard_map/ppermute | solution.py:704
  455.2 381.5 %collective-permute-start.4 = (f32[3,128,1280]{2,1,0:T(8,128)}, f32[3,128,1280]{2,1,0:T(8,128)}, u32[]{:S(2)}, u32[]{:S(2)}) collective-permute-start(f32[3,128,1280]{2,1,0:T(8,128)} %get-tuple-element.75), channel_id=1, source_target_pairs={{0,8},{4,12},{8,0},{12,4},{1,9},{5,13},{9,1},{13,5},{2,10},{6,14},... | collective-permute-start | bytes 5898248 | tf_op jit(solution)/shard_map/ppermute | solution.py:704
  496.2 340.5 %collective-permute-start.5 = (f32[3,128,1280]{2,1,0:T(8,128)}, f32[3,128,1280]{2,1,0:T(8,128)}, u32[]{:S(2)}, u32[]{:S(2)}) collective-permute-start(f32[3,128,1280]{2,1,0:T(8,128)} %get-tuple-element.76), channel_id=1, source_target_pairs={{0,12},{4,8},{8,4},{12,0},{1,13},{5,9},{9,5},{13,1},{2,14},{6,10},... | collective-permute-start | bytes 5898248 | tf_op jit(solution)/shard_map/ppermute | solution.py:704
  527.0 297.6 %copy-start.4 = (s32[1024,8]{0,1:T(8,128)S(1)}, s32[1024,8]{0,1:T(8,128)}, u32[]{:S(2)}) copy-start(s32[1024,8]{0,1:T(8,128)} %param.9) | copy-start | bytes 98308
  836.7 1.3 copy-start.1
  837.9 11.3 %copy-start.2 = (bf16[1024,512]{1,0:T(8,128)(2,1)S(1)}, bf16[1024,512]{1,0:T(8,128)(2,1)}, u32[]{:S(2)}) copy-start(bf16[1024,512]{1,0:T(8,128)(2,1)} %get-tuple-element.112) | copy-start | bytes 3145732

commit v7 on v6

--- a/solution.py
+++ b/solution.py
@@ -448,7 +448,7 @@
 
 
 def spread_kernel(n_fs, n_ep, n_loc, parts, x_ref, dy_ref, table_ref, wg_ref, wu_ref, wd_ref, full, table_all, *refs):
-    n_out = 2 * (n_fs - 1)
+    n_out = 3 * (n_fs - 1)
     own_down, w_out, refs = refs[0], refs[1:n_out + 1], refs[n_out + 1:]
     own, send, recv, c_send, c_recv, t_send, t_recv, own_sem, w_buf, down_buf, in_sem, out_sem, w_send, w_recv = refs
     tok, d = x_ref.shape
@@ -518,7 +518,8 @@
         elif k == 0:
             continue
         else:
-            copy = pltpu.make_async_copy(w_buf.at[n], w_out[n_fs + m - 2].at[k - 1], out_sem.at[n])
+            group = min(k, 2)
+            copy = pltpu.make_async_copy(w_buf.at[n], w_out[group * (n_fs - 1) + m - 1].at[k - group], out_sem.at[n])
         copy.start()
         local.append(copy)
     for phase in range(3):
@@ -553,7 +554,7 @@
     tok, d = x_tok.shape
     exp_local, dsl, f = w_gate.shape
     n_loc = exp_local // n_fs
-    n_slices, groups = n_loc * n_fs, [1] * (n_fs - 1) + [n_loc - 1] * (n_fs - 1)
+    n_slices, groups = n_loc * n_fs, [1] * (2 * n_fs - 2) + [n_loc - 2] * (n_fs - 1)
     parts = parts_of(tok)
     vmem, hbm = pl.BlockSpec(memory_space=pltpu.VMEM), pl.BlockSpec(memory_space=pl.ANY)
     dma = pltpu.SemaphoreType.DMA
@@ -679,9 +680,10 @@
         xdy_all, table, own_down, *packed = spread(x_tok, dy_tok, table, w_gate, w_up, w_down, n_fs, n_ep)
         table = table.reshape(n_dev, n_loc, 2, tok)
         me = lax.axis_index("fsdp").astype(jnp.int32)
-        first_w, later_w = packed[:n_fs - 1], packed[n_fs - 1:]
-        later_w = [lax.ppermute(later_w[m - 1], "fsdp", [(i, i ^ m) for i in range(n_fs)]) for m in range(1, n_fs)]
-        weights = [first_w, later_w]
+        weights = [packed[:n_fs - 1]]
+        for group in (1, 2):
+            weights.append([lax.ppermute(packed[group * (n_fs - 1) + m - 1], "fsdp", [(i, i ^ m) for i in range(n_fs)])
+                            for m in range(1, n_fs)])
 
         pos = table[:, :, 0, :].astype(jnp.int32)
         r = table[:, :, 1, :]
@@ -697,8 +699,8 @@
         for k in range(n_loc):
             info = jnp.stack([rows[k], jnp.maximum(1, blocks(rows[k], TILE)), me])
             dxk, drk, *slices = expert_call(
-                k, max(k - 1, 0), n_loc, info, x_pool, dy_pool, r_pool, (w_gate, w_up, own_down),
-                weights[min(k, 1)], region)
+                k, max(k - 2, 0), n_loc, info, x_pool, dy_pool, r_pool, (w_gate, w_up, own_down),
+                weights[min(k, 2)], region)
             dx_pools.append(dxk)
             dr_pools.append(drk)
             pieces.append([slices[0]] + [lax.ppermute(slices[m], "fsdp", [(i, i ^ m) for i in range(n_fs)])

time: 860 us -> 821 us (0.955)
  Pallas kernels: 665 us -> 616 us
  starting transfers between devices: 18.9 us -> 61.1 us
  waiting for transfers between devices: 145 us -> 110 us
    pallas_call x1, Pallas kernels: 297 us -> 247 us  [collect(): pl.pallas_call(functools.partial(collect_kernel, n_fs, n_ep, parts), out_...]
    ppermute x12, starting transfers between devices: 15.4 us -> 54.1 us  [body(): lax.ppermute(slices[m], 'fsdp', [(i, i ^ m) for i in range(n_fs)])]
    ppermute x3 -> x6, waiting for transfers between devices: 33.4 us -> 0.02 us  [body(): lax.ppermute(packed[group * (n_fs - 1) + m - 1], 'fsdp', [(i, i ^ m) for...]
  transfers between devices with their start and end apart: 15 -> 18, of which waited for: 6 -> 6; matrix products, arithmetic and copies ran while one was open for 1% -> 1% of each run, Pallas kernels for 59% -> 56%
where the time goes in v7:
time: 821 us; the launch traced here: 812 us
  Pallas kernels  616 us (75%)
  waiting for transfers between devices  110 us (13%)
  starting transfers between devices  61.1 us (7%)
  local copies, waits for them, and re-layouts  10.7 us (1%)
  other arithmetic  9.39 us (1%)
    pallas_call x1, Pallas kernels, collect(): pl.pallas_call(functools.partial(collect_kernel, n_fs, n_ep, parts), out_...  247 us
    pallas_call x1, Pallas kernels, spread(): pl.pallas_call(functools.partial(spread_kernel, n_fs, n_ep, n_loc, parts)...  151 us
    pallas_call x4, Pallas kernels, expert_call(): pl.pallas_call(functools.partial(expert_kernel, n_fs), out_shape=[jax.Sha...  118 us
    ppermute x12, waiting for transfers between devices, body(): lax.ppermute(slices[m], 'fsdp', [(i, i ^ m) for i in range(n_fs)])  110 us
    ppermute x12, starting transfers between devices, body(): lax.ppermute(slices[m], 'fsdp', [(i, i ^ m) for i in range(n_fs)])  54.1 us
    pallas_call x2, Pallas kernels, gather_rows(): pl.pallas_call(functools.partial(gather_kernel, n_src, n_loc, region, up(...  48.2 us
    pallas_call x1, Pallas kernels, combine_rows(): pl.pallas_call(functools.partial(combine_kernel, n_src, n_loc, slots), ou...  28.9 us
    pallas_call x2, Pallas kernels, place(): pl.pallas_call(functools.partial(place_kernel, n_fs, n_loc, ks, first), o...  22.4 us
  transfers between devices with their start and end apart: 18, of which 6 were waited for; matrix products, arithmetic and copies ran while one was open for 1% of the time, Pallas kernels for 56%

profile of v7, /device:TPU:0, one launch (start us, length us, event | category | flops | bytes accessed | tf_op | source)
XLA Modules:
  0.0 811.5 jit_solution(14243881175406503926)
XLA Ops:
  0.6 1.0 fusion.1
  1.7 1.0 select_reduce_fusion.1
  3.8 1.2 reshape.47.table_ref
  5.0 151.3 %spread.1 = (bf16[16384,1024]{1,0:T(8,128)(2,1)}, f32[16,8,1024]{2,1,0:T(8,128)}, bf16[4,128,1280]{2,1,0:T(8,128)(2,1)}, bf16[1,3,128,1280]{3,2,1,0:T(8,128)(2,1...) custom-call(bf16[1024,512]{1,0:T(8,128)(2,1)} %x_ref.1, ...), custom_call_target="tpu_custom_call" | custom-call | bytes 67108864 | tf_op jit(solution)/shard_map/spread/pallas_call | solution.py:561
  156.3 0.6 collective-permute-start
  157.0 1.3 collective-permute-start.1
  158.3 1.6 collective-permute-start.2
  160.5 1.3 collective-permute-start.4
  161.8 1.3 copy.22
  163.6 0.9 fusion.2.refs_2_.pos_ref
  164.5 0.6 add.54.refs_0_.cnt
  165.1 0.6 fusion.11
  166.6 0.9 copy.35
  168.0 21.4 %gather_x.1.x_ref = bf16[26624,512]{1,0:T(8,128)(2,1)} custom-call(s32[64]{0:T(128)} %add.54.refs_0_.cnt, s32[64]{0:T(128)} %fusion.8.refs_1_.off, s32[16,4,1024]{2,1,0:T(4,128)} %fusion.2.refs_2_.pos_ref, bf16[16384,1024]{1,0:T(8,128)(2,1)} %get-tuple-element.54.refs_3_.refs_4_), custom_call_target="tpu_custom_call" | custom-call | flops 12582912000 | bytes 33554432 | tf_op jit(solution)/shard_map/gather_x/pallas_call | solution.py:161
  189.4 26.8 %gather_r.1 = (bf16[26624,512]{1,0:T(8,128)(2,1)}, f32[26624,128]{1,0:T(8,128)}) custom-call(s32[64]{0:T(128)} %add.54.refs_0_.cnt, s32[64]{0:T(128)} %fusion.8.refs_1_.off, s32[16,4,1024]{2,1,0:T(4,128)} %fusion.2.refs_2_.pos_ref, f32[16,4,1024]{2,1,0:T(4,128)} %bitcast.30, bf16[16384,1024]{1,0:T(8,128)(2,1)} %get-tuple-element.54.refs_3_.refs_4_), custom_call_target="tpu_custom_call" | custom-call | flops 12582912000 | bytes 33554432 | tf_op jit(solution)/shard_map/gather_r/pallas_call | solution.py:161
  216.1 1.3 add_add_fusion.info
  217.4 29.4 %shard_map.110 = (bf16[6656,512]{1,0:T(8,128)(2,1)}, f32[6656,128]{1,0:T(8,128)}, f32[3,128,1280]{2,1,0:T(8,128)}, f32[3,128,1280]{2,1,0:T(8,128)}, f32[3,128,1280]{2,1,0:T(8,128)}, /*index=5*/f32[3,128,1280]{2,1,0:T(8,128)}) custom-call(s32[3]{0:T(128)} %add_add_fusion.info, bf16[26624,512]{1,0:T(8,128)(2,1)} %gather_x.1.x_ref, ...), custom_call_target="tpu_custom_call" | custom-call | flops 35389440000 | bytes 15728640 | tf_op jit(solution)/shard_map/pallas_call | solution.py:244
  248.7 1.3 add_add_fusion.1.info
  249.9 1.9 add_add_fusion.2
  251.8 1.6 collective-permute-start.5
  253.4 1.0 copy-done.6
  254.3 0.6 collective-permute-start.12
  255.0 1.0 copy-done.7
  255.9 1.3 collective-permute-start.13
  257.3 29.6 %shard_map.111 = (bf16[6656,512]{1,0:T(8,128)(2,1)}, f32[6656,128]{1,0:T(8,128)}, f32[3,128,1280]{2,1,0:T(8,128)}, f32[3,128,1280]{2,1,0:T(8,128)}, f32[3,128,1280]{2,1,0:T(8,128)}, /*index=5*/f32[3,128,1280]{2,1,0:T(8,128)}) custom-call(s32[3]{0:T(128)} %add_add_fusion.1.info, bf16[26624,512]{1,0:T(8,128)(2,1)} %gather_x.1.x_ref, ...), custom_call_target="tpu_custom_call" | custom-call | flops 35389440000 | bytes 15728640 | tf_op jit(solution)/shard_map/pallas_call | solution.py:244
  286.9 1.6 collective-permute-start.14
  288.5 0.6 collective-permute-start.15
  289.1 10.4 %collective-permute-start.16 = (f32[3,128,1280]{2,1,0:T(8,128)}, f32[3,128,1280]{2,1,0:T(8,128)}, u32[]{:S(2)}, u32[]{:S(2)}) collective-permute-start(f32[3,128,1280]{2,1,0:T(8,128)} %get-tuple-element.93), channel_id=1, source_target_pairs={{0,8},{4,12},{8,0},{12,4},{1,9},{5,13},{9,1},{13,5},{2,10},{6,14},... | collective-permute-start | bytes 5898248 | tf_op jit(solution)/shard_map/ppermute | solution.py:706
  299.5 29.3 %shard_map.112 = (bf16[6656,512]{1,0:T(8,128)(2,1)}, f32[6656,128]{1,0:T(8,128)}, f32[3,128,1280]{2,1,0:T(8,128)}, f32[3,128,1280]{2,1,0:T(8,128)}, f32[3,128,1280]{2,1,0:T(8,128)}, /*index=5*/f32[3,128,1280]{2,1,0:T(8,128)}) custom-call(s32[3]{0:T(128)} %get-tuple-element.111.info, bf16[26624,512]{1,0:T(8,128)(2,1)} %gather_x.1.x_ref, ...), custom_call_target="tpu_custom_call" | custom-call | flops 35389440000 | bytes 15728640 | tf_op jit(solution)/shard_map/pallas_call | solution.py:244
  328.8 11.2 %collective-permute-done.12.refs_1_ = f32[3,128,1280]{2,1,0:T(8,128)S(1)} collective-permute-done((f32[3,128,1280]{2,1,0:T(8,128)}, f32[3,128,1280]{2,1,0:T(8,128)S(1)}, u32[]{:S(2)}, u32[]{:S(2)}) %collective-permute-start.12) | collective-permute-done | bytes 1966112 | tf_op jit(solution)/shard_map/ppermute | solution.py:706
  340.0 1.7 collective-permute-start.17
  341.7 12.1 %collective-permute-done.13.refs_2_ = f32[3,128,1280]{2,1,0:T(8,128)} collective-permute-done((f32[3,128,1280]{2,1,0:T(8,128)}, f32[3,128,1280]{2,1,0:T(8,128)}, u32[]{:S(2)}, u32[]{:S(2)}) %collective-permute-start.13) | collective-permute-done | bytes 1966112 | tf_op jit(solution)/shard_map/ppermute | solution.py:706
  353.9 29.3 %shard_map.113 = (bf16[6656,512]{1,0:T(8,128)(2,1)}, f32[6656,128]{1,0:T(8,128)}, f32[3,128,1280]{2,1,0:T(8,128)}, f32[3,128,1280]{2,1,0:T(8,128)}, f32[3,128,1280]{2,1,0:T(8,128)}, /*index=5*/f32[3,128,1280]{2,1,0:T(8,128)}) custom-call(s32[3]{0:T(128)} %get-tuple-element.112.info, bf16[26624,512]{1,0:T(8,128)(2,1)} %gather_x.1.x_ref, ...), custom_call_target="tpu_custom_call" | custom-call | flops 35389440000 | bytes 15728640 | tf_op jit(solution)/shard_map/pallas_call | solution.py:244
  383.1 2.3 collective-permute-start.7
  385.4 39.0 %collective-permute-done.15.refs_5_ = f32[3,128,1280]{2,1,0:T(8,128)} collective-permute-done((f32[3,128,1280]{2,1,0:T(8,128)}, f32[3,128,1280]{2,1,0:T(8,128)}, u32[]{:S(2)}, u32[]{:S(2)}) %collective-permute-start.15) | collective-permute-done | bytes 1966112 | tf_op jit(solution)/shard_map/ppermute | solution.py:706
  424.4 1.7 collective-permute-start.8
  426.1 5.3 collective-permute-done.16.refs_6_
  431.4 2.2 collective-permute-done.17.refs_7_
  433.6 34.0 %collective-permute-start.10 = (f32[3,128,1280]{2,1,0:T(8,128)}, f32[3,128,1280]{2,1,0:T(8,128)}, u32[]{:S(2)}, u32[]{:S(2)}) collective-permute-start(f32[3,128,1280]{2,1,0:T(8,128)} %get-tuple-element.85), channel_id=1, source_target_pairs={{0,8},{4,12},{8,0},{12,4},{1,9},{5,13},{9,1},{13,5},{2,10},{6,14},... | collective-permute-start | bytes 5898248 | tf_op jit(solution)/shard_map/ppermute | solution.py:706
  467.5 40.7 %collective-permute-done.6.refs_1_ = f32[3,128,1280]{2,1,0:T(8,128)} collective-permute-done((f32[3,128,1280]{2,1,0:T(8,128)}, f32[3,128,1280]{2,1,0:T(8,128)}, u32[]{:S(2)}, u32[]{:S(2)}) %collective-permute-start.6) | collective-permute-done | bytes 1966112 | tf_op jit(solution)/shard_map/ppermute | solution.py:706
  508.2 28.9 %combine.1 = (f32[16384,512]{1,0:T(8,128)}, f32[16,4,1024]{2,1,0:T(4,128)}) custom-call(s32[64]{0:T(128)} %add.54.refs_0_.cnt, s32[64]{0:T(128)} %fusion.8.refs_1_.off, s32[16,4,1024]{2,1,0:T(4,128)} %fusion.2.refs_2_.pos_ref, bf16[6656,512]{1,0:T(8,128)(2,1)} %get-tuple-element.61.refs_0_, bf16[6656,512]{1,0:T(8,128)(2,1)} %get-tuple-element.65.refs_1_, ...), custom_call_target="tpu_custom_call" | custom-call | flops 12582912000 | bytes 33554432 | tf_op jit(solution)/shard_map/combine/pallas_call | solution.py:381
  537.1 247.2 %collect.1 = (bf16[1024,512]{1,0:T(8,128)(2,1)}, f32[16,4,1024]{2,1,0:T(4,128)}) custom-call(f32[16384,512]{1,0:T(8,128)} %get-tuple-element.75.part_ref, f32[16,4,1024]{2,1,0:T(4,128)} %get-tuple-element.76.dr_ref), custom_call_target="tpu_custom_call" | custom-call | bytes 67108864 | tf_op jit(solution)/shard_map/collect/pallas_call | solution.py:649
  784.4 1.0 copy.36
  785.5 0.9 select_reduce_fusion
  786.4 11.1 %shard_map.114 = (f32[16,128,1280]{2,1,0:T(8,128)}, f32[16,128,1280]{2,1,0:T(8,128)}, f32[16,1280,128]{2,1,0:T(8,128)}) custom-call(s32[1]{0:T(128)} %bitcast.7.me, f32[3,128,1280]{2,1,0:T(8,128)} %get-tuple-element.87.refs_0_, f32[3,128,1280]{2,1,0:T(8,128)} %copy-done, f32[3,128,1280]{2,1,0:T(8,128)} %collective-permute-done.13.refs_2_, ...), custom_call_target="tpu_custom_call" | custom-call | bytes 31457280 | tf_op jit(solution)/shard_map/pallas_call | solution.py:289
  797.5 1.3 copy-done.1
  798.8 11.3 %shard_map.115 = (f32[16,128,1280]{2,1,0:T(8,128)}, f32[16,128,1280]{2,1,0:T(8,128)}, f32[16,1280,128]{2,1,0:T(8,128)}) custom-call(s32[1]{0:T(128)} %bitcast.7.me, f32[3,128,1280]{2,1,0:T(8,128)} %get-tuple-element.79.refs_0_, f32[3,128,1280]{2,1,0:T(8,128)} %collective-permute-done.6.refs_1_, ...), custom_call_target="tpu_custom_call", output_to_operand_aliasing={{0}: (9, {}), {1}: (10, {}), {2}: (11, {})} | custom-call | bytes 31457280 | tf_op jit(solution)/shard_map/pallas_call | solution.py:289
  810.1 1.0 copy.41
  (42 shorter events, 3.0 us)
Async XLA Ops:
  156.3 95.5 %collective-permute-start = (bf16[1,3,128,1280]{3,2,1,0:T(8,128)(2,1)}, bf16[1,3,128,1280]{3,2,1,0:T(8,128)(2,1)S(1)}, u32[]{:S(2)}, u32[]{:S(2)}) collective-permute-start(bf16[1,3,128,1280]{3,2,1,0:T(8,128)(2,1)} %get-tuple-element.62), channel_id=1, source_target_pairs={{0,4},{4,0},{8,12},{12,8},{1,5},{5,1},{9,13},{13,9},{2,6},{6,2},{1... | collective-permute-start | bytes 2949128 | tf_op jit(solution)/shard_map/ppermute | solution.py:685
  157.0 96.4 %collective-permute-start.1 = (bf16[1,3,128,1280]{3,2,1,0:T(8,128)(2,1)}, bf16[1,3,128,1280]{3,2,1,0:T(8,128)(2,1)S(1)}, u32[]{:S(2)}, u32[]{:S(2)}) collective-permute-start(bf16[1,3,128,1280]{3,2,1,0:T(8,128)(2,1)} %get-tuple-element.63), channel_id=1, source_target_pairs={{0,8},{4,12},{8,0},{12,4},{1,9},{5,13},{9,1},{13,5},{2,10},{6,14},... | collective-permute-start | bytes 2949128 | tf_op jit(solution)/shard_map/ppermute | solution.py:685
  158.3 96.7 %collective-permute-start.2 = (bf16[1,3,128,1280]{3,2,1,0:T(8,128)(2,1)}, bf16[1,3,128,1280]{3,2,1,0:T(8,128)(2,1)S(1)}, u32[]{:S(2)}, u32[]{:S(2)}) collective-permute-start(bf16[1,3,128,1280]{3,2,1,0:T(8,128)(2,1)} %get-tuple-element.64), channel_id=1, source_target_pairs={{0,12},{4,8},{8,4},{12,0},{1,13},{5,9},{9,5},{13,1},{2,14},{6,10},... | collective-permute-start | bytes 2949128 | tf_op jit(solution)/shard_map/ppermute | solution.py:685
  159.9 127.0 %collective-permute-start.3 = (bf16[2,3,128,1280]{3,2,1,0:T(8,128)(2,1)}, bf16[2,3,128,1280]{3,2,1,0:T(8,128)(2,1)}, u32[]{:S(2)}, u32[]{:S(2)}) collective-permute-start(bf16[2,3,128,1280]{3,2,1,0:T(8,128)(2,1)} %get-tuple-element.66), channel_id=1, source_target_pairs={{0,4},{4,0},{8,12},{12,8},{1,5},{5,1},{9,13},{13,9},{2,6},{6,2},{1... | collective-permute-start | bytes 5898248 | tf_op jit(solution)/shard_map/ppermute | solution.py:685
  160.5 128.0 %collective-permute-start.4 = (bf16[2,3,128,1280]{3,2,1,0:T(8,128)(2,1)}, bf16[2,3,128,1280]{3,2,1,0:T(8,128)(2,1)}, u32[]{:S(2)}, u32[]{:S(2)}) collective-permute-start(bf16[2,3,128,1280]{3,2,1,0:T(8,128)(2,1)} %get-tuple-element.67), channel_id=1, source_target_pairs={{0,8},{4,12},{8,0},{12,4},{1,9},{5,13},{9,1},{13,5},{2,10},{6,14},... | collective-permute-start | bytes 5898248 | tf_op jit(solution)/shard_map/ppermute | solution.py:685
  251.8 1.6 copy-start.5
  251.8 37.3 %collective-permute-start.5 = (bf16[2,3,128,1280]{3,2,1,0:T(8,128)(2,1)}, bf16[2,3,128,1280]{3,2,1,0:T(8,128)(2,1)}, u32[]{:S(2)}, u32[]{:S(2)}) collective-permute-start(bf16[2,3,128,1280]{3,2,1,0:T(8,128)(2,1)} %get-tuple-element.68), channel_id=1, source_target_pairs={{0,12},{4,8},{8,4},{12,0},{1,13},{5,9},{9,5},{13,1},{2,14},{6,10},... | collective-permute-start | bytes 5898248 | tf_op jit(solution)/shard_map/ppermute | solution.py:685
  253.4 1.0 copy-start.6
  254.3 85.7 %collective-permute-start.12 = (f32[3,128,1280]{2,1,0:T(8,128)}, f32[3,128,1280]{2,1,0:T(8,128)S(1)}, u32[]{:S(2)}, u32[]{:S(2)}) collective-permute-start(f32[3,128,1280]{2,1,0:T(8,128)} %get-tuple-element.88), channel_id=1, source_target_pairs={{0,4},{4,0},{8,12},{12,8},{1,5},{5,1},{9,13},{13,9},{2,6},{6,2},{1... | collective-permute-start | bytes 5898248 | tf_op jit(solution)/shard_map/ppermute | solution.py:706
  255.0 1.0 copy-start.7
  255.9 30.9 %copy-start.4 = (f32[3,128,1280]{2,1,0:T(8,128)S(1)}, f32[3,128,1280]{2,1,0:T(8,128)}, u32[]{:S(2)}) copy-start(f32[3,128,1280]{2,1,0:T(8,128)} %get-tuple-element.90) | copy-start | bytes 5898244
  255.9 97.9 %collective-permute-start.13 = (f32[3,128,1280]{2,1,0:T(8,128)}, f32[3,128,1280]{2,1,0:T(8,128)}, u32[]{:S(2)}, u32[]{:S(2)}) collective-permute-start(f32[3,128,1280]{2,1,0:T(8,128)} %get-tuple-element.89), channel_id=1, source_target_pairs={{0,8},{4,12},{8,0},{12,4},{1,9},{5,13},{9,1},{13,5},{2,10},{6,14},... | collective-permute-start | bytes 5898248 | tf_op jit(solution)/shard_map/ppermute | solution.py:706
  286.9 96.3 %collective-permute-start.14 = (f32[3,128,1280]{2,1,0:T(8,128)S(1)}, f32[3,128,1280]{2,1,0:T(8,128)}, u32[]{:S(2)}, u32[]{:S(2)}) collective-permute-start(f32[3,128,1280]{2,1,0:T(8,128)S(1)} %copy-done.4), channel_id=1, source_target_pairs={{0,12},{4,8},{8,4},{12,0},{1,13},{5,9},{9,5},{13,1},{2,14},{6,10},... | collective-permute-start | bytes 5898248 | tf_op jit(solution)/shard_map/ppermute | solution.py:706
  288.5 136.0 %collective-permute-start.15 = (f32[3,128,1280]{2,1,0:T(8,128)}, f32[3,128,1280]{2,1,0:T(8,128)}, u32[]{:S(2)}, u32[]{:S(2)}) collective-permute-start(f32[3,128,1280]{2,1,0:T(8,128)} %get-tuple-element.92), channel_id=1, source_target_pairs={{0,4},{4,0},{8,12},{12,8},{1,5},{5,1},{9,13},{13,9},{2,6},{6,2},{1... | collective-permute-start | bytes 5898248 | tf_op jit(solution)/shard_map/ppermute | solution.py:706
  289.1 142.3 %collective-permute-start.16 = (f32[3,128,1280]{2,1,0:T(8,128)}, f32[3,128,1280]{2,1,0:T(8,128)}, u32[]{:S(2)}, u32[]{:S(2)}) collective-permute-start(f32[3,128,1280]{2,1,0:T(8,128)} %get-tuple-element.93), channel_id=1, source_target_pairs={{0,8},{4,12},{8,0},{12,4},{1,9},{5,13},{9,1},{13,5},{2,10},{6,14},... | collective-permute-start | bytes 5898248 | tf_op jit(solution)/shard_map/ppermute | solution.py:706
  340.0 43.1 %copy-start = (f32[3,128,1280]{2,1,0:T(8,128)}, f32[3,128,1280]{2,1,0:T(8,128)S(1)}, u32[]{:S(2)}) copy-start(f32[3,128,1280]{2,1,0:T(8,128)S(1)} %collective-permute-done.12.refs_1_) | copy-start | bytes 5898244
  340.0 93.5 %collective-permute-start.17 = (f32[3,128,1280]{2,1,0:T(8,128)}, f32[3,128,1280]{2,1,0:T(8,128)}, u32[]{:S(2)}, u32[]{:S(2)}) collective-permute-start(f32[3,128,1280]{2,1,0:T(8,128)} %get-tuple-element.94), channel_id=1, source_target_pairs={{0,12},{4,8},{8,4},{12,0},{1,13},{5,9},{9,5},{13,1},{2,14},{6,10},... | collective-permute-start | bytes 5898248 | tf_op jit(solution)/shard_map/ppermute | solution.py:706
  353.8 154.3 %collective-permute-start.6 = (f32[3,128,1280]{2,1,0:T(8,128)}, f32[3,128,1280]{2,1,0:T(8,128)}, u32[]{:S(2)}, u32[]{:S(2)}) collective-permute-start(f32[3,128,1280]{2,1,0:T(8,128)} %get-tuple-element.80), channel_id=1, source_target_pairs={{0,4},{4,0},{8,12},{12,8},{1,5},{5,1},{9,13},{13,9},{2,6},{6,2},{1... | collective-permute-start | bytes 5898248 | tf_op jit(solution)/shard_map/ppermute | solution.py:706
  383.1 414.3 %collective-permute-start.7 = (f32[3,128,1280]{2,1,0:T(8,128)}, f32[3,128,1280]{2,1,0:T(8,128)S(1)}, u32[]{:S(2)}, u32[]{:S(2)}) collective-permute-start(f32[3,128,1280]{2,1,0:T(8,128)} %get-tuple-element.81), channel_id=1, source_target_pairs={{0,8},{4,12},{8,0},{12,4},{1,9},{5,13},{9,1},{13,5},{2,10},{6,14},... | collective-permute-start | bytes 5898248 | tf_op jit(solution)/shard_map/ppermute | solution.py:706
  424.4 373.1 %collective-permute-start.8 = (f32[3,128,1280]{2,1,0:T(8,128)}, f32[3,128,1280]{2,1,0:T(8,128)}, u32[]{:S(2)}, u32[]{:S(2)}) collective-permute-start(f32[3,128,1280]{2,1,0:T(8,128)} %get-tuple-element.82), channel_id=1, source_target_pairs={{0,12},{4,8},{8,4},{12,0},{1,13},{5,9},{9,5},{13,1},{2,14},{6,10},... | collective-permute-start | bytes 5898248 | tf_op jit(solution)/shard_map/ppermute | solution.py:706
  431.4 366.1 %collective-permute-start.9 = (f32[3,128,1280]{2,1,0:T(8,128)}, f32[3,128,1280]{2,1,0:T(8,128)}, u32[]{:S(2)}, u32[]{:S(2)}) collective-permute-start(f32[3,128,1280]{2,1,0:T(8,128)} %get-tuple-element.84), channel_id=1, source_target_pairs={{0,4},{4,0},{8,12},{12,8},{1,5},{5,1},{9,13},{13,9},{2,6},{6,2},{1... | collective-permute-start | bytes 5898248 | tf_op jit(solution)/shard_map/ppermute | solution.py:706
  433.6 363.9 %collective-permute-start.10 = (f32[3,128,1280]{2,1,0:T(8,128)}, f32[3,128,1280]{2,1,0:T(8,128)}, u32[]{:S(2)}, u32[]{:S(2)}) collective-permute-start(f32[3,128,1280]{2,1,0:T(8,128)} %get-tuple-element.85), channel_id=1, source_target_pairs={{0,8},{4,12},{8,0},{12,4},{1,9},{5,13},{9,1},{13,5},{2,10},{6,14},... | collective-permute-start | bytes 5898248 | tf_op jit(solution)/shard_map/ppermute | solution.py:706
  508.2 289.3 %collective-permute-start.11 = (f32[3,128,1280]{2,1,0:T(8,128)}, f32[3,128,1280]{2,1,0:T(8,128)}, u32[]{:S(2)}, u32[]{:S(2)}) collective-permute-start(f32[3,128,1280]{2,1,0:T(8,128)} %get-tuple-element.86), channel_id=1, source_target_pairs={{0,12},{4,8},{8,4},{12,0},{1,13},{5,9},{9,5},{13,1},{2,14},{6,10},... | collective-permute-start | bytes 5898248 | tf_op jit(solution)/shard_map/ppermute | solution.py:706
  537.1 248.3 %copy-start.3 = (s32[1024,8]{0,1:T(8,128)S(1)}, s32[1024,8]{0,1:T(8,128)}, u32[]{:S(2)}) copy-start(s32[1024,8]{0,1:T(8,128)} %param.9) | copy-start | bytes 98308
  797.5 1.4 copy-start.1
  798.8 11.3 %copy-start.2 = (bf16[1024,512]{1,0:T(8,128)(2,1)S(1)}, bf16[1024,512]{1,0:T(8,128)(2,1)}, u32[]{:S(2)}) copy-start(bf16[1024,512]{1,0:T(8,128)(2,1)} %get-tuple-element.118) | copy-start | bytes 3145732
